TPU v7x, 32 devices: a whole 2x2x4 slice. The times are simulated.
32 devices in a mesh: rep: 8 (over y, x, core), tp: 4 (over z).
Axes of the slice: x: 2, y: 2, z: 4, core: 2. Of those that a mesh axis runs over, the one named last changes fastest.
Arguments:
- tokens: bfloat16 [4096, 8192], P('rep'), may hold values from -6 to 6
- query_weight: float32 [8192, 8192], P(('rep', 'tp')), may hold values from -0.0625 to 0.0625
- key_weight: float32 [8192, 1024], P(('rep', 'tp')), may hold values from -0.0625 to 0.0625
- value_weight: float32 [8192, 1024], P(('rep', 'tp')), may hold values from -0.0625 to 0.0625
- cache_keys: bfloat16 [256, 128, 1024], P('rep', None, 'tp'), may hold values from -240 to 240
- cache_values: bfloat16 [256, 128, 1024], P('rep', None, 'tp'), may hold values from -6 to 6
- lengths: int32 [8, 2], P('rep'), may hold values from 1 to 2048
- page_table: int32 [8, 2, 16], P('rep'), may hold values from 0 to 31, as said below
Outputs:
- attended: bfloat16 [4096, 8192], P('rep', 'tp')
- new_cache: bfloat16 [2, 4096, 1024], P(None, 'rep', 'tp')
Inputs may be any that keep to these rules, and one draw needn't show every extreme that they name: For each group g, the 2 x 16 entries of page_table[g] name each of the group's local pool pages 0 to 31 exactly once.
All inputs are finite; a program needn't handle non-finite values.
Results may differ from a plain program's by a relative error of at most 0.008.
The roundings to bfloat16 on the way count: a program that leaves them out, or rounds other values in their place, can miss the bound.
Values may be sent and summed in bfloat16 or wider, within the bound.
No kernel may reach another device: no remote copies, remote signals or barrier semaphores. Data moves between devices by JAX's collectives and lax.ppermute only.
A program may use at most 192 MiB of HBM per device.

v0:
```python
import jax
import jax.numpy as jnp
from jax import lax
from jax.sharding import PartitionSpec as P

HEADS = 64
KV_HEADS = 8
HEAD_DIM = 128
SEQS = 2
NEW = 256
TOK = 512
MAXLEN = 2048


ROPE_THETA = 500000.0


def rotate(vectors, positions):
    half_dim = HEAD_DIM // 2
    frequency = ROPE_THETA ** (-2.0 * jnp.arange(half_dim, dtype=jnp.float32) / HEAD_DIM)
    angles = positions.astype(jnp.float32)[:, None] * frequency[None, :]
    cosine_part = jnp.cos(angles)[:, None, :]
    sine_part = jnp.sin(angles)[:, None, :]
    first_half = vectors[..., :half_dim]
    second_half = vectors[..., half_dim:]
    return jnp.concatenate(
        [
            first_half * cosine_part - second_half * sine_part,
            second_half * cosine_part + first_half * sine_part,
        ],
        axis=-1,
    )


def per_device(
    tokens, query_weight, key_weight, value_weight, cache_keys, cache_values, lengths, page_table
):
    weights = (
        query_weight.astype(jnp.bfloat16),
        key_weight.astype(jnp.bfloat16),
        value_weight.astype(jnp.bfloat16),
    )
    slabs = (
        lax.all_to_all(weights[0], "tp", split_axis=1, concat_axis=0, tiled=True),
        lax.all_to_all(weights[1], "tp", split_axis=1, concat_axis=0, tiled=True),
        lax.all_to_all(weights[2], "tp", split_axis=1, concat_axis=0, tiled=True),
    )
    pieces = (
        lax.all_gather(slabs[0], "rep", axis=0, tiled=True),
        lax.all_gather(slabs[1], "rep", axis=0, tiled=True),
        lax.all_gather(slabs[2], "rep", axis=0, tiled=True),
    )
    raw_query, raw_key, raw_value = tuple(
        (jnp.dot(tokens, piece, preferred_element_type=jnp.float32) for piece in pieces)
    )
    kv_local = raw_key.shape[1] // HEAD_DIM
    group_size = HEADS // KV_HEADS
    scale = 1.0 / HEAD_DIM**0.5
    seq_lengths = lengths[0]
    positions = (seq_lengths[:, None] + jnp.arange(NEW, dtype=jnp.int32)[None, :]).reshape(TOK)
    queries = rotate(raw_query.reshape(TOK, kv_local * group_size, HEAD_DIM), positions).astype(
        jnp.bfloat16
    )
    new_keys = rotate(raw_key.reshape(TOK, kv_local, HEAD_DIM), positions).astype(jnp.bfloat16)
    new_values = raw_value.astype(jnp.bfloat16).reshape(TOK, kv_local, HEAD_DIM)

    def one_sequence(inner):
        seq_queries, seq_keys, seq_values, page_rows, length = inner
        old_keys = cache_keys[page_rows].reshape(MAXLEN, kv_local, HEAD_DIM)
        old_values = cache_values[page_rows].reshape(MAXLEN, kv_local, HEAD_DIM)
        all_keys = jnp.concatenate([old_keys, seq_keys], axis=0)
        all_values = jnp.concatenate([old_values, seq_values], axis=0)
        grouped = seq_queries.reshape(NEW, kv_local, group_size, HEAD_DIM)
        scores = (
            jnp.einsum("nkgd,mkd->kgnm", grouped, all_keys, preferred_element_type=jnp.float32)
            * scale
        )
        key_index = jnp.arange(MAXLEN + NEW, dtype=jnp.int32)[None, :]
        query_index = jnp.arange(NEW, dtype=jnp.int32)[:, None]
        visible = jnp.where(
            key_index < MAXLEN, key_index < length, key_index - MAXLEN <= query_index
        )
        scores = jnp.where(visible[None, None], scores, -1e30)
        maxima = jnp.max(scores, axis=-1, keepdims=True)
        expons = jnp.exp(scores - maxima)
        probs = (expons / jnp.sum(expons, axis=-1, keepdims=True)).astype(jnp.bfloat16)
        output = jnp.einsum("kgnm,mkd->nkgd", probs, all_values, preferred_element_type=jnp.float32)
        return output.astype(jnp.bfloat16).reshape(NEW, kv_local * group_size * HEAD_DIM)

    attended = lax.map(
        one_sequence,
        (
            queries.reshape(SEQS, NEW, kv_local * group_size, HEAD_DIM),
            new_keys.reshape(SEQS, NEW, kv_local, HEAD_DIM),
            new_values.reshape(SEQS, NEW, kv_local, HEAD_DIM),
            page_table[0],
            seq_lengths,
        ),
    )
    new_cache = jnp.stack(
        [new_keys.reshape(TOK, kv_local * HEAD_DIM), new_values.reshape(TOK, kv_local * HEAD_DIM)]
    )
    return (attended.reshape(TOK, kv_local * group_size * HEAD_DIM), new_cache)


def solution(mesh):
    return jax.shard_map(
        per_device,
        mesh=mesh,
        in_specs=(
            P("rep", None),
            P(("rep", "tp"), None),
            P(("rep", "tp"), None),
            P(("rep", "tp"), None),
            P("rep", None, "tp"),
            P("rep", None, "tp"),
            P("rep", None),
            P("rep", None, None),
        ),
        out_specs=(P("rep", "tp"), P(None, "rep", "tp")),
        check_vma=False,
    )
```

profile of v0, /device:TPU:0, one launch (start us, length us, event | category | flops | bytes accessed | tf_op | source)
XLA Modules:
  0.0 450.6 jit_solution(10481622972108164320)
XLA Ops:
  7.2 0.0 all-gather.6.cloned.1.call-start
  7.2 1.5 copy.33
  8.7 20.6 %all_to_all.57 = bf16[256,4,256]{0,2,1:T(8,128)(2,1)S(1)} all-to-all(bf16[256,4,256]{0,2,1:T(8,128)(2,1)S(1)} %bitcast.110), channel_id=1, replica_groups=mesh['rep'=8,'tp'=4] {'tp'}, dimensions={1} | all-to-all | bytes 1048576 | tf_op jit(solution)/shard_map/all_to_all | solution.py:45
  29.4 1.0 copy.34
  30.4 0.0 all-gather.4.cloned.1.call-start
  30.5 0.2 copy.31
  30.7 16.6 %all_to_all.58 = bf16[256,4,256]{0,2,1:T(8,128)(2,1)S(1)} all-to-all(bf16[256,4,256]{0,2,1:T(8,128)(2,1)S(1)} %bitcast.111), channel_id=1, replica_groups=mesh['rep'=8,'tp'=4] {'tp'}, dimensions={1} | all-to-all | bytes 1048576 | tf_op jit(solution)/shard_map/all_to_all | solution.py:46
  47.3 1.0 copy.32
  48.3 0.0 all-gather.8.cloned.1.call-start
  48.3 7.6 %copy.35 = bf16[256,8192]{0,1:T(8,128)(2,1)} copy(f32[256,8192]{1,0:T(8,128)} %param.11) | data formatting | bytes 12582912 | tf_op args[1]
  55.9 97.8 %all_to_all.59 = bf16[256,4,2048]{0,2,1:T(8,128)(2,1)} all-to-all(bf16[256,4,2048]{0,2,1:T(8,128)(2,1)} %bitcast.105), channel_id=1, replica_groups=mesh['rep'=8,'tp'=4] {'tp'}, dimensions={1} | all-to-all | bytes 8388608 | tf_op jit(solution)/shard_map/all_to_all | solution.py:44
  153.8 6.3 %copy.36 = bf16[4,256,2048]{2,1,0:T(8,128)(2,1)} copy(bf16[4,256,2048]{1,2,0:T(8,128)(2,1)} %bitcast.107) | data formatting | bytes 8388608 | tf_op jit(solution)/shard_map/all_to_all | solution.py:44
  160.1 0.6 copy-done.2
  160.7 0.1 convert_bitcast_fusion
  160.8 0.5 multiply_cosine_fusion
  161.4 7.1 %fusion.23 = f32[512,256]{0,1:T(8,128)S(1)} fusion(bf16[512,8192]{1,0:T(8,128)(2,1)} %param.10, bf16[8192,256]{1,0:T(8,128)(2,1)} %all-gather.6.cloned.1.call-done), kind=kOutput, calls=%fused_computation.51 | convolution fusion | flops 2147483648 | bytes 13107200 | tf_op jit(solution)/shard_map/dot_general | solution.py:54
  168.4 0.1 subtract_convert_fusion.1
  168.6 0.3 pad_maximum_fusion.2
  169.0 0.2 copy.40
  169.2 0.0 all-gather.4.cloned.1.call-done
  169.2 9.0 %convolution_convert_fusion = bf16[512,256]{1,0:T(8,128)(2,1)S(1)} fusion(bf16[512,8192]{1,0:T(8,128)(2,1)} %param.10, bf16[8192,256]{1,0:T(8,128)(2,1)} %all-gather.4.cloned.1.call-done), kind=kOutput, calls=%fused_computation.40 | convolution fusion | flops 2147614720 | bytes 12845056 | tf_op jit(solution)/shard_map/dot_general | solution.py:54
  178.3 0.8 reshape_reshape.3
  179.1 0.1 copy.50
  179.2 0.8 pad_maximum_fusion.1
  180.0 140.0 %all-gather.8.cloned.1.call-done = bf16[8192,2048]{1,0:T(8,128)(2,1)} async-done(((bf16[1024,2048]{1,0:T(8,128)(2,1)}), bf16[8192,2048]{1,0:T(8,128)(2,1)}) %all-gather.8.cloned.1.call-update) | async-done | bytes 33554448 | tf_op jit(solution)/shard_map/all_gather | solution.py:49
  320.0 25.8 %fusion.24 = f32[512,2048]{0,1:T(8,128)} fusion(bf16[512,8192]{1,0:T(8,128)(2,1)} %param.10, bf16[8192,2048]{1,0:T(8,128)(2,1)} %all-gather.8.cloned.1.call-done), kind=kOutput, calls=%fused_computation.52 | convolution fusion | flops 17179869184 | bytes 46137344 | tf_op jit(solution)/shard_map/reshape | solution.py:61
  345.8 2.9 subtract_convert_fusion
  348.7 0.3 concatenate.36
  349.0 1.1 concatenate.37
  350.2 3.9 pad_maximum_fusion
  354.1 3.7 copy.41
  357.8 86.2 %while.12 = (s32[]{:T(128)}, bf16[2,256,2048]{2,1,0:T(8,128)(2,1)}, s32[2,16]{1,0:T(2,128)S(1)}, bf16[32,128,256]{2,1,0:T(8,128)(2,1)}, bf16[2,256,2,128]{3,2,1,...) while((s32[]{:T(128)}, bf16[2,256,2048]{2,1,0:T(8,128)(2,1)}, ...), condition=%wide.region_3.4_spmd, body=%wide.region_0.3_spmd.sunk | while | flops 4894894080 | bytes 100859848 | solution.py:90
  357.8 0.6 dynamic_slice.53
  358.4 0.6 iota_compare_fusion.4
  359.1 1.9 fusion.39
  361.0 2.2 gather_fusion
  363.2 0.3 reshape.269
  363.5 0.1 copy.60
  363.7 1.3 constant_dynamic-slice_fusion.5
  365.0 17.5 %fusion.41 = (f32[2,8,256]{2,1,0:T(8,128)S(1)}, f32[2,8,256,2304]{2,3,1,0:T(8,128)}) fusion(bf16[256,2,8,128]{3,0,2,1:T(8,128)(2,1)S(1)} %bitcast.103, pred[256,2304]{0,1:T(8,128)(4,1)S(1)} %fusion.39, bf16[256,2,128]{2,0,1:T(8,128)(2,1)S(1)} %dynamic-slice_bitcast_fusion.2, bf16[2048,2,128]{2,0,1:T(8,128)(2,1)S(1)} %copy.60), kind=kOutput, calls=%fused_computation.50.clone.1 | convolution fusion | flops 2456029440 | bytes 40583168 | tf_op jit(solution)/shard_map/while/body/eval_jaxpr/sub | solution.py:85
  382.4 2.2 gather_fusion.1
  384.7 0.3 reshape.270
  384.9 0.8 copy.62
  385.8 0.1 constant_dynamic-slice_fusion.6
  385.9 0.1 copy.61
  386.0 13.3 %fusion.42 = bf16[2,128,8,256]{3,1,2,0:T(8,128)(2,1)S(1)} fusion(f32[2,8,256,2304]{2,3,1,0:T(8,128)} %get-tuple-element.232, f32[2,8,256]{2,1,0:T(8,128)S(1)} %get-tuple-element.233, bf16[256,2,128]{0,2,1:T(8,128)(2,1)S(1)} %bitcast.109, bf16[2048,2,128]{0,2,1:T(8,128)(2,1)S(1)} %copy.62), kind=kOutput, calls=%fused_computation.14.clone.1 | convolution fusion | flops 2437677056 | bytes 39993344 | tf_op jit(solution)/shard_map/while/body/eval_jaxpr/kgnm,mkd->nkgd/dot_general | solution.py:87
  399.3 0.6 copy.63
  399.9 1.0 constant_dynamic-update-slice_fusion.2
  401.0 0.6 dynamic_slice.53
  401.5 0.6 iota_compare_fusion.4
  402.2 1.9 fusion.39
  404.1 2.2 gather_fusion
  406.3 0.3 reshape.269
  406.6 0.1 copy.60
  406.8 1.3 constant_dynamic-slice_fusion.5
  408.1 17.5 %fusion.41 = (f32[2,8,256]{2,1,0:T(8,128)S(1)}, f32[2,8,256,2304]{2,3,1,0:T(8,128)}) fusion(bf16[256,2,8,128]{3,0,2,1:T(8,128)(2,1)S(1)} %bitcast.103, pred[256,2304]{0,1:T(8,128)(4,1)S(1)} %fusion.39, bf16[256,2,128]{2,0,1:T(8,128)(2,1)S(1)} %dynamic-slice_bitcast_fusion.2, bf16[2048,2,128]{2,0,1:T(8,128)(2,1)S(1)} %copy.60), kind=kOutput, calls=%fused_computation.50.clone.1 | convolution fusion | flops 2456029440 | bytes 40583168 | tf_op jit(solution)/shard_map/while/body/eval_jaxpr/sub | solution.py:85
  425.6 2.2 gather_fusion.1
  427.8 0.3 reshape.270
  428.1 0.8 copy.62
  428.9 0.1 constant_dynamic-slice_fusion.6
  429.0 0.1 copy.61
  429.1 13.3 %fusion.42 = bf16[2,128,8,256]{3,1,2,0:T(8,128)(2,1)S(1)} fusion(f32[2,8,256,2304]{2,3,1,0:T(8,128)} %get-tuple-element.232, f32[2,8,256]{2,1,0:T(8,128)S(1)} %get-tuple-element.233, bf16[256,2,128]{0,2,1:T(8,128)(2,1)S(1)} %bitcast.109, bf16[2048,2,128]{0,2,1:T(8,128)(2,1)S(1)} %copy.62), kind=kOutput, calls=%fused_computation.14.clone.1 | convolution fusion | flops 2437677056 | bytes 39993344 | tf_op jit(solution)/shard_map/while/body/eval_jaxpr/kgnm,mkd->nkgd/dot_general | solution.py:87
  442.4 0.6 copy.63
  443.0 1.0 constant_dynamic-update-slice_fusion.2
  (25 shorter events, 0.3 us)
Async XLA Ops:
  7.2 23.3 %copy-start.1 = (f32[256,1024]{1,0:T(8,128)S(1)}, f32[256,1024]{1,0:T(8,128)}, u32[]{:S(2)}) copy-start(f32[256,1024]{1,0:T(8,128)} %param.13) | copy-start | bytes 3145732
  7.2 154.2 %all-gather.6.cloned.1.call-start = ((), (), s32[]{:S(2)}) async-start(), calls=%async_computation.4 | async-start | bytes 4718592 | tf_op jit(solution)/shard_map/all_gather | solution.py:50
  30.4 138.8 %all-gather.4.cloned.1.call-start = ((), (), s32[]{:S(2)}) async-start(), calls=%async_computation.3 | async-start | bytes 4718592 | tf_op jit(solution)/shard_map/all_gather | solution.py:51
  48.3 271.8 %all-gather.8.cloned.1.call-start = ((), (), s32[]{:S(2)}) async-start(), calls=%async_computation.5 | async-start | bytes 37748736 | tf_op jit(solution)/shard_map/all_gather | solution.py:49
  160.0 0.7 copy-start.2
  350.2 7.7 %copy-start.3 = (s32[1,2,16]{2,1,0:T(2,128)S(1)}, s32[1,2,16]{2,1,0:T(2,128)}, u32[]{:S(2)}) copy-start(s32[1,2,16]{2,1,0:T(2,128)} %param.17) | copy-start | bytes 388
  354.1 3.7 copy-start
Sparse Core Ops, SparseCore 0:
  30.5 35.6 all-gather.5
  68.7 36.5 all-gather.3
  160.2 159.7 all-gather.7
where the time goes:
time: 451 us
  waiting for transfers between devices  140 us (31%)
  blocking collectives  135 us (30%)
  matrix products  103 us (23%)
  local copies, waits for them, and re-layouts  44 us (10%)
  between operations  13.9 us (3%)
  other arithmetic  13.8 us (3%)
    all_gather x1, waiting for transfers between devices, per_device(): lax.all_gather(slabs[0], 'rep', axis=0, tiled=True)  140 us
    all_to_all x1, blocking collectives, per_device(): lax.all_to_all(weights[0], 'tp', split_axis=1, concat_axis=0, tiled=True)  97.8 us
    sub x2, matrix products, one_sequence(): expons = jnp.exp(scores - maxima)  34.9 us
    dot_general x2, matrix products, one_sequence(): jnp.einsum('kgnm,mkd->nkgd', probs, all_values, preferred_element_type=jn...  26.5 us
    reshape x1, matrix products, per_device(): raw_query.reshape(TOK, kv_local * group_size, HEAD_DIM)  25.8 us
    all_to_all x1, blocking collectives, per_device(): lax.all_to_all(weights[1], 'tp', split_axis=1, concat_axis=0, tiled=True)  20.6 us
    all_to_all x1, blocking collectives, per_device(): lax.all_to_all(weights[2], 'tp', split_axis=1, concat_axis=0, tiled=True)  16.6 us
    dot_general x2, matrix products, per_device(): jnp.dot(tokens, piece, preferred_element_type=jnp.float32)  16.1 us
  transfers between devices with their start and end apart: 3, of which 1 were waited for; matrix products, arithmetic and copies ran while one was open for 8% of the time, Pallas kernels for 0%

commit v1 on v0

--- a/solution.py
+++ b/solution.py
@@ -1,6 +1,10 @@
+import functools
+
 import jax
 import jax.numpy as jnp
 from jax import lax
+from jax.experimental import pallas as pl
+from jax.experimental.pallas import tpu as pltpu
 from jax.sharding import PartitionSpec as P
 
 HEADS = 64
@@ -10,12 +14,16 @@
 NEW = 256
 TOK = 512
 MAXLEN = 2048
-
-
 ROPE_THETA = 500000.0
-
-
-def rotate(vectors, positions):
+KEY_BLOCK = 512
+VMEM_LIMIT = 56 * 1024 * 1024
+BF = jnp.bfloat16
+
+HEAD_CHUNKS = (1, 3, 3, 1)
+OWN_ORDER = (0, 1, 2, 3)
+
+
+def plain_rotate(vectors, positions):
     half_dim = HEAD_DIM // 2
     frequency = ROPE_THETA ** (-2.0 * jnp.arange(half_dim, dtype=jnp.float32) / HEAD_DIM)
     angles = positions.astype(jnp.float32)[:, None] * frequency[None, :]
@@ -32,7 +40,7 @@
     )
 
 
-def per_device(
+def plain(
     tokens, query_weight, key_weight, value_weight, cache_keys, cache_values, lengths, page_table
 ):
     weights = (
@@ -58,10 +66,10 @@
     scale = 1.0 / HEAD_DIM**0.5
     seq_lengths = lengths[0]
     positions = (seq_lengths[:, None] + jnp.arange(NEW, dtype=jnp.int32)[None, :]).reshape(TOK)
-    queries = rotate(raw_query.reshape(TOK, kv_local * group_size, HEAD_DIM), positions).astype(
+    queries = plain_rotate(raw_query.reshape(TOK, kv_local * group_size, HEAD_DIM), positions).astype(
         jnp.bfloat16
     )
-    new_keys = rotate(raw_key.reshape(TOK, kv_local, HEAD_DIM), positions).astype(jnp.bfloat16)
+    new_keys = plain_rotate(raw_key.reshape(TOK, kv_local, HEAD_DIM), positions).astype(jnp.bfloat16)
     new_values = raw_value.astype(jnp.bfloat16).reshape(TOK, kv_local, HEAD_DIM)
 
     def one_sequence(inner):
@@ -103,9 +111,427 @@
     return (attended.reshape(TOK, kv_local * group_size * HEAD_DIM), new_cache)
 
 
+def rotate(v, cos, sin):
+    half = HEAD_DIM // 2
+    swapped = jnp.concatenate([v[:, half:], v[:, :half]], axis=1)
+    return v * cos + swapped * sin
+
+
+def pack_kernel(jobs, n_recv, starts_ref, *refs):
+    weights, received = refs[:3], refs[3 : 3 + n_recv]
+    outs = refs[3 + n_recv : 3 + n_recv + len(jobs)]
+    buf, sems = refs[-2:]
+    flat, at = [], 0
+    for out, pieces in zip(outs, jobs):
+        for row, col, width, source, begin in pieces:
+            if source >= 3:
+                continue
+            src = weights[source].at[:, pl.ds(pl.multiple_of(starts_ref[begin], 128), width)]
+            copy = pltpu.make_async_copy(src, buf.at[:, pl.ds(at, width)], sems.at[len(flat)])
+            copy.start()
+            flat.append((copy, out, row, col, width, at))
+            at += width
+    rows = buf.shape[0]
+    for out, pieces in zip(outs, jobs):
+        for row, col, width, source, begin in pieces:
+            if source >= 3:
+                out[row : row + rows, col : col + width] = received[source - 3][:, begin : begin + width]
+    for copy, out, row, col, width, at in flat:
+        copy.wait()
+        out[row : row + rows, col : col + width] = buf[:, at : at + width].astype(BF)
+
+
+def pack(jobs, shapes, starts, weights, received):
+    n = sum(1 for pieces in jobs for piece in pieces if piece[3] < 3)
+    total = sum(piece[2] for pieces in jobs for piece in pieces if piece[3] < 3)
+    rows = weights[0].shape[0]
+    return pl.pallas_call(
+        functools.partial(pack_kernel, jobs, len(received)),
+        out_shape=[jax.ShapeDtypeStruct(shape, BF) for shape in shapes],
+        grid_spec=pltpu.PrefetchScalarGridSpec(
+            num_scalar_prefetch=1,
+            grid=(1,),
+            in_specs=[pl.BlockSpec(memory_space=pl.ANY)] * 3
+            + [pl.BlockSpec(a.shape, lambda i, _: (0, 0)) for a in received],
+            out_specs=[pl.BlockSpec(shape, lambda i, _: (0, 0)) for shape in shapes],
+            scratch_shapes=[pltpu.VMEM((rows, total), jnp.float32), pltpu.SemaphoreType.DMA((n,))],
+        ),
+        compiler_params=pltpu.CompilerParams(vmem_limit_bytes=VMEM_LIMIT),
+        cost_estimate=pl.CostEstimate(flops=1000000, bytes_accessed=rows * total * 6, transcendentals=0),
+    )(starts, *weights, *received)
+
+
+def move_kernel(jobs, *refs):
+    n_in = 1 + max(job[0] for job in jobs)
+    ins, outs, sems = refs[:n_in], refs[n_in:-1], refs[-1]
+    copies = []
+    for k, (source, first, rows, target, to) in enumerate(jobs):
+        copies.append(
+            pltpu.make_async_copy(
+                ins[source].at[pl.ds(first, rows)], outs[target].at[pl.ds(to, rows)], sems.at[k]
+            )
+        )
+        copies[-1].start()
+    for copy in copies:
+        copy.wait()
+
+
+def move(jobs, arrays, shapes):
+    return pl.pallas_call(
+        functools.partial(move_kernel, jobs),
+        out_shape=[jax.ShapeDtypeStruct(shape, BF) for shape in shapes],
+        in_specs=[pl.BlockSpec(memory_space=pl.ANY)] * len(arrays),
+        out_specs=[pl.BlockSpec(memory_space=pltpu.VMEM)] * len(shapes),
+        scratch_shapes=[pltpu.SemaphoreType.DMA((len(jobs),))],
+        compiler_params=pltpu.CompilerParams(vmem_limit_bytes=16 * 1024 * 1024),
+        cost_estimate=pl.CostEstimate(
+            flops=1000000, bytes_accessed=sum(4 * a * b for a, b in shapes), transcendentals=0
+        ),
+    )(*arrays)
+
+
+def lanes(x):
+    return [x[:, i * 128 : (i + 1) * 128] for i in range(x.shape[1] // 128)]
+
+
+def spread(column):
+    return jnp.broadcast_to(column, (column.shape[0], 128))
+
+
+def order_kernel(shard, order_ref, theirs_ref, mine_ref, out_ref, sems):
+    i = pl.program_id(0)
+    rows, depth = out_ref.shape
+    half = pl.num_programs(0) // 2
+
+    def copies(ref, first):
+        for k in range(depth // shard):
+            src = ref.at[pl.ds(first, rows), pl.ds(pl.multiple_of(order_ref[k] * shard, shard), shard)]
+            yield pltpu.make_async_copy(src, out_ref.at[:, pl.ds(k * shard, shard)], sems.at[k])
+
+    @pl.when(i < half)
+    def _():
+        for copy in copies(theirs_ref, i * rows):
+            copy.start()
+
+    @pl.when(i >= half)
+    def _():
+        for copy in copies(mine_ref, (i - half) * rows):
+            copy.start()
+
+    for copy in copies(mine_ref, 0):
+        copy.wait()
+
+
+def chunk_kernel(places, heads, with_kv, block, len_ref, tok_ref, cos_ref, sin_ref, ok_ref, ov_ref, *refs):
+    if with_kv:
+        weights, refs = refs[: len(places)], refs[len(places) :]
+        theirs_ref, mine_ref, fresh_ref = refs[:3]
+        refs = refs[3:]
+    else:
+        fresh_ref, weights, refs = refs[0], refs[1 : 1 + len(places)], refs[1 + len(places) :]
+        theirs_ref, mine_ref = refs[:2]
+        refs = refs[2:]
+    q_ref, e_ref, m_ref, l_ref, top_ref, acc_ref = refs
+    i = pl.program_id(0)
+    new = tok_ref.shape[0]
+    length = len_ref[i]
+    blocks = (length + block - 1) // block
+    factor = (1.0 / HEAD_DIM**0.5) * 1.4426950408889634
+    nt = (((1,), (1,)), ((), ()))
+
+    raw = None
+    for place, ref in zip(places, weights):
+        part = jnp.dot(tok_ref[:, place : place + ref.shape[0]], ref[...], preferred_element_type=jnp.float32)
+        raw = part if raw is None else raw + part
+    raw = [raw[:, h * HEAD_DIM : (h + 1) * HEAD_DIM] for h in range(raw.shape[1] // HEAD_DIM)]
+    if with_kv:
+        fresh_ref[0] = rotate(raw[0], cos_ref[...], sin_ref[...]).astype(BF)
+        fresh_ref[1] = raw[1].astype(BF)
+        raw = raw[2:]
+    for h in range(heads):
+        q_ref[h * new : (h + 1) * new, :] = rotate(raw[h], cos_ref[...], sin_ref[...]).astype(BF)
+
+    s = lax.dot_general(q_ref[...], fresh_ref[0], nt, preferred_element_type=jnp.float32)
+    row = lax.broadcasted_iota(jnp.int32, s.shape, 0) % new
+    col = lax.broadcasted_iota(jnp.int32, s.shape, 1)
+    parts = lanes(jnp.where(col <= row, s, -1e30))
+    m = functools.reduce(jnp.maximum, parts)
+    es = [jnp.exp2((c - m) * factor) for c in parts]
+    for j, e in enumerate(es):
+        e_ref[0, :, j * 128 : (j + 1) * 128] = e
+    m_ref[0] = m
+    l_ref[...] = sum(es)
+
+    @pl.loop(0, blocks)
+    def _(b):
+        start = pl.multiple_of(b * block, block)
+        s = lax.dot_general(q_ref[...], ok_ref[0, pl.ds(start, block), :], nt, preferred_element_type=jnp.float32)
+        at = lax.broadcasted_iota(jnp.int32, s.shape, 1)
+        parts = lanes(jnp.where(at < length - start, s, -1e30))
+        before = m_ref[b]
+        m = functools.reduce(jnp.maximum, parts, before)
+        es = [jnp.exp2((c - m) * factor) for c in parts]
+        for j, e in enumerate(es):
+            e_ref[b + 1, :, j * 128 : (j + 1) * 128] = e
+        m_ref[b + 1] = m
+        l_ref[...] = l_ref[...] * jnp.exp2((before - m) * factor) + sum(es)
+
+    last = m_ref[blocks]
+    top = spread(jnp.max(last, axis=1, keepdims=True))
+    total = jnp.sum(l_ref[...] * jnp.exp2((last - top) * factor), axis=1, keepdims=True)
+    top_ref[...] = top
+    inverse = spread(1.0 / total)
+    l_ref[...] = inverse
+
+    def probs(slot, n):
+        scale = jnp.exp2((m_ref[slot] - top_ref[...]) * factor) * l_ref[...]
+        return jnp.concatenate(
+            [(e_ref[slot, :, j * 128 : (j + 1) * 128] * scale).astype(BF) for j in range(n)], axis=1
+        )
+
+    acc_ref[...] = jnp.dot(probs(0, new // 128), fresh_ref[1], preferred_element_type=jnp.float32)
+
+    @pl.loop(0, blocks)
+    def _(b):
+        start = pl.multiple_of(b * block, block)
+        acc_ref[...] += jnp.dot(
+            probs(b + 1, block // 128), ov_ref[0, pl.ds(start, block), :], preferred_element_type=jnp.float32
+        )
+
+    def write(out_ref):
+        for h in range(heads):
+            out_ref[:, h * HEAD_DIM : (h + 1) * HEAD_DIM] = acc_ref[h * new : (h + 1) * new, :].astype(BF)
+
+    half = pl.num_programs(0) // 2
+    pl.when(i < half)(lambda: write(theirs_ref))
+    pl.when(i >= half)(lambda: write(mine_ref))
+
+
+def by_core(R, T, tokens, query_weight, key_weight, value_weight, cache_keys, cache_values, lengths, page_table):
+    tok_rows, depth = tokens.shape
+    shard = query_weight.shape[0]
+    seqs = lengths.shape[1]
+    new = tok_rows // seqs
+    q_local = query_weight.shape[1] // T
+    q_core = q_local // 2
+    kv_width = key_weight.shape[1] // T
+    r, z = lax.axis_index("rep"), lax.axis_index("tp")
+    core = r % 2
+    max_len = cache_keys.shape[1] * page_table.shape[2]
+
+    def xor(a, bit):
+        return lax.ppermute(a, "rep", [(i, i ^ bit) for i in range(R)])
+
+    head_chunks = HEAD_CHUNKS
+    widths = [(n + 2 * (c == 0)) * HEAD_DIM for c, n in enumerate(head_chunks)]
+    firsts = [sum(widths[:c]) for c in range(len(widths))]
+    own_firsts, col = {}, 0
+    for c in OWN_ORDER:
+        own_firsts[c] = col
+        col += widths[c]
+    whole = sum(widths)
+    n_chunks = len(widths)
+
+    starts = []
+    for s in range(T):
+        target = (z + s) % T
+        for h in (core, 1 - core):
+            starts += [target * q_local + h * q_core, target * kv_width + h * HEAD_DIM, target * kv_width + h * HEAD_DIM]
+    for s in range(T):
+        target = (z + s) % T
+        for h in (core, 1 - core):
+            base = target * q_local + h * q_core
+            starts += [base + firsts[c] - 2 * HEAD_DIM if c else base for c in range(n_chunks)]
+    starts = jnp.stack(starts).astype(jnp.int32)
+    weights = (query_weight, key_weight, value_weight)
+
+    def pieces(s, other, c, row, col):
+        base, q_base = 3 * (2 * s + other), 6 * T + n_chunks * (2 * s + other)
+        if c:
+            return [(row, col, widths[c], 0, q_base + c)]
+        return [
+            (row, col, HEAD_DIM, 1, base + 1),
+            (row, col + HEAD_DIM, HEAD_DIM, 2, base + 2),
+            (row, col + 2 * HEAD_DIM, widths[0] - 2 * HEAD_DIM, 0, q_base),
+        ]
+
+    def all_chunks(s, other, row, col):
+        return [p for c in range(n_chunks) for p in pieces(s, other, c, row, col + own_firsts[c])]
+
+    send_a = pack([all_chunks(0, 1, 0, 0)], [(shard, whole)], starts, weights, [])[0]
+    got_a = xor(send_a, 1)
+
+    def their_half(chunks):
+        job, col, place = [], 0, {}
+        for c in chunks:
+            for s in range(1, T):
+                job += pieces(s, 1, c, 0, col)
+                place[s, c] = col
+                col += widths[c]
+        return pack([job], [(shard, col)], starts, weights, [])[0], place
+
+    def to_send(got, place):
+        jobs, shapes = [], []
+        for s, c in place:
+            jobs.append(pieces(s, 0, c, 0, 0) + [(shard, 0, widths[c], 3, place[s, c])])
+            shapes.append((2 * shard, widths[c]))
+        return dict(zip(place, pack(jobs, shapes, starts, weights, [got])))
+
+    send_b, place_b = their_half([0])
+    got_b = xor(send_b, 1)
+    own = pack([all_chunks(0, 0, 0, 0) + [(shard, 0, whole, 3, 0)]], [(2 * shard, whole)], starts, weights, [got_a])[0]
+    ready = to_send(got_b, place_b)
+    send_c, place_c = their_half(range(1, n_chunks))
+    got_c = xor(send_c, 1)
+    ready.update(to_send(got_c, place_c))
+
+    def over_tp(c):
+        got = []
+        for s in range(1, T):
+            got.append(lax.ppermute(ready[s, c], "tp", [(t, (t + s) % T) for t in range(T)]))
+        rows = got[0].shape[0]
+        jobs = [(k, 0, rows, 0, k * rows) for k in range(T - 1)]
+        return move(jobs, got, [((T - 1) * rows, widths[c])])[0]
+
+    def gather(piece):
+        by_x, by_y = xor(piece, 2), xor(piece, 4)
+        n = piece.shape[0] // 2
+        jobs = [(0, 0, n, 0, 0), (1, n, n, 1, 0)]
+        low, high = move(jobs, [by_y, by_x], [(n, piece.shape[1])] * 2)
+        far = [(6, 0, xor(low, 2)), (6, n, xor(high, 4))]
+        return [(0, 0, piece), (2, 0, by_x), (4, 0, by_y), *far]
+
+    own_all = gather(own)
+    rest_all = [gather(over_tp(c)) for c in range(n_chunks)]
+
+    their_tokens = xor(tokens, 1)
+    seq_lengths = jnp.concatenate([xor(lengths, 1)[0], lengths[0]])
+    old = jnp.stack(
+        [a[page_table[0]].reshape(seqs, max_len, kv_width) for a in (cache_keys, cache_values)]
+    )
+    mine_old = lax.dynamic_slice_in_dim(old, core * HEAD_DIM, HEAD_DIM, 3)
+    their_old = xor(lax.dynamic_slice_in_dim(old, (1 - core) * HEAD_DIM, HEAD_DIM, 3), 1)
+    old_keys, old_values = [jnp.concatenate([their_old[k], mine_old[k]], axis=0) for k in range(2)]
+
+    order, place = [], {}
+    for shifts in ([0], list(range(1, T))):
+        for d in range(0, R, 2):
+            place[d, shifts[0]] = len(order) * shard
+            order += [(r ^ (d + e)) * T + (z - s) % T for s in shifts for e in range(2)]
+    order = jnp.stack(order).astype(jnp.int32)
+    rows_all = 2 * tok_rows
+    params = pltpu.CompilerParams(vmem_limit_bytes=VMEM_LIMIT)
+    call = pl.pallas_call(
+        functools.partial(order_kernel, shard),
+        out_shape=jax.ShapeDtypeStruct((rows_all, depth), BF),
+        grid_spec=pltpu.PrefetchScalarGridSpec(
+            num_scalar_prefetch=1,
+            grid=(2 * seqs,),
+            in_specs=[pl.BlockSpec(memory_space=pl.ANY)] * 2,
+            out_specs=pl.BlockSpec((new, depth), lambda i, _: (i, 0)),
+            scratch_shapes=[pltpu.SemaphoreType.DMA((depth // shard,))],
+        ),
+        compiler_params=params,
+        cost_estimate=pl.CostEstimate(flops=1000000, bytes_accessed=4 * rows_all * depth, transcendentals=0),
+        name="order_tokens",
+    )
+    tok = call(order, their_tokens, tokens)
+
+    half = HEAD_DIM // 2
+    frequency = ROPE_THETA ** (-2.0 * jnp.arange(half, dtype=jnp.float32) / HEAD_DIM)
+    positions = (seq_lengths[:, None] + jnp.arange(new, dtype=jnp.int32)[None, :]).reshape(rows_all)
+    angles = positions.astype(jnp.float32)[:, None] * frequency[None, :]
+    cos, sin = jnp.cos(angles), jnp.sin(angles)
+    cos, sin = jnp.concatenate([cos, cos], axis=1), jnp.concatenate([-sin, sin], axis=1)
+
+    def attend(c, fresh):
+        n = head_chunks[c]
+        width = n * HEAD_DIM
+        with_kv = c == 0
+        block = KEY_BLOCK if n > 1 else 2 * KEY_BLOCK
+        slots = max_len // block + 1
+        specs, arrays, places = [], [], []
+        for s, first, parts in ((0, own_firsts[c], own_all), (1, 0, rest_all[c])):
+            for d, o, a in parts:
+                specs.append(
+                    pl.BlockSpec((a.shape[0], widths[c]), functools.partial(lambda k, *_: (0, k), first // widths[c]))
+                )
+                arrays.append(a)
+                places.append(place[d, s] + o)
+        row = lambda i, *_: (i, 0)
+        out_shape = [jax.ShapeDtypeStruct((tok_rows, width), BF)] * 2
+        out_specs = [
+            pl.BlockSpec((new, width), lambda i, *_: (jnp.minimum(i, seqs - 1), 0)),
+            pl.BlockSpec((new, width), lambda i, *_: (jnp.maximum(i - seqs, 0), 0)),
+        ]
+        fresh_spec = pl.BlockSpec((2, new, HEAD_DIM), lambda i, *_: (0, i, 0))
+        if with_kv:
+            out_shape.append(jax.ShapeDtypeStruct((2, rows_all, HEAD_DIM), BF))
+            out_specs.append(fresh_spec)
+        call = pl.pallas_call(
+            functools.partial(chunk_kernel, places, n, with_kv, block),
+            out_shape=out_shape,
+            grid_spec=pltpu.PrefetchScalarGridSpec(
+                num_scalar_prefetch=1,
+                grid=(2 * seqs,),
+                in_specs=[
+                    pl.BlockSpec((new, depth), row),
+                    pl.BlockSpec((new, HEAD_DIM), row),
+                    pl.BlockSpec((new, HEAD_DIM), row),
+                    pl.BlockSpec((1, max_len, HEAD_DIM), lambda i, *_: (i, 0, 0)),
+                    pl.BlockSpec((1, max_len, HEAD_DIM), lambda i, *_: (i, 0, 0)),
+                    *([] if with_kv else [fresh_spec]),
+                    *specs,
+                ],
+                out_specs=out_specs,
+                scratch_shapes=[
+                    pltpu.VMEM((n * new, HEAD_DIM), BF),
+                    pltpu.VMEM((slots, n * new, block), jnp.float32),
+                    pltpu.VMEM((slots, n * new, 128), jnp.float32),
+                    pltpu.VMEM((n * new, 128), jnp.float32),
+                    pltpu.VMEM((n * new, 128), jnp.float32),
+                    pltpu.VMEM((n * new, 128), jnp.float32),
+                ],
+            ),
+            compiler_params=params,
+            cost_estimate=pl.CostEstimate(
+                flops=2 * rows_all * width * (depth + 2 * (max_len + new)),
+                bytes_accessed=(rows_all + width) * depth * 2,
+                transcendentals=rows_all * n * (max_len + new),
+            ),
+        )
+        extra = () if with_kv else (fresh,)
+        return call(seq_lengths, tok, cos, sin, old_keys, old_values, *extra, *arrays)
+
+    out, at, fresh = jnp.zeros((tok_rows, q_local), BF), 0, None
+    for c in range(n_chunks):
+        theirs, mine, *rest = attend(c, fresh)
+        if rest:
+            fresh = rest[0]
+            back = xor(fresh[:, :tok_rows], 1)
+            kept = fresh[:, tok_rows:]
+            new_cache = jnp.concatenate(
+                [jnp.where(core == 0, kept, back), jnp.where(core == 0, back, kept)], axis=2
+            )
+        theirs = xor(theirs, 1)
+        out = lax.dynamic_update_slice(out, mine, (0, core * q_core + at))
+        out = lax.dynamic_update_slice(out, theirs, (0, (1 - core) * q_core + at))
+        at += head_chunks[c] * HEAD_DIM
+    return out, new_cache
+
+
+def per_device(R, T, *args):
+    _, query_weight, key_weight = args[:3]
+    heads = query_weight.shape[1] // T // HEAD_DIM
+    kv = key_weight.shape[1] // T // HEAD_DIM
+    if R == 8 and kv == 2 and heads == 16:
+        return by_core(R, T, *args)
+    return plain(*args)
+
+
 def solution(mesh):
     return jax.shard_map(
-        per_device,
+        functools.partial(per_device, mesh.shape["rep"], mesh.shape["tp"]),
         mesh=mesh,
         in_specs=(
             P("rep", None),

time: 451 us -> 416 us (0.922)
  the two profiles are of different devices: /device:TPU:0 before, /device:TPU:25 now
where the time goes in v1:
time: 416 us; the launch traced here: 415 us
  waiting for transfers between devices  173 us (42%)
  Pallas kernels  150 us (36%)
  starting transfers between devices  59.1 us (14%)
  local copies, waits for them, and re-layouts  20.5 us (5%)
  other arithmetic  10.9 us (3%)
    ppermute x31, waiting for transfers between devices, xor(): return lax.ppermute(a, 'rep', [(i, i ^ bit) for i in range(R)])  111 us
    pallas_call x4, Pallas kernels, attend(): call(seq_lengths, tok, cos, sin, old_keys, old_values, *extra, *arrays)  99.7 us
    ppermute x12, waiting for transfers between devices, over_tp(): lax.ppermute(ready[s, c], 'tp', [(t, (t + s) % T) for t in range(T)])  62.4 us
    ppermute x12, starting transfers between devices, over_tp(): lax.ppermute(ready[s, c], 'tp', [(t, (t + s) % T) for t in range(T)])  32 us
    ppermute x31, starting transfers between devices, xor(): return lax.ppermute(a, 'rep', [(i, i ^ bit) for i in range(R)])  27 us
    pallas_call x6, Pallas kernels, pack(): pl.pallas_call(functools.partial(pack_kernel, jobs, len(received)), out_s...  23.2 us
    pallas_call x1, Pallas kernels, by_core(): tok = call(order, their_tokens, tokens)  16.7 us
    pallas_call x9, Pallas kernels, move(): pl.pallas_call(functools.partial(move_kernel, jobs), out_shape=[jax.Shape...  10.6 us
  transfers between devices with their start and end apart: 43, of which 13 were waited for; matrix products, arithmetic and copies ran while one was open for 5% of the time, Pallas kernels for 36%

profile of v1, /device:TPU:25, one launch (start us, length us, event | category | flops | bytes accessed | tf_op | source)
XLA Modules:
  0.0 415.1 jit_solution(12537172989875615550)
XLA Ops:
  2.0 3.5 shard_map.103
  5.7 2.9 shard_map.98
  9.1 2.9 shard_map.95
  12.6 4.6 %collective-permute-done.8.refs_3_ = bf16[256,1152]{1,0:T(8,128)(2,1)S(1)} collective-permute-done((bf16[256,1152]{1,0:T(8,128)(2,1)}, bf16[256,1152]{1,0:T(8,128)(2,1)S(1)}, u32[]{:S(2)}, u32[]{:S(2)}) %collective-permute-start.8) | collective-permute-done | bytes 589856 | tf_op jit(solution)/shard_map/ppermute | solution.py:323
  17.2 0.8 copy-done.37
  18.0 4.2 %shard_map.99 = (bf16[512,384]{1,0:T(8,128)(2,1)}, bf16[512,384]{1,0:T(8,128)(2,1)}, bf16[512,384]{1,0:T(8,128)(2,1)}) custom-call(s32[56]{0:T(128)} %stack.315.starts_ref, f32[256,8192]{1,0:T(8,128)} %refs_0_.11, f32[256,1024]{1,0:T(8,128)} %refs_1_.11, f32[256,1024]{1,0:T(8,128)} %refs_2_.11, bf16[256,1152]{1,0:T(8,128)(2,1)} %copy-done.37), custom_call_target="tpu_custom_call" | custom-call | flops 1000000 | bytes 1769472 | tf_op jit(solution)/shard_map/pallas_call | solution.py:148
  22.3 1.3 collective-permute-start.10
  23.8 0.9 copy-done.35
  24.7 5.3 %shard_map.104 = (bf16[512,384]{1,0:T(8,128)(2,1)}, bf16[512,384]{1,0:T(8,128)(2,1)}, bf16[512,384]{1,0:T(8,128)(2,1)}, bf16[512,384]{1,0:T(8,128)(2,1)}, bf16[5...) custom-call(s32[56]{0:T(128)} %stack.315.starts_ref, ...), custom_call_target="tpu_custom_call" | custom-call | flops 1000000 | bytes 4128768 | tf_op jit(solution)/shard_map/pallas_call | solution.py:148
  30.1 2.2 collective-permute-start.34
  33.5 2.2 collective-permute-start.18
  35.7 22.3 %collective-permute-done.10.refs_1_ = bf16[512,384]{1,0:T(8,128)(2,1)S(1)} collective-permute-done((bf16[512,384]{1,0:T(8,128)(2,1)}, bf16[512,384]{1,0:T(8,128)(2,1)S(1)}, u32[]{:S(2)}, u32[]{:S(2)}) %collective-permute-start.10) | collective-permute-done | bytes 393248 | tf_op jit(solution)/shard_map/ppermute | solution.py:391
  58.0 0.7 copy-done.22
  58.7 20.7 %collective-permute-start.35 = (bf16[512,128]{1,0:T(8,128)(2,1)}, bf16[512,128]{1,0:T(8,128)(2,1)S(1)}, u32[]{:S(2)}, u32[]{:S(2)}) collective-permute-start(bf16[512,128]{1,0:T(8,128)(2,1)} %get-tuple-element.58), channel_id=1, source_target_pairs={{0,2},{1,3},{2,0},{3,1},{4,6},{5,7},{6,4},{7,5},{8,10},{9,11},{10,... | collective-permute-start | bytes 393224 | tf_op jit(solution)/shard_map/ppermute | solution.py:391
  79.5 4.3 %shard_map.96.refs_0_.refs_1_ = bf16[512,1280]{1,0:T(8,128)(2,1)} custom-call(s32[56]{0:T(128)} %stack.315.starts_ref, f32[256,8192]{1,0:T(8,128)} %refs_0_.11, f32[256,1024]{1,0:T(8,128)} %refs_1_.11, f32[256,1024]{1,0:T(8,128)} %refs_2_.11, bf16[256,1280]{1,0:T(8,128)(2,1)} %copy-done.36), custom_call_target="tpu_custom_call" | custom-call | flops 1000000 | bytes 1966080 | tf_op jit(solution)/shard_map/pallas_call | solution.py:148
  83.8 10.7 %collective-permute-done.35.refs_1_ = bf16[512,128]{1,0:T(8,128)(2,1)S(1)} collective-permute-done((bf16[512,128]{1,0:T(8,128)(2,1)}, bf16[512,128]{1,0:T(8,128)(2,1)S(1)}, u32[]{:S(2)}, u32[]{:S(2)}) %collective-permute-start.35) | collective-permute-done | bytes 131104 | tf_op jit(solution)/shard_map/ppermute | solution.py:391
  95.1 1.2 collective-permute-start.4
  96.4 2.0 gather_fusion
  98.4 3.7 gather_fusion.1
  102.1 3.3 collective-permute-start.26
  105.4 4.2 %fusion.1 = (bf16[2,2,2048,128]{3,2,1,0:T(8,128)(2,1)}, bf16[2,2,2048,128]{3,2,1,0:T(8,128)(2,1)}) fusion(s32[]{:T(128)S(6)} %select_n.160, bf16[1,2,2048,256]{3,2,1,0:T(8,128)(2,1)S(1)} %bitcast.91, bf16[1,2,2048,256]{3,2,1,0:T(8,128)(2,1)} %bitcast.92, s32[]{:T(128)S(6)} %select_n.161), kind=kLoop, calls=%fused_computation.7 | loop fusion | flops 8388608 | bytes 8388616 | tf_op jit(solution)/shard_map/stack | solution.py:409
  109.7 2.3 collective-permute-start.2
  112.0 5.8 %collective-permute-done.26.refs_0_ = bf16[512,384]{1,0:T(8,128)(2,1)S(1)} collective-permute-done((bf16[512,384]{1,0:T(8,128)(2,1)}, bf16[512,384]{1,0:T(8,128)(2,1)S(1)}, u32[]{:S(2)}, u32[]{:S(2)}) %collective-permute-start.26) | collective-permute-done | bytes 393248 | tf_op jit(solution)/shard_map/ppermute | solution.py:391
  117.8 2.1 collective-permute-start.28
  119.9 23.2 %collective-permute-done.27.refs_1_ = bf16[512,384]{1,0:T(8,128)(2,1)S(1)} collective-permute-done((bf16[512,384]{1,0:T(8,128)(2,1)}, bf16[512,384]{1,0:T(8,128)(2,1)S(1)}, u32[]{:S(2)}, u32[]{:S(2)}) %collective-permute-start.27) | collective-permute-done | bytes 393248 | tf_op jit(solution)/shard_map/ppermute | solution.py:391
  143.1 1.2 collective-permute-start.5
  144.3 1.2 shard_map.111.refs_6_
  145.6 0.8 copy-done.18
  146.7 1.6 shard_map.100.refs_5_
  148.3 8.0 %collective-permute-done.37.refs_1_.refs_7_ = bf16[1536,128]{1,0:T(8,128)(2,1)S(1)} collective-permute-done((bf16[1536,128]{1,0:T(8,128)(2,1)S(1)}, bf16[1536,128]{1,0:T(8,128)(2,1)S(1)}, u32[]{:S(2)}, u32[]{:S(2)}) %collective-permute-start.37) | collective-permute-done | bytes 393248 | tf_op jit(solution)/shard_map/ppermute | solution.py:323
  156.8 16.2 %collective-permute-done.5.refs_0_.refs_2_.refs_3_ = bf16[512,1280]{1,0:T(8,128)(2,1)S(1)} collective-permute-done((bf16[512,1280]{1,0:T(8,128)(2,1)S(1)}, bf16[512,1280]{1,0:T(8,128)(2,1)S(1)}, u32[]{:S(2)}, u32[]{:S(2)}) %collective-permute-start.5) | collective-permute-done | bytes 1310752 | tf_op jit(solution)/shard_map/ppermute | solution.py:323
  173.1 1.2 collective-permute-start.38
  174.3 1.5 shard_map.97
  175.8 30.8 %collective-permute-done.38.refs_0_.refs_8_ = bf16[1536,128]{1,0:T(8,128)(2,1)S(1)} collective-permute-done((bf16[1536,128]{1,0:T(8,128)(2,1)S(1)}, bf16[1536,128]{1,0:T(8,128)(2,1)S(1)}, u32[]{:S(2)}, u32[]{:S(2)}) %collective-permute-start.38) | collective-permute-done | bytes 393248 | tf_op jit(solution)/shard_map/ppermute | solution.py:323
  208.3 1.4 shard_map.105.refs_6_
  210.4 1.3 collective-permute-start.21
  211.7 1.2 collective-permute-start.22
  213.4 9.3 %collective-permute-done.6.refs_3_.refs_4_ = bf16[256,1280]{1,0:T(8,128)(2,1)} collective-permute-done((bf16[256,1280]{1,0:T(8,128)(2,1)}, bf16[256,1280]{1,0:T(8,128)(2,1)}, u32[]{:S(2)}, u32[]{:S(2)}) %collective-permute-start.6) | collective-permute-done | bytes 655392 | tf_op jit(solution)/shard_map/ppermute | solution.py:323
  222.7 1.2 collective-permute-start.30
  224.1 1.9 fusion.2
  226.0 1.3 pad_maximum_fusion.2
  228.5 2.3 shard_map.101
  230.8 17.0 %collective-permute-done.21.refs_1_.refs_7_ = bf16[1536,384]{1,0:T(8,128)(2,1)S(1)} collective-permute-done((bf16[1536,384]{1,0:T(8,128)(2,1)S(1)}, bf16[1536,384]{1,0:T(8,128)(2,1)S(1)}, u32[]{:S(2)}, u32[]{:S(2)}) %collective-permute-start.21) | collective-permute-done | bytes 1179680 | tf_op jit(solution)/shard_map/ppermute | solution.py:323
  247.8 1.2 collective-permute-start.7
  249.3 23.9 %collective-permute-done.29.refs_1_.refs_7_ = bf16[1536,384]{1,0:T(8,128)(2,1)S(1)} collective-permute-done((bf16[1536,384]{1,0:T(8,128)(2,1)S(1)}, bf16[1536,384]{1,0:T(8,128)(2,1)S(1)}, u32[]{:S(2)}, u32[]{:S(2)}) %collective-permute-start.29) | collective-permute-done | bytes 1179680 | tf_op jit(solution)/shard_map/ppermute | solution.py:323
  273.2 1.2 collective-permute-start.15
  274.5 1.7 slice_bitcast_fusion.1
  276.2 1.1 shard_map.106
  278.0 2.4 pad_maximum_fusion
  280.7 16.7 %order_tokens.1.tok_ref = bf16[1024,8192]{1,0:T(8,128)(2,1)} custom-call(s32[32]{0:T(128)} %stack.273.order_ref, bf16[512,8192]{1,0:T(8,128)(2,1)} %collective-permute-done.1.theirs_ref, bf16[512,8192]{1,0:T(8,128)(2,1)} %mine_ref.1), custom_call_target="tpu_custom_call" | custom-call | flops 1000000 | bytes 33554432 | tf_op jit(solution)/shard_map/order_tokens/pallas_call | solution.py:438
  297.4 1.3 collective-permute-start.39
  298.7 1.0 collective-permute-start.40
  300.0 22.7 %shard_map.102 = (bf16[512,128]{1,0:T(8,128)(2,1)}, bf16[512,128]{1,0:T(8,128)(2,1)}, bf16[2,1024,128]{2,1,0:T(8,128)(2,1)}) custom-call(s32[4]{0:T(128)} %copy-done.44, bf16[1024,8192]{1,0:T(8,128)(2,1)} %order_tokens.1.tok_ref, f32[1024,128]{1,0:T(8,128)} %get-tuple-element.75.cos_ref, f32[1024,128]{1,0:T(8,128)} %get-tuple-element.76.sin_ref, ...), custom_call_target="tpu_custom_call" | custom-call | flops 3355443200 | bytes 18874368 | tf_op jit(solution)/shard_map/pallas_call | solution.py:504
  322.7 1.0 slice.23
  323.8 5.6 %collective-permute-start.16 = (bf16[512,128]{1,0:T(8,128)(2,1)}, bf16[512,128]{1,0:T(8,128)(2,1)S(1)}, u32[]{:S(2)}, u32[]{:S(2)}) collective-permute-start(bf16[512,128]{1,0:T(8,128)(2,1)} %get-tuple-element.41), channel_id=1, source_target_pairs={{0,4},{4,0},{8,12},{12,8},{16,20},{20,16},{24,28},{28,24},{1,5},{5... | collective-permute-start | bytes 393224 | tf_op jit(solution)/shard_map/ppermute | solution.py:323
  329.4 30.3 %shard_map.107 = (bf16[512,384]{1,0:T(8,128)(2,1)}, bf16[512,384]{1,0:T(8,128)(2,1)}) custom-call(s32[4]{0:T(128)} %copy-done.44, bf16[1024,8192]{1,0:T(8,128)(2,1)} %order_tokens.1.tok_ref, f32[1024,128]{1,0:T(8,128)} %get-tuple-element.75.cos_ref, f32[1024,128]{1,0:T(8,128)} %get-tuple-element.76.sin_ref, bf16[4,2048,128]{2,1,0:T(8,128)(2,1)} %get-tuple-element.77.ok_ref, ...), custom_call_target="tpu_custom_call" | custom-call | flops 10066329600 | bytes 23068672 | tf_op jit(solution)/shard_map/pallas_call | solution.py:504
  359.7 0.9 collective-permute-start.25
  360.6 0.8 copy-done.49
  361.5 30.1 %shard_map.110 = (bf16[512,384]{1,0:T(8,128)(2,1)}, bf16[512,384]{1,0:T(8,128)(2,1)}) custom-call(s32[4]{0:T(128)} %copy-done.44, bf16[1024,8192]{1,0:T(8,128)(2,1)} %order_tokens.1.tok_ref, f32[1024,128]{1,0:T(8,128)} %get-tuple-element.75.cos_ref, f32[1024,128]{1,0:T(8,128)} %get-tuple-element.76.sin_ref, bf16[4,2048,128]{2,1,0:T(8,128)(2,1)} %get-tuple-element.77.ok_ref, ...), custom_call_target="tpu_custom_call" | custom-call | flops 10066329600 | bytes 23068672 | tf_op jit(solution)/shard_map/pallas_call | solution.py:504
  391.5 0.8 collective-permute-start.33
  393.7 16.7 %shard_map.113 = (bf16[512,128]{1,0:T(8,128)(2,1)}, bf16[512,128]{1,0:T(8,128)(2,1)}) custom-call(s32[4]{0:T(128)} %copy-done.44, bf16[1024,8192]{1,0:T(8,128)(2,1)} %order_tokens.1.tok_ref, f32[1024,128]{1,0:T(8,128)} %get-tuple-element.75.cos_ref, f32[1024,128]{1,0:T(8,128)} %get-tuple-element.76.sin_ref, bf16[4,2048,128]{2,1,0:T(8,128)(2,1)} %get-tuple-element.77.ok_ref, ...), custom_call_target="tpu_custom_call" | custom-call | flops 3355443200 | bytes 18874368 | tf_op jit(solution)/shard_map/pallas_call | solution.py:504
  411.6 0.9 collective-permute-done.42
  412.5 0.9 pad_maximum_fusion.4
  413.8 1.3 copy-done.34
  (175 shorter events, 14.2 us)
Async XLA Ops:
  0.6 95.7 %copy-start = (bf16[32,128,256]{2,1,0:T(8,128)(2,1)S(1)}, bf16[32,128,256]{2,1,0:T(8,128)(2,1)}, u32[]{:S(2)}) copy-start(bf16[32,128,256]{2,1,0:T(8,128)(2,1)} %param.12) | copy-start | bytes 6291460
  0.6 276.9 %collective-permute-start.1 = (bf16[512,8192]{1,0:T(8,128)(2,1)}, bf16[512,8192]{1,0:T(8,128)(2,1)}, u32[]{:S(2)}, u32[]{:S(2)}) collective-permute-start(bf16[512,8192]{1,0:T(8,128)(2,1)} %mine_ref.1), channel_id=1, source_target_pairs={{0,4},{4,0},{8,12},{12,8},{16,20},{20,16},{24,28},{28,24},{1,5},{5... | collective-permute-start | bytes 25165832 | tf_op jit(solution)/shard_map/ppermute | solution.py:323
  5.6 18.0 %collective-permute-start.17 = (bf16[256,2688]{1,0:T(8,128)(2,1)}, bf16[256,2688]{1,0:T(8,128)(2,1)S(1)}, u32[]{:S(2)}, u32[]{:S(2)}) collective-permute-start(bf16[256,2688]{1,0:T(8,128)(2,1)} %shard_map.103), channel_id=1, source_target_pairs={{0,4},{4,0},{8,12},{12,8},{16,20},{20,16},{24,28},{28,24},{1,5},{5... | collective-permute-start | bytes 4128776 | tf_op jit(solution)/shard_map/ppermute | solution.py:323
  8.7 8.5 %collective-permute-start.8 = (bf16[256,1152]{1,0:T(8,128)(2,1)}, bf16[256,1152]{1,0:T(8,128)(2,1)S(1)}, u32[]{:S(2)}, u32[]{:S(2)}) collective-permute-start(bf16[256,1152]{1,0:T(8,128)(2,1)} %shard_map.98), channel_id=1, source_target_pairs={{0,4},{4,0},{8,12},{12,8},{16,20},{20,16},{24,28},{28,24},{1,5},{5... | collective-permute-start | bytes 1769480 | tf_op jit(solution)/shard_map/ppermute | solution.py:323
  12.1 18.0 %collective-permute-start.3 = (bf16[256,1280]{1,0:T(8,128)(2,1)}, bf16[256,1280]{1,0:T(8,128)(2,1)S(1)}, u32[]{:S(2)}, u32[]{:S(2)}) collective-permute-start(bf16[256,1280]{1,0:T(8,128)(2,1)} %shard_map.95), channel_id=1, source_target_pairs={{0,4},{4,0},{8,12},{12,8},{16,20},{20,16},{24,28},{28,24},{1,5},{5... | collective-permute-start | bytes 1966088 | tf_op jit(solution)/shard_map/ppermute | solution.py:323
  12.2 10.0 %collective-permute-start = (s32[1,2]{1,0:T(1,128)S(1)}, s32[1,2]{1,0:T(1,128)S(1)}, u32[]{:S(2)}, u32[]{:S(2)}) collective-permute-start(s32[1,2]{1,0:T(1,128)S(1)} %copy-done.51), channel_id=1, source_target_pairs={{0,4},{4,0},{8,12},{12,8},{16,20},{20,16},{24,28},{28,24},{1,5},{5... | collective-permute-start | bytes 32 | tf_op jit(solution)/shard_map/ppermute | solution.py:323
  22.2 10.6 %collective-permute-start.9 = (bf16[512,384]{1,0:T(8,128)(2,1)}, bf16[512,384]{1,0:T(8,128)(2,1)S(1)}, u32[]{:S(2)}, u32[]{:S(2)}) collective-permute-start(bf16[512,384]{1,0:T(8,128)(2,1)} %get-tuple-element.35), channel_id=1, source_target_pairs={{0,1},{1,2},{2,3},{3,0},{4,5},{5,6},{6,7},{7,4},{8,9},{9,10},{10,1... | collective-permute-start | bytes 1179656 | tf_op jit(solution)/shard_map/ppermute | solution.py:391
  22.3 35.7 %collective-permute-start.10 = (bf16[512,384]{1,0:T(8,128)(2,1)}, bf16[512,384]{1,0:T(8,128)(2,1)S(1)}, u32[]{:S(2)}, u32[]{:S(2)}) collective-permute-start(bf16[512,384]{1,0:T(8,128)(2,1)} %get-tuple-element.36), channel_id=1, source_target_pairs={{0,2},{1,3},{2,0},{3,1},{4,6},{5,7},{6,4},{7,5},{8,10},{9,11},{10,... | collective-permute-start | bytes 1179656 | tf_op jit(solution)/shard_map/ppermute | solution.py:391
  23.6 55.8 %copy-start.45 = (s32[1,2,16]{2,1,0:T(2,128)S(1)}, s32[1,2,16]{2,1,0:T(2,128)}, u32[]{:S(2)}) copy-start(s32[1,2,16]{2,1,0:T(2,128)} %param.15) | copy-start | bytes 388
  23.6 35.1 %collective-permute-start.11 = (bf16[512,384]{1,0:T(8,128)(2,1)}, bf16[512,384]{1,0:T(8,128)(2,1)S(1)}, u32[]{:S(2)}, u32[]{:S(2)}) collective-permute-start(bf16[512,384]{1,0:T(8,128)(2,1)} %get-tuple-element.37), channel_id=1, source_target_pairs={{0,3},{1,0},{2,1},{3,2},{4,7},{5,4},{6,5},{7,6},{8,11},{9,8},{10,9... | collective-permute-start | bytes 1179656 | tf_op jit(solution)/shard_map/ppermute | solution.py:391
  30.0 49.4 %copy-start.36 = (bf16[256,1280]{1,0:T(8,128)(2,1)}, bf16[256,1280]{1,0:T(8,128)(2,1)S(1)}, u32[]{:S(2)}) copy-start(bf16[256,1280]{1,0:T(8,128)(2,1)S(1)} %collective-permute-done.3.refs_3_) | copy-start | bytes 1966084
  30.1 49.3 %collective-permute-start.34 = (bf16[512,128]{1,0:T(8,128)(2,1)}, bf16[512,128]{1,0:T(8,128)(2,1)S(1)}, u32[]{:S(2)}, u32[]{:S(2)}) collective-permute-start(bf16[512,128]{1,0:T(8,128)(2,1)} %get-tuple-element.57), channel_id=1, source_target_pairs={{0,1},{1,2},{2,3},{3,0},{4,5},{5,6},{6,7},{7,4},{8,9},{9,10},{10,1... | collective-permute-start | bytes 393224 | tf_op jit(solution)/shard_map/ppermute | solution.py:391
  33.5 68.6 %collective-permute-start.18 = (bf16[512,384]{1,0:T(8,128)(2,1)}, bf16[512,384]{1,0:T(8,128)(2,1)}, u32[]{:S(2)}, u32[]{:S(2)}) collective-permute-start(bf16[512,384]{1,0:T(8,128)(2,1)} %get-tuple-element.43), channel_id=1, source_target_pairs={{0,1},{1,2},{2,3},{3,0},{4,5},{5,6},{6,7},{7,4},{8,9},{9,10},{10,1... | collective-permute-start | bytes 1179656 | tf_op jit(solution)/shard_map/ppermute | solution.py:391
  58.7 46.6 %collective-permute-start.19 = (bf16[512,384]{1,0:T(8,128)(2,1)}, bf16[512,384]{1,0:T(8,128)(2,1)}, u32[]{:S(2)}, u32[]{:S(2)}) collective-permute-start(bf16[512,384]{1,0:T(8,128)(2,1)} %get-tuple-element.44), channel_id=1, source_target_pairs={{0,2},{1,3},{2,0},{3,1},{4,6},{5,7},{6,4},{7,5},{8,10},{9,11},{10,... | collective-permute-start | bytes 1179656 | tf_op jit(solution)/shard_map/ppermute | solution.py:391
  58.7 25.1 %copy-start.24 = (bf16[512,384]{1,0:T(8,128)(2,1)}, bf16[512,384]{1,0:T(8,128)(2,1)S(1)}, u32[]{:S(2)}) copy-start(bf16[512,384]{1,0:T(8,128)(2,1)S(1)} %collective-permute-done.11.refs_2_) | copy-start | bytes 1179652
  58.7 35.8 %collective-permute-start.35 = (bf16[512,128]{1,0:T(8,128)(2,1)}, bf16[512,128]{1,0:T(8,128)(2,1)S(1)}, u32[]{:S(2)}, u32[]{:S(2)}) collective-permute-start(bf16[512,128]{1,0:T(8,128)(2,1)} %get-tuple-element.58), channel_id=1, source_target_pairs={{0,2},{1,3},{2,0},{3,1},{4,6},{5,7},{6,4},{7,5},{8,10},{9,11},{10,... | collective-permute-start | bytes 393224 | tf_op jit(solution)/shard_map/ppermute | solution.py:391
  79.4 17.0 %collective-permute-start.36 = (bf16[512,128]{1,0:T(8,128)(2,1)}, bf16[512,128]{1,0:T(8,128)(2,1)}, u32[]{:S(2)}, u32[]{:S(2)}) collective-permute-start(bf16[512,128]{1,0:T(8,128)(2,1)} %get-tuple-element.59), channel_id=1, source_target_pairs={{0,3},{1,0},{2,1},{3,2},{4,7},{5,4},{6,5},{7,6},{8,11},{9,8},{10,9... | collective-permute-start | bytes 393224 | tf_op jit(solution)/shard_map/ppermute | solution.py:391
  95.1 61.4 %collective-permute-start.4 = (bf16[512,1280]{1,0:T(8,128)(2,1)}, bf16[512,1280]{1,0:T(8,128)(2,1)S(1)}, u32[]{:S(2)}, u32[]{:S(2)}) collective-permute-start(bf16[512,1280]{1,0:T(8,128)(2,1)} %shard_map.96.refs_0_.refs_1_), channel_id=1, source_target_pairs={{0,8},{4,12},{8,0},{12,4},{16,24},{20,28},{24,16},{28,20},{1,9},{5... | collective-permute-start | bytes 3932168 | tf_op jit(solution)/shard_map/ppermute | solution.py:323
  96.3 13.3 %collective-permute-start.20 = (bf16[512,384]{1,0:T(8,128)(2,1)}, bf16[512,384]{1,0:T(8,128)(2,1)}, u32[]{:S(2)}, u32[]{:S(2)}) collective-permute-start(bf16[512,384]{1,0:T(8,128)(2,1)} %get-tuple-element.45), channel_id=1, source_target_pairs={{0,3},{1,0},{2,1},{3,2},{4,7},{5,4},{6,5},{7,6},{8,11},{9,8},{10,9... | collective-permute-start | bytes 1179656 | tf_op jit(solution)/shard_map/ppermute | solution.py:391
  102.1 15.7 %collective-permute-start.26 = (bf16[512,384]{1,0:T(8,128)(2,1)}, bf16[512,384]{1,0:T(8,128)(2,1)S(1)}, u32[]{:S(2)}, u32[]{:S(2)}) collective-permute-start(bf16[512,384]{1,0:T(8,128)(2,1)} %get-tuple-element.50), channel_id=1, source_target_pairs={{0,1},{1,2},{2,3},{3,0},{4,5},{5,6},{6,7},{7,4},{8,9},{9,10},{10,1... | collective-permute-start | bytes 1179656 | tf_op jit(solution)/shard_map/ppermute | solution.py:391
  105.4 37.7 %collective-permute-start.27 = (bf16[512,384]{1,0:T(8,128)(2,1)}, bf16[512,384]{1,0:T(8,128)(2,1)S(1)}, u32[]{:S(2)}, u32[]{:S(2)}) collective-permute-start(bf16[512,384]{1,0:T(8,128)(2,1)} %get-tuple-element.51), channel_id=1, source_target_pairs={{0,2},{1,3},{2,0},{3,1},{4,6},{5,7},{6,4},{7,5},{8,10},{9,11},{10,... | collective-permute-start | bytes 1179656 | tf_op jit(solution)/shard_map/ppermute | solution.py:391
  105.4 12.4 %copy-start.50 = (bf16[512,384]{1,0:T(8,128)(2,1)S(1)}, bf16[512,384]{1,0:T(8,128)(2,1)}, u32[]{:S(2)}) copy-start(bf16[512,384]{1,0:T(8,128)(2,1)} %get-tuple-element.52) | copy-start | bytes 1179652
  105.4 37.7 %copy-start.30 = (bf16[512,1280]{1,0:T(8,128)(2,1)S(1)}, bf16[512,1280]{1,0:T(8,128)(2,1)}, u32[]{:S(2)}) copy-start(bf16[512,1280]{1,0:T(8,128)(2,1)} %shard_map.96.refs_0_.refs_1_) | copy-start | bytes 3932164
  105.4 39.0 %copy-start.27 = (bf16[512,128]{1,0:T(8,128)(2,1)S(1)}, bf16[512,128]{1,0:T(8,128)(2,1)}, u32[]{:S(2)}) copy-start(bf16[512,128]{1,0:T(8,128)(2,1)} %copy-done.26) | copy-start | bytes 393220
  105.4 41.3 %copy-start.21 = (bf16[512,384]{1,0:T(8,128)(2,1)S(1)}, bf16[512,384]{1,0:T(8,128)(2,1)}, u32[]{:S(2)}) copy-start(bf16[512,384]{1,0:T(8,128)(2,1)} %copy-done.20) | copy-start | bytes 1179652
  105.4 41.3 %copy-start.23 = (bf16[512,384]{1,0:T(8,128)(2,1)S(1)}, bf16[512,384]{1,0:T(8,128)(2,1)}, u32[]{:S(2)}) copy-start(bf16[512,384]{1,0:T(8,128)(2,1)} %copy-done.22) | copy-start | bytes 1179652
  105.4 41.3 %copy-start.25 = (bf16[512,384]{1,0:T(8,128)(2,1)S(1)}, bf16[512,384]{1,0:T(8,128)(2,1)}, u32[]{:S(2)}) copy-start(bf16[512,384]{1,0:T(8,128)(2,1)} %copy-done.24) | copy-start | bytes 1179652
  109.7 100.7 %collective-permute-start.2 = (bf16[2,2,2048,128]{3,2,1,0:T(8,128)(2,1)}, bf16[2,2,2048,128]{3,2,1,0:T(8,128)(2,1)}, u32[]{:S(2)}, u32[]{:S(2)}) collective-permute-start(bf16[2,2,2048,128]{3,2,1,0:T(8,128)(2,1)} %get-tuple-element.64), channel_id=1, source_target_pairs={{0,4},{4,0},{8,12},{12,8},{16,20},{20,16},{24,28},{28,24},{1,5},{5... | collective-permute-start | bytes 6291464 | tf_op jit(solution)/shard_map/ppermute | solution.py:323
  117.8 58.0 %copy-start.14 = (bf16[512,384]{1,0:T(8,128)(2,1)}, bf16[512,384]{1,0:T(8,128)(2,1)S(1)}, u32[]{:S(2)}) copy-start(bf16[512,384]{1,0:T(8,128)(2,1)S(1)} %collective-permute-done.26.refs_0_) | copy-start | bytes 1179652
  117.8 27.8 %collective-permute-start.28 = (bf16[512,384]{1,0:T(8,128)(2,1)S(1)}, bf16[512,384]{1,0:T(8,128)(2,1)S(1)}, u32[]{:S(2)}, u32[]{:S(2)}) collective-permute-start(bf16[512,384]{1,0:T(8,128)(2,1)S(1)} %copy-done.50), channel_id=1, source_target_pairs={{0,3},{1,0},{2,1},{3,2},{4,7},{5,4},{6,5},{7,6},{8,11},{9,8},{10,9... | collective-permute-start | bytes 1179656 | tf_op jit(solution)/shard_map/ppermute | solution.py:391
  143.1 32.7 %copy-start.16 = (bf16[512,384]{1,0:T(8,128)(2,1)}, bf16[512,384]{1,0:T(8,128)(2,1)S(1)}, u32[]{:S(2)}) copy-start(bf16[512,384]{1,0:T(8,128)(2,1)S(1)} %collective-permute-done.27.refs_1_) | copy-start | bytes 1179652
  143.1 29.9 %collective-permute-start.5 = (bf16[512,1280]{1,0:T(8,128)(2,1)S(1)}, bf16[512,1280]{1,0:T(8,128)(2,1)S(1)}, u32[]{:S(2)}, u32[]{:S(2)}) collective-permute-start(bf16[512,1280]{1,0:T(8,128)(2,1)S(1)} %copy-done.30), channel_id=1, source_target_pairs={{0,16},{4,20},{8,24},{12,28},{16,0},{20,4},{24,8},{28,12},{1,17},{... | collective-permute-start | bytes 3932168 | tf_op jit(solution)/shard_map/ppermute | solution.py:323
  145.6 30.2 %copy-start.4 = (bf16[1536,128]{1,0:T(8,128)(2,1)}, bf16[1536,128]{1,0:T(8,128)(2,1)S(1)}, u32[]{:S(2)}) copy-start(bf16[1536,128]{1,0:T(8,128)(2,1)S(1)} %shard_map.111.refs_6_) | copy-start | bytes 1179652
  146.4 9.9 %collective-permute-start.37 = (bf16[1536,128]{1,0:T(8,128)(2,1)S(1)}, bf16[1536,128]{1,0:T(8,128)(2,1)S(1)}, u32[]{:S(2)}, u32[]{:S(2)}) collective-permute-start(bf16[1536,128]{1,0:T(8,128)(2,1)S(1)} %shard_map.111.refs_6_), channel_id=1, source_target_pairs={{0,8},{4,12},{8,0},{12,4},{16,24},{20,28},{24,16},{28,20},{1,9},{5... | collective-permute-start | bytes 1179656 | tf_op jit(solution)/shard_map/ppermute | solution.py:323
  156.3 71.0 %copy-start.5 = (bf16[1536,128]{1,0:T(8,128)(2,1)}, bf16[1536,128]{1,0:T(8,128)(2,1)S(1)}, u32[]{:S(2)}) copy-start(bf16[1536,128]{1,0:T(8,128)(2,1)S(1)} %collective-permute-done.37.refs_1_.refs_7_) | copy-start | bytes 1179652
  156.3 55.4 %collective-permute-start.12 = (bf16[1536,384]{1,0:T(8,128)(2,1)}, bf16[1536,384]{1,0:T(8,128)(2,1)}, u32[]{:S(2)}, u32[]{:S(2)}) collective-permute-start(bf16[1536,384]{1,0:T(8,128)(2,1)} %shard_map.100.refs_5_), channel_id=1, source_target_pairs={{0,8},{4,12},{8,0},{12,4},{16,24},{20,28},{24,16},{28,20},{1,9},{5... | collective-permute-start | bytes 3538952 | tf_op jit(solution)/shard_map/ppermute | solution.py:323
  156.6 53.2 %copy-start.2 = (bf16[512,1280]{1,0:T(8,128)(2,1)}, bf16[512,1280]{1,0:T(8,128)(2,1)S(1)}, u32[]{:S(2)}) copy-start(bf16[512,1280]{1,0:T(8,128)(2,1)S(1)} %collective-permute-done.4.refs_1_.refs_2_) | copy-start | bytes 3932164
  156.6 56.4 %collective-permute-start.13 = (bf16[1536,384]{1,0:T(8,128)(2,1)}, bf16[1536,384]{1,0:T(8,128)(2,1)}, u32[]{:S(2)}, u32[]{:S(2)}) collective-permute-start(bf16[1536,384]{1,0:T(8,128)(2,1)} %shard_map.100.refs_5_), channel_id=1, source_target_pairs={{0,16},{4,20},{8,24},{12,28},{16,0},{20,4},{24,8},{28,12},{1,17},{... | collective-permute-start | bytes 3538952 | tf_op jit(solution)/shard_map/ppermute | solution.py:323
  173.0 36.7 %copy-start.3 = (bf16[512,1280]{1,0:T(8,128)(2,1)}, bf16[512,1280]{1,0:T(8,128)(2,1)S(1)}, u32[]{:S(2)}) copy-start(bf16[512,1280]{1,0:T(8,128)(2,1)S(1)} %collective-permute-done.5.refs_0_.refs_2_.refs_3_) | copy-start | bytes 3932164
  173.1 33.6 %collective-permute-start.38 = (bf16[1536,128]{1,0:T(8,128)(2,1)S(1)}, bf16[1536,128]{1,0:T(8,128)(2,1)S(1)}, u32[]{:S(2)}, u32[]{:S(2)}) collective-permute-start(bf16[1536,128]{1,0:T(8,128)(2,1)S(1)} %shard_map.111.refs_6_), channel_id=1, source_target_pairs={{0,16},{4,20},{8,24},{12,28},{16,0},{20,4},{24,8},{28,12},{1,17},{... | collective-permute-start | bytes 1179656 | tf_op jit(solution)/shard_map/ppermute | solution.py:323
  207.4 15.3 %collective-permute-start.6 = (bf16[256,1280]{1,0:T(8,128)(2,1)}, bf16[256,1280]{1,0:T(8,128)(2,1)}, u32[]{:S(2)}, u32[]{:S(2)}) collective-permute-start(bf16[256,1280]{1,0:T(8,128)(2,1)} %get-tuple-element.33), channel_id=1, source_target_pairs={{0,8},{4,12},{8,0},{12,4},{16,24},{20,28},{24,16},{28,20},{1,9},{5... | collective-permute-start | bytes 1966088 | tf_op jit(solution)/shard_map/ppermute | solution.py:323
  210.4 12.2 %copy-start.8 = (bf16[1536,384]{1,0:T(8,128)(2,1)}, bf16[1536,384]{1,0:T(8,128)(2,1)S(1)}, u32[]{:S(2)}) copy-start(bf16[1536,384]{1,0:T(8,128)(2,1)S(1)} %shard_map.108.refs_6_) | copy-start | bytes 3538948
  210.4 37.4 %collective-permute-start.21 = (bf16[1536,384]{1,0:T(8,128)(2,1)S(1)}, bf16[1536,384]{1,0:T(8,128)(2,1)S(1)}, u32[]{:S(2)}, u32[]{:S(2)}) collective-permute-start(bf16[1536,384]{1,0:T(8,128)(2,1)S(1)} %shard_map.105.refs_6_), channel_id=1, source_target_pairs={{0,8},{4,12},{8,0},{12,4},{16,24},{20,28},{24,16},{28,20},{1,9},{5... | collective-permute-start | bytes 3538952 | tf_op jit(solution)/shard_map/ppermute | solution.py:323
  211.7 37.4 %collective-permute-start.22 = (bf16[1536,384]{1,0:T(8,128)(2,1)S(1)}, bf16[1536,384]{1,0:T(8,128)(2,1)S(1)}, u32[]{:S(2)}, u32[]{:S(2)}) collective-permute-start(bf16[1536,384]{1,0:T(8,128)(2,1)S(1)} %shard_map.105.refs_6_), channel_id=1, source_target_pairs={{0,16},{4,20},{8,24},{12,28},{16,0},{20,4},{24,8},{28,12},{1,17},{... | collective-permute-start | bytes 3538952 | tf_op jit(solution)/shard_map/ppermute | solution.py:323
  213.0 60.3 %collective-permute-start.29 = (bf16[1536,384]{1,0:T(8,128)(2,1)S(1)}, bf16[1536,384]{1,0:T(8,128)(2,1)S(1)}, u32[]{:S(2)}, u32[]{:S(2)}) collective-permute-start(bf16[1536,384]{1,0:T(8,128)(2,1)S(1)} %shard_map.108.refs_6_), channel_id=1, source_target_pairs={{0,8},{4,12},{8,0},{12,4},{16,24},{20,28},{24,16},{28,20},{1,9},{5... | collective-permute-start | bytes 3538952 | tf_op jit(solution)/shard_map/ppermute | solution.py:323
  222.7 54.6 %collective-permute-start.30 = (bf16[1536,384]{1,0:T(8,128)(2,1)S(1)}, bf16[1536,384]{1,0:T(8,128)(2,1)S(1)}, u32[]{:S(2)}, u32[]{:S(2)}) collective-permute-start(bf16[1536,384]{1,0:T(8,128)(2,1)S(1)} %shard_map.108.refs_6_), channel_id=1, source_target_pairs={{0,16},{4,20},{8,24},{12,28},{16,0},{20,4},{24,8},{28,12},{1,17},{... | collective-permute-start | bytes 3538952 | tf_op jit(solution)/shard_map/ppermute | solution.py:323
  247.8 28.3 %copy-start.11 = (bf16[1536,384]{1,0:T(8,128)(2,1)}, bf16[1536,384]{1,0:T(8,128)(2,1)S(1)}, u32[]{:S(2)}) copy-start(bf16[1536,384]{1,0:T(8,128)(2,1)S(1)} %collective-permute-done.21.refs_1_.refs_7_) | copy-start | bytes 3538948
  247.8 49.6 %collective-permute-start.7 = (bf16[256,1280]{1,0:T(8,128)(2,1)}, bf16[256,1280]{1,0:T(8,128)(2,1)}, u32[]{:S(2)}, u32[]{:S(2)}) collective-permute-start(bf16[256,1280]{1,0:T(8,128)(2,1)} %get-tuple-element.34), channel_id=1, source_target_pairs={{0,16},{4,20},{8,24},{12,28},{16,0},{20,4},{24,8},{28,12},{1,17},{... | collective-permute-start | bytes 1966088 | tf_op jit(solution)/shard_map/ppermute | solution.py:323
  249.1 27.1 %copy-start.12 = (bf16[1536,384]{1,0:T(8,128)(2,1)}, bf16[1536,384]{1,0:T(8,128)(2,1)S(1)}, u32[]{:S(2)}) copy-start(bf16[1536,384]{1,0:T(8,128)(2,1)S(1)} %collective-permute-done.22.refs_0_.refs_8_) | copy-start | bytes 3538948
  249.1 49.6 %collective-permute-start.14 = (bf16[768,384]{1,0:T(8,128)(2,1)}, bf16[768,384]{1,0:T(8,128)(2,1)}, u32[]{:S(2)}, u32[]{:S(2)}) collective-permute-start(bf16[768,384]{1,0:T(8,128)(2,1)} %get-tuple-element.38), channel_id=1, source_target_pairs={{0,8},{4,12},{8,0},{12,4},{16,24},{20,28},{24,16},{28,20},{1,9},{5... | collective-permute-start | bytes 1769480 | tf_op jit(solution)/shard_map/ppermute | solution.py:323
  273.2 7.2 %copy-start.10 = (bf16[1536,384]{1,0:T(8,128)(2,1)}, bf16[1536,384]{1,0:T(8,128)(2,1)S(1)}, u32[]{:S(2)}) copy-start(bf16[1536,384]{1,0:T(8,128)(2,1)S(1)} %collective-permute-done.29.refs_1_.refs_7_) | copy-start | bytes 3538948
  273.2 26.5 %collective-permute-start.15 = (bf16[768,384]{1,0:T(8,128)(2,1)}, bf16[768,384]{1,0:T(8,128)(2,1)}, u32[]{:S(2)}, u32[]{:S(2)}) collective-permute-start(bf16[768,384]{1,0:T(8,128)(2,1)} %get-tuple-element.39), channel_id=1, source_target_pairs={{0,16},{4,20},{8,24},{12,28},{16,0},{20,4},{24,8},{28,12},{1,17},{... | collective-permute-start | bytes 1769480 | tf_op jit(solution)/shard_map/ppermute | solution.py:323
  277.3 46.4 %collective-permute-start.23 = (bf16[768,384]{1,0:T(8,128)(2,1)}, bf16[768,384]{1,0:T(8,128)(2,1)S(1)}, u32[]{:S(2)}, u32[]{:S(2)}) collective-permute-start(bf16[768,384]{1,0:T(8,128)(2,1)} %get-tuple-element.46), channel_id=1, source_target_pairs={{0,8},{4,12},{8,0},{12,4},{16,24},{20,28},{24,16},{28,20},{1,9},{5... | collective-permute-start | bytes 1769480 | tf_op jit(solution)/shard_map/ppermute | solution.py:323
  277.6 46.2 %collective-permute-start.24 = (bf16[768,384]{1,0:T(8,128)(2,1)S(1)}, bf16[768,384]{1,0:T(8,128)(2,1)S(1)}, u32[]{:S(2)}, u32[]{:S(2)}) collective-permute-start(bf16[768,384]{1,0:T(8,128)(2,1)S(1)} %get-tuple-element.47), channel_id=1, source_target_pairs={{0,16},{4,20},{8,24},{12,28},{16,0},{20,4},{24,8},{28,12},{1,17},{... | collective-permute-start | bytes 1769480 | tf_op jit(solution)/shard_map/ppermute | solution.py:323
  280.6 16.8 %copy-start.29 = (bf16[768,128]{1,0:T(8,128)(2,1)S(1)}, bf16[768,128]{1,0:T(8,128)(2,1)}, u32[]{:S(2)}) copy-start(bf16[768,128]{1,0:T(8,128)(2,1)} %copy-done.28) | copy-start | bytes 589828
  297.4 94.9 %collective-permute-start.39 = (bf16[768,128]{1,0:T(8,128)(2,1)S(1)}, bf16[768,128]{1,0:T(8,128)(2,1)S(1)}, u32[]{:S(2)}, u32[]{:S(2)}) collective-permute-start(bf16[768,128]{1,0:T(8,128)(2,1)S(1)} %copy-done.29), channel_id=1, source_target_pairs={{0,8},{4,12},{8,0},{12,4},{16,24},{20,28},{24,16},{28,20},{1,9},{5... | collective-permute-start | bytes 589832 | tf_op jit(solution)/shard_map/ppermute | solution.py:323
  298.7 93.6 %collective-permute-start.40 = (bf16[768,128]{1,0:T(8,128)(2,1)S(1)}, bf16[768,128]{1,0:T(8,128)(2,1)S(1)}, u32[]{:S(2)}, u32[]{:S(2)}) collective-permute-start(bf16[768,128]{1,0:T(8,128)(2,1)S(1)} %get-tuple-element.61), channel_id=1, source_target_pairs={{0,16},{4,20},{8,24},{12,28},{16,0},{20,4},{24,8},{28,12},{1,17},{... | collective-permute-start | bytes 589832 | tf_op jit(solution)/shard_map/ppermute | solution.py:323
  299.7 60.0 %collective-permute-start.31 = (bf16[768,384]{1,0:T(8,128)(2,1)S(1)}, bf16[768,384]{1,0:T(8,128)(2,1)S(1)}, u32[]{:S(2)}, u32[]{:S(2)}) collective-permute-start(bf16[768,384]{1,0:T(8,128)(2,1)S(1)} %get-tuple-element.53), channel_id=1, source_target_pairs={{0,8},{4,12},{8,0},{12,4},{16,24},{20,28},{24,16},{28,20},{1,9},{5... | collective-permute-start | bytes 1769480 | tf_op jit(solution)/shard_map/ppermute | solution.py:323
  323.7 36.9 %collective-permute-start.32 = (bf16[768,384]{1,0:T(8,128)(2,1)S(1)}, bf16[768,384]{1,0:T(8,128)(2,1)S(1)}, u32[]{:S(2)}, u32[]{:S(2)}) collective-permute-start(bf16[768,384]{1,0:T(8,128)(2,1)S(1)} %get-tuple-element.54), channel_id=1, source_target_pairs={{0,16},{4,20},{8,24},{12,28},{16,0},{20,4},{24,8},{28,12},{1,17},{... | collective-permute-start | bytes 1769480 | tf_op jit(solution)/shard_map/ppermute | solution.py:323
  323.8 87.6 %collective-permute-start.16 = (bf16[512,128]{1,0:T(8,128)(2,1)}, bf16[512,128]{1,0:T(8,128)(2,1)S(1)}, u32[]{:S(2)}, u32[]{:S(2)}) collective-permute-start(bf16[512,128]{1,0:T(8,128)(2,1)} %get-tuple-element.41), channel_id=1, source_target_pairs={{0,4},{4,0},{8,12},{12,8},{16,20},{20,16},{24,28},{28,24},{1,5},{5... | collective-permute-start | bytes 393224 | tf_op jit(solution)/shard_map/ppermute | solution.py:323
  359.7 53.7 %collective-permute-start.25 = (bf16[512,384]{1,0:T(8,128)(2,1)}, bf16[512,384]{1,0:T(8,128)(2,1)S(1)}, u32[]{:S(2)}, u32[]{:S(2)}) collective-permute-start(bf16[512,384]{1,0:T(8,128)(2,1)} %get-tuple-element.49), channel_id=1, source_target_pairs={{0,4},{4,0},{8,12},{12,8},{16,20},{20,16},{24,28},{28,24},{1,5},{5... | collective-permute-start | bytes 1179656 | tf_op jit(solution)/shard_map/ppermute | solution.py:323
  391.5 22.1 %collective-permute-start.33 = (bf16[512,384]{1,0:T(8,128)(2,1)}, bf16[512,384]{1,0:T(8,128)(2,1)S(1)}, u32[]{:S(2)}, u32[]{:S(2)}) collective-permute-start(bf16[512,384]{1,0:T(8,128)(2,1)} %get-tuple-element.56), channel_id=1, source_target_pairs={{0,4},{4,0},{8,12},{12,8},{16,20},{20,16},{24,28},{28,24},{1,5},{5... | collective-permute-start | bytes 1179656 | tf_op jit(solution)/shard_map/ppermute | solution.py:323
  410.5 3.3 collective-permute-start.41
  410.5 1.9 collective-permute-start.42
  (31 other events, 67.1 us)

commit v2 on v1

--- a/solution.py
+++ b/solution.py
@@ -19,7 +19,8 @@
 VMEM_LIMIT = 56 * 1024 * 1024
 BF = jnp.bfloat16
 
-HEAD_CHUNKS = (1, 3, 3, 1)
+HEAD_CHUNKS = (0, 3, 3, 2)
+SPLIT = ()
 OWN_ORDER = (0, 1, 2, 3)
 
 
@@ -198,56 +199,108 @@
     return jnp.broadcast_to(column, (column.shape[0], 128))
 
 
-def order_kernel(shard, order_ref, theirs_ref, mine_ref, out_ref, sems):
-    i = pl.program_id(0)
-    rows, depth = out_ref.shape
-    half = pl.num_programs(0) // 2
-
-    def copies(ref, first):
-        for k in range(depth // shard):
-            src = ref.at[pl.ds(first, rows), pl.ds(pl.multiple_of(order_ref[k] * shard, shard), shard)]
-            yield pltpu.make_async_copy(src, out_ref.at[:, pl.ds(k * shard, shard)], sems.at[k])
-
-    @pl.when(i < half)
-    def _():
-        for copy in copies(theirs_ref, i * rows):
-            copy.start()
-
-    @pl.when(i >= half)
-    def _():
-        for copy in copies(mine_ref, (i - half) * rows):
-            copy.start()
-
-    for copy in copies(mine_ref, 0):
+def pages_kernel(core_ref, table_ref, ck_ref, cv_ref, mine_ref, theirs_ref, sems):
+    seqs, pages = table_ref.shape
+    size = ck_ref.shape[1]
+    copies = []
+    for k, ref in enumerate((ck_ref, cv_ref)):
+        for s in range(seqs):
+            for p in range(pages):
+                for h, out in ((core_ref[0], mine_ref), (1 - core_ref[0], theirs_ref)):
+                    src = ref.at[table_ref[s, p], :, pl.ds(pl.multiple_of(h * HEAD_DIM, HEAD_DIM), HEAD_DIM)]
+                    copy = pltpu.make_async_copy(src, out.at[k, s, pl.ds(p * size, size)], sems.at[len(copies)])
+                    copy.start()
+                    copies.append(copy)
+    for copy in copies:
         copy.wait()
 
 
-def chunk_kernel(places, heads, with_kv, block, len_ref, tok_ref, cos_ref, sin_ref, ok_ref, ov_ref, *refs):
+def chunk_kernel(
+    shard, places, heads, with_kv, block, base, n_out, len_ref, order_ref, cos_ref, sin_ref,
+    their_tok, my_tok, their_old, my_old, *refs
+):
+    if not with_kv:
+        fresh_ref, refs = refs[0], refs[1:]
+    weights, refs = refs[: len(places)], refs[len(places) :]
+    out_refs, refs = refs[:n_out], refs[n_out:]
     if with_kv:
-        weights, refs = refs[: len(places)], refs[len(places) :]
-        theirs_ref, mine_ref, fresh_ref = refs[:3]
-        refs = refs[3:]
-    else:
-        fresh_ref, weights, refs = refs[0], refs[1 : 1 + len(places)], refs[1 + len(places) :]
-        theirs_ref, mine_ref = refs[:2]
-        refs = refs[2:]
-    q_ref, e_ref, m_ref, l_ref, top_ref, acc_ref = refs
-    i = pl.program_id(0)
-    new = tok_ref.shape[0]
+        fresh_ref, refs = refs[0], refs[1:]
+    tok_ref, w_ref, old_ref, q_ref, e_ref, m_ref, l_ref, top_ref, acc_ref, sems, w_sems = refs
+    step = pl.program_id(0)
+    steps = pl.num_programs(0)
+    i = step + base
+    slot = step % 2
+    new = tok_ref.shape[1]
     length = len_ref[i]
     blocks = (length + block - 1) // block
     factor = (1.0 / HEAD_DIM**0.5) * 1.4426950408889634
     nt = (((1,), (1,)), ((), ()))
-
-    raw = None
-    for place, ref in zip(places, weights):
-        part = jnp.dot(tok_ref[:, place : place + ref.shape[0]], ref[...], preferred_element_type=jnp.float32)
-        raw = part if raw is None else raw + part
+    seqs = their_old.shape[1]
+
+    def inputs(tok, old, seq, slot):
+        return [
+            pltpu.make_async_copy(tok.at[pl.ds(seq * new, new)], tok_ref.at[slot], sems.at[slot, 0]),
+            pltpu.make_async_copy(old.at[0, seq], old_ref.at[slot, 0], sems.at[slot, 1]),
+            pltpu.make_async_copy(old.at[1, seq], old_ref.at[slot, 1], sems.at[slot, 2]),
+        ]
+
+    def fetch(seq, slot):
+        @pl.when(seq < seqs)
+        def _():
+            for copy in inputs(their_tok, their_old, seq, slot):
+                copy.start()
+
+        @pl.when(seq >= seqs)
+        def _():
+            for copy in inputs(my_tok, my_old, seq - seqs, slot):
+                copy.start()
+
+    copies = []
+    for (entry, col), ref in zip(places, weights):
+        for j in range(ref.shape[0] // shard):
+            to = pl.multiple_of(order_ref[entry + j] * shard, shard)
+            copies.append(
+                pltpu.make_async_copy(
+                    ref.at[pl.ds(j * shard, shard), pl.ds(col, w_ref.shape[1])],
+                    w_ref.at[pl.ds(to, shard)],
+                    w_sems.at[len(copies)],
+                )
+            )
+
+    @pl.when(step == 0)
+    def _():
+        fetch(i, slot)
+        for copy in copies:
+            copy.start()
+
+    @pl.when(step + 1 < steps)
+    def _():
+        fetch(i + 1, 1 - slot)
+
+    for copy in inputs(my_tok, my_old, 0, slot):
+        copy.wait()
+
+    @pl.when(step == 0)
+    def _():
+        for copy in copies:
+            copy.wait()
+
+    raw = jnp.dot(tok_ref[slot], w_ref[...], preferred_element_type=jnp.float32)
     raw = [raw[:, h * HEAD_DIM : (h + 1) * HEAD_DIM] for h in range(raw.shape[1] // HEAD_DIM)]
     if with_kv:
         fresh_ref[0] = rotate(raw[0], cos_ref[...], sin_ref[...]).astype(BF)
         fresh_ref[1] = raw[1].astype(BF)
         raw = raw[2:]
+    if heads == 0:
+        half = steps // 2
+
+        def write_new(out_ref):
+            for k in range(2):
+                out_ref[:, k * HEAD_DIM : (k + 1) * HEAD_DIM] = fresh_ref[k]
+
+        pl.when(step < half)(lambda: write_new(out_refs[0]))
+        pl.when(step >= half)(lambda: write_new(out_refs[1]))
+        return
     for h in range(heads):
         q_ref[h * new : (h + 1) * new, :] = rotate(raw[h], cos_ref[...], sin_ref[...]).astype(BF)
 
@@ -265,7 +318,7 @@
     @pl.loop(0, blocks)
     def _(b):
         start = pl.multiple_of(b * block, block)
-        s = lax.dot_general(q_ref[...], ok_ref[0, pl.ds(start, block), :], nt, preferred_element_type=jnp.float32)
+        s = lax.dot_general(q_ref[...], old_ref[slot, 0, pl.ds(start, block), :], nt, preferred_element_type=jnp.float32)
         at = lax.broadcasted_iota(jnp.int32, s.shape, 1)
         parts = lanes(jnp.where(at < length - start, s, -1e30))
         before = m_ref[b]
@@ -295,16 +348,23 @@
     def _(b):
         start = pl.multiple_of(b * block, block)
         acc_ref[...] += jnp.dot(
-            probs(b + 1, block // 128), ov_ref[0, pl.ds(start, block), :], preferred_element_type=jnp.float32
+            probs(b + 1, block // 128), old_ref[slot, 1, pl.ds(start, block), :], preferred_element_type=jnp.float32
         )
 
     def write(out_ref):
+        if with_kv:
+            for k in range(2):
+                cols = slice((heads + k) * HEAD_DIM, (heads + k + 1) * HEAD_DIM)
+                out_ref[:, cols] = fresh_ref[k]
         for h in range(heads):
             out_ref[:, h * HEAD_DIM : (h + 1) * HEAD_DIM] = acc_ref[h * new : (h + 1) * new, :].astype(BF)
 
-    half = pl.num_programs(0) // 2
-    pl.when(i < half)(lambda: write(theirs_ref))
-    pl.when(i >= half)(lambda: write(mine_ref))
+    if n_out == 1:
+        write(out_refs[0])
+    else:
+        half = pl.num_programs(0) // 2
+        pl.when(step < half)(lambda: write(out_refs[0]))
+        pl.when(step >= half)(lambda: write(out_refs[1]))
 
 
 def by_core(R, T, tokens, query_weight, key_weight, value_weight, cache_keys, cache_values, lengths, page_table):
@@ -352,14 +412,10 @@
         return [
             (row, col, HEAD_DIM, 1, base + 1),
             (row, col + HEAD_DIM, HEAD_DIM, 2, base + 2),
-            (row, col + 2 * HEAD_DIM, widths[0] - 2 * HEAD_DIM, 0, q_base),
-        ]
+        ] + ([(row, col + 2 * HEAD_DIM, widths[0] - 2 * HEAD_DIM, 0, q_base)] if head_chunks[0] else [])
 
     def all_chunks(s, other, row, col):
         return [p for c in range(n_chunks) for p in pieces(s, other, c, row, col + own_firsts[c])]
-
-    send_a = pack([all_chunks(0, 1, 0, 0)], [(shard, whole)], starts, weights, [])[0]
-    got_a = xor(send_a, 1)
 
     def their_half(chunks):
         job, col, place = [], 0, {}
@@ -379,8 +435,10 @@
 
     send_b, place_b = their_half([0])
     got_b = xor(send_b, 1)
-    own = pack([all_chunks(0, 0, 0, 0) + [(shard, 0, whole, 3, 0)]], [(2 * shard, whole)], starts, weights, [got_a])[0]
+    own_mine = pack([all_chunks(0, 0, 0, 0)], [(shard, whole)], starts, weights, [])[0]
     ready = to_send(got_b, place_b)
+    send_a = pack([all_chunks(0, 1, 0, 0)], [(shard, whole)], starts, weights, [])[0]
+    own_other = xor(send_a, 1)
     send_c, place_c = their_half(range(1, n_chunks))
     got_c = xor(send_c, 1)
     ready.update(to_send(got_c, place_c))
@@ -401,41 +459,42 @@
         far = [(6, 0, xor(low, 2)), (6, n, xor(high, 4))]
         return [(0, 0, piece), (2, 0, by_x), (4, 0, by_y), *far]
 
-    own_all = gather(own)
+    by_x, by_y = xor(own_mine, 2), xor(own_mine, 4)
+    other_x, other_y = xor(own_other, 2), xor(own_other, 4)
+    own_all = [
+        (0, 0, own_mine), (0, shard, own_other), (2, 0, by_x), (2, shard, other_x), (4, 0, by_y),
+        (4, shard, other_y), (6, 0, xor(by_y, 2)), (6, shard, xor(other_x, 4)),
+    ]
     rest_all = [gather(over_tp(c)) for c in range(n_chunks)]
 
     their_tokens = xor(tokens, 1)
     seq_lengths = jnp.concatenate([xor(lengths, 1)[0], lengths[0]])
-    old = jnp.stack(
-        [a[page_table[0]].reshape(seqs, max_len, kv_width) for a in (cache_keys, cache_values)]
-    )
-    mine_old = lax.dynamic_slice_in_dim(old, core * HEAD_DIM, HEAD_DIM, 3)
-    their_old = xor(lax.dynamic_slice_in_dim(old, (1 - core) * HEAD_DIM, HEAD_DIM, 3), 1)
-    old_keys, old_values = [jnp.concatenate([their_old[k], mine_old[k]], axis=0) for k in range(2)]
+    old_shape = (2, seqs, max_len, HEAD_DIM)
+    call = pl.pallas_call(
+        pages_kernel,
+        out_shape=[jax.ShapeDtypeStruct(old_shape, BF)] * 2,
+        grid_spec=pltpu.PrefetchScalarGridSpec(
+            num_scalar_prefetch=2,
+            grid=(1,),
+            in_specs=[pl.BlockSpec(memory_space=pl.ANY)] * 2,
+            out_specs=[pl.BlockSpec(old_shape, lambda i, *_: (0, 0, 0, 0))] * 2,
+            scratch_shapes=[pltpu.SemaphoreType.DMA((4 * seqs * page_table.shape[2],))],
+        ),
+        compiler_params=pltpu.CompilerParams(vmem_limit_bytes=VMEM_LIMIT),
+        cost_estimate=pl.CostEstimate(flops=1000000, bytes_accessed=8000000, transcendentals=0),
+        name="old",
+    )
+    my_old, for_them = call(core[None].astype(jnp.int32), page_table[0], cache_keys, cache_values)
+    their_old = xor(for_them, 1)
 
     order, place = [], {}
     for shifts in ([0], list(range(1, T))):
         for d in range(0, R, 2):
-            place[d, shifts[0]] = len(order) * shard
+            place[d, shifts[0]] = len(order)
             order += [(r ^ (d + e)) * T + (z - s) % T for s in shifts for e in range(2)]
     order = jnp.stack(order).astype(jnp.int32)
     rows_all = 2 * tok_rows
     params = pltpu.CompilerParams(vmem_limit_bytes=VMEM_LIMIT)
-    call = pl.pallas_call(
-        functools.partial(order_kernel, shard),
-        out_shape=jax.ShapeDtypeStruct((rows_all, depth), BF),
-        grid_spec=pltpu.PrefetchScalarGridSpec(
-            num_scalar_prefetch=1,
-            grid=(2 * seqs,),
-            in_specs=[pl.BlockSpec(memory_space=pl.ANY)] * 2,
-            out_specs=pl.BlockSpec((new, depth), lambda i, _: (i, 0)),
-            scratch_shapes=[pltpu.SemaphoreType.DMA((depth // shard,))],
-        ),
-        compiler_params=params,
-        cost_estimate=pl.CostEstimate(flops=1000000, bytes_accessed=4 * rows_all * depth, transcendentals=0),
-        name="order_tokens",
-    )
-    tok = call(order, their_tokens, tokens)
 
     half = HEAD_DIM // 2
     frequency = ROPE_THETA ** (-2.0 * jnp.arange(half, dtype=jnp.float32) / HEAD_DIM)
@@ -444,79 +503,99 @@
     cos, sin = jnp.cos(angles), jnp.sin(angles)
     cos, sin = jnp.concatenate([cos, cos], axis=1), jnp.concatenate([-sin, sin], axis=1)
 
-    def attend(c, fresh):
+    def attend(c, fresh, group=None):
         n = head_chunks[c]
         width = n * HEAD_DIM
         with_kv = c == 0
-        block = KEY_BLOCK if n > 1 else 2 * KEY_BLOCK
+        base = seqs * (group or 0)
+        count = seqs if group is not None else 2 * seqs
+        n_out = count // seqs
+        block = KEY_BLOCK
         slots = max_len // block + 1
-        specs, arrays, places = [], [], []
+        m = max(n, 1) * new
+        arrays, places = [], []
         for s, first, parts in ((0, own_firsts[c], own_all), (1, 0, rest_all[c])):
             for d, o, a in parts:
-                specs.append(
-                    pl.BlockSpec((a.shape[0], widths[c]), functools.partial(lambda k, *_: (0, k), first // widths[c]))
-                )
                 arrays.append(a)
-                places.append(place[d, s] + o)
-        row = lambda i, *_: (i, 0)
-        out_shape = [jax.ShapeDtypeStruct((tok_rows, width), BF)] * 2
-        out_specs = [
-            pl.BlockSpec((new, width), lambda i, *_: (jnp.minimum(i, seqs - 1), 0)),
-            pl.BlockSpec((new, width), lambda i, *_: (jnp.maximum(i - seqs, 0), 0)),
-        ]
-        fresh_spec = pl.BlockSpec((2, new, HEAD_DIM), lambda i, *_: (0, i, 0))
+                places.append((place[d, s] + o // shard, first))
+        row = lambda i, *_: (i + base, 0)
+        out_width = width + 2 * HEAD_DIM * with_kv
+        out_shape = [jax.ShapeDtypeStruct((tok_rows, out_width), BF)] * n_out
+        if n_out == 1:
+            out_specs = [pl.BlockSpec((new, out_width), lambda i, *_: (i, 0))]
+        else:
+            out_specs = [
+                pl.BlockSpec((new, out_width), lambda i, *_: (jnp.minimum(i, seqs - 1), 0)),
+                pl.BlockSpec((new, out_width), lambda i, *_: (jnp.maximum(i - seqs, 0), 0)),
+            ]
+        fresh_spec = pl.BlockSpec((2, new, HEAD_DIM), lambda i, *_: (0, i + base, 0))
         if with_kv:
             out_shape.append(jax.ShapeDtypeStruct((2, rows_all, HEAD_DIM), BF))
             out_specs.append(fresh_spec)
+        anywhere = pl.BlockSpec(memory_space=pl.ANY)
         call = pl.pallas_call(
-            functools.partial(chunk_kernel, places, n, with_kv, block),
+            functools.partial(chunk_kernel, shard, places, n, with_kv, block, base, n_out),
             out_shape=out_shape,
             grid_spec=pltpu.PrefetchScalarGridSpec(
-                num_scalar_prefetch=1,
-                grid=(2 * seqs,),
+                num_scalar_prefetch=2,
+                grid=(count,),
                 in_specs=[
-                    pl.BlockSpec((new, depth), row),
                     pl.BlockSpec((new, HEAD_DIM), row),
                     pl.BlockSpec((new, HEAD_DIM), row),
-                    pl.BlockSpec((1, max_len, HEAD_DIM), lambda i, *_: (i, 0, 0)),
-                    pl.BlockSpec((1, max_len, HEAD_DIM), lambda i, *_: (i, 0, 0)),
+                    *[anywhere] * 4,
                     *([] if with_kv else [fresh_spec]),
-                    *specs,
+                    *[anywhere] * len(arrays),
                 ],
                 out_specs=out_specs,
                 scratch_shapes=[
-                    pltpu.VMEM((n * new, HEAD_DIM), BF),
-                    pltpu.VMEM((slots, n * new, block), jnp.float32),
-                    pltpu.VMEM((slots, n * new, 128), jnp.float32),
-                    pltpu.VMEM((n * new, 128), jnp.float32),
-                    pltpu.VMEM((n * new, 128), jnp.float32),
-                    pltpu.VMEM((n * new, 128), jnp.float32),
+                    pltpu.VMEM((2, new, depth), BF),
+                    pltpu.VMEM((depth, widths[c]), BF),
+                    pltpu.VMEM((2, 2, max_len, HEAD_DIM), BF),
+                    pltpu.VMEM((m, HEAD_DIM), BF),
+                    pltpu.VMEM((slots, m, block), jnp.float32),
+                    pltpu.VMEM((slots, m, 128), jnp.float32),
+                    pltpu.VMEM((m, 128), jnp.float32),
+                    pltpu.VMEM((m, 128), jnp.float32),
+                    pltpu.VMEM((m, 128), jnp.float32),
+                    pltpu.SemaphoreType.DMA((2, 3)),
+                    pltpu.SemaphoreType.DMA((depth // shard,)),
                 ],
             ),
             compiler_params=params,
             cost_estimate=pl.CostEstimate(
-                flops=2 * rows_all * width * (depth + 2 * (max_len + new)),
-                bytes_accessed=(rows_all + width) * depth * 2,
-                transcendentals=rows_all * n * (max_len + new),
+                flops=count * new * width * 2 * (depth + 2 * (max_len + new)),
+                bytes_accessed=(count * new + width) * depth * 2,
+                transcendentals=count * new * n * (max_len + new),
             ),
         )
         extra = () if with_kv else (fresh,)
-        return call(seq_lengths, tok, cos, sin, old_keys, old_values, *extra, *arrays)
+        return call(
+            seq_lengths, order, cos, sin, their_tokens, tokens, their_old, my_old, *extra, *arrays
+        )
 
     out, at, fresh = jnp.zeros((tok_rows, q_local), BF), 0, None
     for c in range(n_chunks):
-        theirs, mine, *rest = attend(c, fresh)
-        if rest:
+        if c in SPLIT:
+            (theirs,), (mine,) = attend(c, fresh, 0), attend(c, fresh, 1)
+        else:
+            theirs, mine, *rest = attend(c, fresh)
+        theirs = xor(theirs, 1)
+        width = head_chunks[c] * HEAD_DIM
+        if c == 0:
             fresh = rest[0]
-            back = xor(fresh[:, :tok_rows], 1)
-            kept = fresh[:, tok_rows:]
-            new_cache = jnp.concatenate(
-                [jnp.where(core == 0, kept, back), jnp.where(core == 0, back, kept)], axis=2
-            )
-        theirs = xor(theirs, 1)
-        out = lax.dynamic_update_slice(out, mine, (0, core * q_core + at))
-        out = lax.dynamic_update_slice(out, theirs, (0, (1 - core) * q_core + at))
-        at += head_chunks[c] * HEAD_DIM
+            parts = []
+            for k in range(2):
+                cols = slice(width + k * HEAD_DIM, width + (k + 1) * HEAD_DIM)
+                pair = (mine[:, cols], theirs[:, cols])
+                parts.append(
+                    jnp.concatenate([jnp.where(core == 0, *pair), jnp.where(core == 0, *pair[::-1])], axis=1)
+                )
+            new_cache = jnp.stack(parts)
+        if not width:
+            continue
+        out = lax.dynamic_update_slice(out, mine[:, :width], (0, core * q_core + at))
+        out = lax.dynamic_update_slice(out, theirs[:, :width], (0, (1 - core) * q_core + at))
+        at += width
     return out, new_cache
 
 

time: 416 us -> 385 us (0.925)
  the two profiles are of different devices: /device:TPU:25 before, /device:TPU:0 now
where the time goes in v2:
time: 385 us; the launch traced here: 383 us
  waiting for transfers between devices  168 us (44%)
  Pallas kernels  134 us (35%)
  starting transfers between devices  64 us (17%)
  local copies, waits for them, and re-layouts  10.8 us (3%)
  other arithmetic  4.33 us (1%)
    ppermute x32, waiting for transfers between devices, xor(): return lax.ppermute(a, 'rep', [(i, i ^ bit) for i in range(R)])  119 us
    pallas_call x4, Pallas kernels, attend(): call(seq_lengths, order, cos, sin, their_tokens, tokens, their_old, my_ol...  101 us
    ppermute x12, waiting for transfers between devices, over_tp(): lax.ppermute(ready[s, c], 'tp', [(t, (t + s) % T) for t in range(T)])  48.9 us
    ppermute x12, starting transfers between devices, over_tp(): lax.ppermute(ready[s, c], 'tp', [(t, (t + s) % T) for t in range(T)])  39.8 us
    ppermute x32, starting transfers between devices, xor(): return lax.ppermute(a, 'rep', [(i, i ^ bit) for i in range(R)])  24.2 us
    pallas_call x6, Pallas kernels, pack(): pl.pallas_call(functools.partial(pack_kernel, jobs, len(received)), out_s...  21.7 us
    unnamed x71, local copies, waits for them, and re-layouts  8.8 us
  transfers between devices with their start and end apart: 44, of which 17 were waited for; matrix products, arithmetic and copies ran while one was open for 2% of the time, Pallas kernels for 35%

profile of v2, /device:TPU:0, one launch (start us, length us, event | category | flops | bytes accessed | tf_op | source)
XLA Modules:
  0.0 382.9 jit_solution(1243163828223297493)
XLA Ops:
  1.2 0.7 stack.296.starts_ref
  1.9 2.7 shard_map.97
  4.8 10.0 %collective-permute-done.10.refs_3_ = bf16[256,768]{1,0:T(8,128)(2,1)S(1)} collective-permute-done((bf16[256,768]{1,0:T(8,128)(2,1)}, bf16[256,768]{1,0:T(8,128)(2,1)S(1)}, u32[]{:S(2)}, u32[]{:S(2)}) %collective-permute-start.10) | collective-permute-done | bytes 393248 | tf_op jit(solution)/shard_map/ppermute | solution.py:383
  14.7 0.7 copy-done.23
  15.5 3.8 shard_map.98
  19.3 3.0 collective-permute-start.11
  22.3 2.9 shard_map.96
  25.3 2.9 shard_map.95.refs_0_.refs_1_
  28.2 1.6 collective-permute-start.6
  29.8 2.7 collective-permute-start.12
  32.5 3.7 shard_map.102
  36.3 8.5 %collective-permute-done.12.refs_1_ = bf16[512,256]{1,0:T(8,128)(2,1)S(1)} collective-permute-done((bf16[512,256]{1,0:T(8,128)(2,1)S(1)}, bf16[512,256]{1,0:T(8,128)(2,1)S(1)}, u32[]{:S(2)}, u32[]{:S(2)}) %collective-permute-start.12) | collective-permute-done | bytes 262176 | tf_op jit(solution)/shard_map/ppermute | solution.py:449
  44.8 2.2 collective-permute-start.13
  47.1 5.3 %collective-permute-done.13.refs_2_ = bf16[512,256]{1,0:T(8,128)(2,1)S(1)} collective-permute-done((bf16[512,256]{1,0:T(8,128)(2,1)S(1)}, bf16[512,256]{1,0:T(8,128)(2,1)S(1)}, u32[]{:S(2)}, u32[]{:S(2)}) %collective-permute-start.13) | collective-permute-done | bytes 262176 | tf_op jit(solution)/shard_map/ppermute | solution.py:449
  52.5 1.1 collective-permute-done
  53.6 1.5 collective-permute-start.14
  56.2 31.1 %collective-permute-done.4.refs_2_.refs_3_ = bf16[256,1280]{1,0:T(8,128)(2,1)S(1)} collective-permute-done((bf16[256,1280]{1,0:T(8,128)(2,1)S(1)}, bf16[256,1280]{1,0:T(8,128)(2,1)S(1)}, u32[]{:S(2)}, u32[]{:S(2)}) %collective-permute-start.4) | collective-permute-done | bytes 655392 | tf_op jit(solution)/shard_map/ppermute | solution.py:383
  87.2 1.5 collective-permute-start.5
  90.2 1.1 copy-done.18
  91.3 1.5 collective-permute-start.16
  92.8 5.7 %shard_map.103 = (bf16[512,384]{1,0:T(8,128)(2,1)}, bf16[512,384]{1,0:T(8,128)(2,1)}, bf16[512,384]{1,0:T(8,128)(2,1)}, bf16[512,384]{1,0:T(8,128)(2,1)}, bf16[5...) custom-call(s32[56]{0:T(128)} %stack.296.starts_ref, ...), custom_call_target="tpu_custom_call" | custom-call | flops 1000000 | bytes 4718592 | tf_op jit(solution)/shard_map/pallas_call | solution.py:149
  98.5 6.3 %collective-permute-done.5.refs_3_.refs_4_ = bf16[256,1280]{1,0:T(8,128)(2,1)S(1)} collective-permute-done((bf16[256,1280]{1,0:T(8,128)(2,1)S(1)}, bf16[256,1280]{1,0:T(8,128)(2,1)S(1)}, u32[]{:S(2)}, u32[]{:S(2)}) %collective-permute-start.5) | collective-permute-done | bytes 655392 | tf_op jit(solution)/shard_map/ppermute | solution.py:383
  104.8 1.6 collective-permute-start.35
  106.5 12.4 %collective-permute-done.8.refs_6_.refs_7_ = bf16[256,1280]{1,0:T(8,128)(2,1)S(1)} collective-permute-done((bf16[256,1280]{1,0:T(8,128)(2,1)S(1)}, bf16[256,1280]{1,0:T(8,128)(2,1)S(1)}, u32[]{:S(2)}, u32[]{:S(2)}) %collective-permute-start.8) | collective-permute-done | bytes 655392 | tf_op jit(solution)/shard_map/ppermute | solution.py:383
  118.9 1.1 collective-permute-start.20
  119.9 5.7 %collective-permute-done.16.refs_11_ = bf16[768,256]{1,0:T(8,128)(2,1)S(1)} collective-permute-done((bf16[768,256]{1,0:T(8,128)(2,1)S(1)}, bf16[768,256]{1,0:T(8,128)(2,1)S(1)}, u32[]{:S(2)}, u32[]{:S(2)}) %collective-permute-start.16) | collective-permute-done | bytes 393248 | tf_op jit(solution)/shard_map/ppermute | solution.py:383
  125.6 4.0 %collective-permute-start.21 = (bf16[512,384]{1,0:T(8,128)(2,1)}, bf16[512,384]{1,0:T(8,128)(2,1)S(1)}, u32[]{:S(2)}, u32[]{:S(2)}) collective-permute-start(bf16[512,384]{1,0:T(8,128)(2,1)} %get-tuple-element.43), channel_id=1, source_target_pairs={{0,3},{1,0},{2,1},{3,2},{4,7},{5,4},{6,5},{7,6},{8,11},{9,8},{10,9... | collective-permute-start | bytes 1179656 | tf_op jit(solution)/shard_map/ppermute | solution.py:449
  130.0 9.9 %collective-permute-done.20.refs_1_ = bf16[512,384]{1,0:T(8,128)(2,1)S(1)} collective-permute-done((bf16[512,384]{1,0:T(8,128)(2,1)}, bf16[512,384]{1,0:T(8,128)(2,1)S(1)}, u32[]{:S(2)}, u32[]{:S(2)}) %collective-permute-start.20) | collective-permute-done | bytes 393248 | tf_op jit(solution)/shard_map/ppermute | solution.py:449
  140.2 5.9 %collective-permute-done.21.refs_2_ = bf16[512,384]{1,0:T(8,128)(2,1)S(1)} collective-permute-done((bf16[512,384]{1,0:T(8,128)(2,1)}, bf16[512,384]{1,0:T(8,128)(2,1)S(1)}, u32[]{:S(2)}, u32[]{:S(2)}) %collective-permute-start.21) | collective-permute-done | bytes 393248 | tf_op jit(solution)/shard_map/ppermute | solution.py:449
  146.1 9.5 %collective-permute-start.27 = (bf16[512,384]{1,0:T(8,128)(2,1)}, bf16[512,384]{1,0:T(8,128)(2,1)S(1)}, u32[]{:S(2)}, u32[]{:S(2)}) collective-permute-start(bf16[512,384]{1,0:T(8,128)(2,1)} %get-tuple-element.48), channel_id=1, source_target_pairs={{0,1},{1,2},{2,3},{3,0},{4,5},{5,6},{6,7},{7,4},{8,9},{9,10},{10,1... | collective-permute-start | bytes 1179656 | tf_op jit(solution)/shard_map/ppermute | solution.py:449
  156.2 1.2 collective-permute-done.36.refs_1_
  157.4 1.5 collective-permute-start.22
  158.9 12.1 %collective-permute-start.28 = (bf16[512,384]{1,0:T(8,128)(2,1)S(1)}, bf16[512,384]{1,0:T(8,128)(2,1)S(1)}, u32[]{:S(2)}, u32[]{:S(2)}) collective-permute-start(bf16[512,384]{1,0:T(8,128)(2,1)S(1)} %copy-done.31), channel_id=1, source_target_pairs={{0,2},{1,3},{2,0},{3,1},{4,6},{5,7},{6,4},{7,5},{8,10},{9,11},{10,... | collective-permute-start | bytes 1179656 | tf_op jit(solution)/shard_map/ppermute | solution.py:449
  171.2 1.6 collective-permute-start.38
  173.2 15.5 %collective-permute-done.28.refs_1_ = bf16[512,384]{1,0:T(8,128)(2,1)S(1)} collective-permute-done((bf16[512,384]{1,0:T(8,128)(2,1)S(1)}, bf16[512,384]{1,0:T(8,128)(2,1)S(1)}, u32[]{:S(2)}, u32[]{:S(2)}) %collective-permute-start.28) | collective-permute-done | bytes 393248 | tf_op jit(solution)/shard_map/ppermute | solution.py:449
  188.7 3.3 collective-permute-start.29
  192.0 6.1 %old.1 = (bf16[2,2,2048,128]{3,2,1,0:T(8,128)(2,1)}, bf16[2,2,2048,128]{3,2,1,0:T(8,128)(2,1)}) custom-call(s32[1]{0:T(128)} %bitcast.34.core_ref, s32[2,16]{1,0:T(2,128)} %bitcast.76, bf16[32,128,256]{2,1,0:T(8,128)(2,1)} %ck_ref.1, bf16[32,128,256]{2,1,0:T(8,128)(2,1)} %cv_ref.1), custom_call_target="tpu_custom_call" | custom-call | flops 1000000 | bytes 8000000 | tf_op jit(solution)/shard_map/old/pallas_call | solution.py:487
  198.1 2.5 collective-permute-done.29.refs_2_
  200.6 1.4 collective-permute-done.38.refs_1_.refs_10_
  202.4 1.6 shard_map.107.refs_9_
  204.1 1.7 collective-permute-start.30
  205.8 1.0 copy-done.7
  206.9 1.5 collective-permute-start.31
  208.4 0.7 stack.263.order_ref
  209.0 22.0 %collective-permute-done.23.refs_0_.refs_11_ = bf16[1536,384]{1,0:T(8,128)(2,1)} collective-permute-done((bf16[1536,384]{1,0:T(8,128)(2,1)S(1)}, bf16[1536,384]{1,0:T(8,128)(2,1)}, u32[]{:S(2)}, u32[]{:S(2)}) %collective-permute-start.23) | collective-permute-done | bytes 1179680 | tf_op jit(solution)/shard_map/ppermute | solution.py:383
  231.4 1.3 copy-done.8
  232.7 1.1 shard_map.105
  233.8 1.7 collective-permute-start.24
  235.5 20.8 %collective-permute-done.31.refs_0_.refs_11_ = bf16[1536,384]{1,0:T(8,128)(2,1)} collective-permute-done((bf16[1536,384]{1,0:T(8,128)(2,1)}, bf16[1536,384]{1,0:T(8,128)(2,1)}, u32[]{:S(2)}, u32[]{:S(2)}) %collective-permute-start.31) | collective-permute-done | bytes 1179680 | tf_op jit(solution)/shard_map/ppermute | solution.py:383
  256.7 1.9 fusion
  258.6 1.3 pad_maximum_fusion
  260.3 1.3 shard_map.108
  261.6 8.6 %collective-permute-done.9.refs_7_.refs_8_ = bf16[256,1280]{1,0:T(8,128)(2,1)S(1)} collective-permute-done((bf16[256,1280]{1,0:T(8,128)(2,1)S(1)}, bf16[256,1280]{1,0:T(8,128)(2,1)S(1)}, u32[]{:S(2)}, u32[]{:S(2)}) %collective-permute-start.9) | collective-permute-done | bytes 655392 | tf_op jit(solution)/shard_map/ppermute | solution.py:383
  270.2 1.5 collective-permute-start.40
  272.6 13.6 %shard_map.101 = (bf16[512,256]{1,0:T(8,128)(2,1)}, bf16[512,256]{1,0:T(8,128)(2,1)}, bf16[2,1024,128]{2,1,0:T(8,128)(2,1)}) custom-call(s32[4]{0:T(128)} %copy-done.28, s32[32]{0:T(128)} %stack.263.order_ref, f32[1024,128]{1,0:T(8,128)} %get-tuple-element.71.cos_ref, f32[1024,128]{1,0:T(8,128)} %get-tuple-element.72.sin_ref, ...), custom_call_target="tpu_custom_call" | custom-call | bytes 16777216 | tf_op jit(solution)/shard_map/pallas_call | solution.py:572
  286.2 1.8 collective-permute-start.33
  288.0 31.6 %shard_map.106 = (bf16[512,384]{1,0:T(8,128)(2,1)}, bf16[512,384]{1,0:T(8,128)(2,1)}) custom-call(s32[4]{0:T(128)} %copy-done.28, s32[32]{0:T(128)} %stack.263.order_ref, f32[1024,128]{1,0:T(8,128)} %get-tuple-element.71.cos_ref, f32[1024,128]{1,0:T(8,128)} %get-tuple-element.72.sin_ref, bf16[512,8192]{1,0:T(8,128)(2,1)} %collective-permute-done.1.their_tok, ...), custom_call_target="tpu_custom_call" | custom-call | flops 10066329600 | bytes 23068672 | tf_op jit(solution)/shard_map/pallas_call | solution.py:572
  320.4 0.8 copy-done.30
  321.3 31.8 %shard_map.109 = (bf16[512,384]{1,0:T(8,128)(2,1)}, bf16[512,384]{1,0:T(8,128)(2,1)}) custom-call(s32[4]{0:T(128)} %copy-done.28, s32[32]{0:T(128)} %stack.263.order_ref, f32[1024,128]{1,0:T(8,128)} %get-tuple-element.71.cos_ref, f32[1024,128]{1,0:T(8,128)} %get-tuple-element.72.sin_ref, bf16[512,8192]{1,0:T(8,128)(2,1)} %collective-permute-done.1.their_tok, ...), custom_call_target="tpu_custom_call" | custom-call | flops 10066329600 | bytes 23068672 | tf_op jit(solution)/shard_map/pallas_call | solution.py:572
  353.6 0.7 copy-done.21
  354.4 0.7 copy-done.22
  355.1 23.9 %shard_map.112 = (bf16[512,256]{1,0:T(8,128)(2,1)}, bf16[512,256]{1,0:T(8,128)(2,1)}) custom-call(s32[4]{0:T(128)} %copy-done.28, s32[32]{0:T(128)} %stack.263.order_ref, f32[1024,128]{1,0:T(8,128)} %get-tuple-element.71.cos_ref, f32[1024,128]{1,0:T(8,128)} %get-tuple-element.72.sin_ref, bf16[512,8192]{1,0:T(8,128)(2,1)} %collective-permute-done.1.their_tok, ...), custom_call_target="tpu_custom_call" | custom-call | flops 6710886400 | bytes 20971520 | tf_op jit(solution)/shard_map/pallas_call | solution.py:572
  380.3 0.8 pad_maximum_fusion.2
  381.5 1.3 copy-done.17
  (132 shorter events, 10.7 us)
Async XLA Ops:
  0.6 271.6 %collective-permute-start.1 = (bf16[512,8192]{1,0:T(8,128)(2,1)}, bf16[512,8192]{1,0:T(8,128)(2,1)}, u32[]{:S(2)}, u32[]{:S(2)}) collective-permute-start(bf16[512,8192]{1,0:T(8,128)(2,1)} %my_tok.7), channel_id=1, source_target_pairs={{0,4},{4,0},{8,12},{12,8},{16,20},{20,16},{24,28},{28,24},{1,5},{5... | collective-permute-start | bytes 25165832 | tf_op jit(solution)/shard_map/ppermute | solution.py:383
  4.6 10.1 %collective-permute-start.10 = (bf16[256,768]{1,0:T(8,128)(2,1)}, bf16[256,768]{1,0:T(8,128)(2,1)S(1)}, u32[]{:S(2)}, u32[]{:S(2)}) collective-permute-start(bf16[256,768]{1,0:T(8,128)(2,1)} %shard_map.97), channel_id=1, source_target_pairs={{0,4},{4,0},{8,12},{12,8},{16,20},{20,16},{24,28},{28,24},{1,5},{5... | collective-permute-start | bytes 1179656 | tf_op jit(solution)/shard_map/ppermute | solution.py:383
  19.3 16.9 %collective-permute-start.11 = (bf16[512,256]{1,0:T(8,128)(2,1)}, bf16[512,256]{1,0:T(8,128)(2,1)S(1)}, u32[]{:S(2)}, u32[]{:S(2)}) collective-permute-start(bf16[512,256]{1,0:T(8,128)(2,1)} %get-tuple-element.35), channel_id=1, source_target_pairs={{0,1},{1,2},{2,3},{3,0},{4,5},{5,6},{6,7},{7,4},{8,9},{9,10},{10,1... | collective-permute-start | bytes 786440 | tf_op jit(solution)/shard_map/ppermute | solution.py:449
  25.2 29.9 %collective-permute-start.3 = (bf16[256,1280]{1,0:T(8,128)(2,1)}, bf16[256,1280]{1,0:T(8,128)(2,1)S(1)}, u32[]{:S(2)}, u32[]{:S(2)}) collective-permute-start(bf16[256,1280]{1,0:T(8,128)(2,1)} %shard_map.96), channel_id=1, source_target_pairs={{0,4},{4,0},{8,12},{12,8},{16,20},{20,16},{24,28},{28,24},{1,5},{5... | collective-permute-start | bytes 1966088 | tf_op jit(solution)/shard_map/ppermute | solution.py:383
  28.2 27.3 %collective-permute-start.6 = (bf16[256,1280]{1,0:T(8,128)(2,1)}, bf16[256,1280]{1,0:T(8,128)(2,1)S(1)}, u32[]{:S(2)}, u32[]{:S(2)}) collective-permute-start(bf16[256,1280]{1,0:T(8,128)(2,1)} %shard_map.95.refs_0_.refs_1_), channel_id=1, source_target_pairs={{0,16},{4,20},{8,24},{12,28},{16,0},{20,4},{24,8},{28,12},{1,17},{... | collective-permute-start | bytes 1966088 | tf_op jit(solution)/shard_map/ppermute | solution.py:383
  29.8 15.0 %copy-start.32 = (bf16[512,256]{1,0:T(8,128)(2,1)S(1)}, bf16[512,256]{1,0:T(8,128)(2,1)}, u32[]{:S(2)}) copy-start(bf16[512,256]{1,0:T(8,128)(2,1)} %get-tuple-element.37) | copy-start | bytes 786436
  29.8 22.6 %copy-start.34 = (s32[1,2]{1,0:T(1,128)S(1)}, s32[1,2]{1,0:T(1,128)}, u32[]{:S(2)}) copy-start(s32[1,2]{1,0:T(1,128)} %param.14) | copy-start | bytes 28
  29.8 25.8 %copy-start.9 = (bf16[256,1280]{1,0:T(8,128)(2,1)S(1)}, bf16[256,1280]{1,0:T(8,128)(2,1)}, u32[]{:S(2)}) copy-start(bf16[256,1280]{1,0:T(8,128)(2,1)} %shard_map.95.refs_0_.refs_1_) | copy-start | bytes 1966084
  29.8 15.0 %collective-permute-start.12 = (bf16[512,256]{1,0:T(8,128)(2,1)S(1)}, bf16[512,256]{1,0:T(8,128)(2,1)S(1)}, u32[]{:S(2)}, u32[]{:S(2)}) collective-permute-start(bf16[512,256]{1,0:T(8,128)(2,1)S(1)} %copy-done.33), channel_id=1, source_target_pairs={{0,2},{1,3},{2,0},{3,1},{4,6},{5,7},{6,4},{7,5},{8,10},{9,11},{10,... | collective-permute-start | bytes 786440 | tf_op jit(solution)/shard_map/ppermute | solution.py:449
  36.2 53.9 %collective-permute-start.18 = (bf16[256,3072]{1,0:T(8,128)(2,1)}, bf16[256,3072]{1,0:T(8,128)(2,1)S(1)}, u32[]{:S(2)}, u32[]{:S(2)}) collective-permute-start(bf16[256,3072]{1,0:T(8,128)(2,1)} %shard_map.102), channel_id=1, source_target_pairs={{0,4},{4,0},{8,12},{12,8},{16,20},{20,16},{24,28},{28,24},{1,5},{5... | collective-permute-start | bytes 4718600 | tf_op jit(solution)/shard_map/ppermute | solution.py:383
  44.8 7.6 %collective-permute-start.13 = (bf16[512,256]{1,0:T(8,128)(2,1)S(1)}, bf16[512,256]{1,0:T(8,128)(2,1)S(1)}, u32[]{:S(2)}, u32[]{:S(2)}) collective-permute-start(bf16[512,256]{1,0:T(8,128)(2,1)S(1)} %copy-done.32), channel_id=1, source_target_pairs={{0,3},{1,0},{2,1},{3,2},{4,7},{5,4},{6,5},{7,6},{8,11},{9,8},{10,9... | collective-permute-start | bytes 786440 | tf_op jit(solution)/shard_map/ppermute | solution.py:449
  52.4 1.2 collective-permute-start
  52.5 46.0 %copy-start = (bf16[1536,256]{1,0:T(8,128)(2,1)}, bf16[1536,256]{1,0:T(8,128)(2,1)S(1)}, u32[]{:S(2)}) copy-start(bf16[1536,256]{1,0:T(8,128)(2,1)S(1)} %shard_map.99.refs_8_) | copy-start | bytes 2359300
  53.6 35.2 %collective-permute-start.14 = (bf16[1536,256]{1,0:T(8,128)(2,1)S(1)}, bf16[1536,256]{1,0:T(8,128)(2,1)S(1)}, u32[]{:S(2)}, u32[]{:S(2)}) collective-permute-start(bf16[1536,256]{1,0:T(8,128)(2,1)S(1)} %shard_map.99.refs_8_), channel_id=1, source_target_pairs={{0,8},{4,12},{8,0},{12,4},{16,24},{20,28},{24,16},{28,20},{1,9},{5... | collective-permute-start | bytes 2359304 | tf_op jit(solution)/shard_map/ppermute | solution.py:383
  55.0 43.4 %copy-start.10 = (bf16[256,1280]{1,0:T(8,128)(2,1)}, bf16[256,1280]{1,0:T(8,128)(2,1)S(1)}, u32[]{:S(2)}) copy-start(bf16[256,1280]{1,0:T(8,128)(2,1)S(1)} %collective-permute-done.3.refs_1_.refs_2_) | copy-start | bytes 1966084
  55.1 34.2 %collective-permute-start.15 = (bf16[1536,256]{1,0:T(8,128)(2,1)S(1)}, bf16[1536,256]{1,0:T(8,128)(2,1)S(1)}, u32[]{:S(2)}, u32[]{:S(2)}) collective-permute-start(bf16[1536,256]{1,0:T(8,128)(2,1)S(1)} %shard_map.99.refs_8_), channel_id=1, source_target_pairs={{0,16},{4,20},{8,24},{12,28},{16,0},{20,4},{24,8},{28,12},{1,17},{... | collective-permute-start | bytes 2359304 | tf_op jit(solution)/shard_map/ppermute | solution.py:383
  55.6 42.9 %copy-start.11 = (bf16[256,1280]{1,0:T(8,128)(2,1)}, bf16[256,1280]{1,0:T(8,128)(2,1)S(1)}, u32[]{:S(2)}) copy-start(bf16[256,1280]{1,0:T(8,128)(2,1)S(1)} %collective-permute-done.6.refs_4_.refs_5_) | copy-start | bytes 1966084
  55.6 31.6 %collective-permute-start.4 = (bf16[256,1280]{1,0:T(8,128)(2,1)S(1)}, bf16[256,1280]{1,0:T(8,128)(2,1)S(1)}, u32[]{:S(2)}, u32[]{:S(2)}) collective-permute-start(bf16[256,1280]{1,0:T(8,128)(2,1)S(1)} %copy-done.9), channel_id=1, source_target_pairs={{0,8},{4,12},{8,0},{12,4},{16,24},{20,28},{24,16},{28,20},{1,9},{5... | collective-permute-start | bytes 1966088 | tf_op jit(solution)/shard_map/ppermute | solution.py:383
  87.2 11.3 %copy-start.12 = (bf16[256,1280]{1,0:T(8,128)(2,1)}, bf16[256,1280]{1,0:T(8,128)(2,1)S(1)}, u32[]{:S(2)}) copy-start(bf16[256,1280]{1,0:T(8,128)(2,1)S(1)} %collective-permute-done.4.refs_2_.refs_3_) | copy-start | bytes 1966084
  87.2 17.6 %collective-permute-start.5 = (bf16[256,1280]{1,0:T(8,128)(2,1)S(1)}, bf16[256,1280]{1,0:T(8,128)(2,1)S(1)}, u32[]{:S(2)}, u32[]{:S(2)}) collective-permute-start(bf16[256,1280]{1,0:T(8,128)(2,1)S(1)} %collective-permute-done.3.refs_1_.refs_2_), channel_id=1, source_target_pairs={{0,8},{4,12},{8,0},{12,4},{16,24},{20,28},{24,16},{28,20},{1,9},{5... | collective-permute-start | bytes 1966088 | tf_op jit(solution)/shard_map/ppermute | solution.py:383
  88.7 9.8 %copy-start.1 = (bf16[1536,256]{1,0:T(8,128)(2,1)}, bf16[1536,256]{1,0:T(8,128)(2,1)S(1)}, u32[]{:S(2)}) copy-start(bf16[1536,256]{1,0:T(8,128)(2,1)S(1)} %collective-permute-done.14.refs_1_.refs_9_) | copy-start | bytes 2359300
  88.7 16.1 %collective-permute-start.7 = (bf16[256,1280]{1,0:T(8,128)(2,1)S(1)}, bf16[256,1280]{1,0:T(8,128)(2,1)S(1)}, u32[]{:S(2)}, u32[]{:S(2)}) collective-permute-start(bf16[256,1280]{1,0:T(8,128)(2,1)S(1)} %collective-permute-done.3.refs_1_.refs_2_), channel_id=1, source_target_pairs={{0,16},{4,20},{8,24},{12,28},{16,0},{20,4},{24,8},{28,12},{1,17},{... | collective-permute-start | bytes 1966088 | tf_op jit(solution)/shard_map/ppermute | solution.py:383
  89.2 9.3 %copy-start.2 = (bf16[1536,256]{1,0:T(8,128)(2,1)}, bf16[1536,256]{1,0:T(8,128)(2,1)S(1)}, u32[]{:S(2)}) copy-start(bf16[1536,256]{1,0:T(8,128)(2,1)S(1)} %collective-permute-done.15.refs_0_.refs_10_) | copy-start | bytes 2359300
  89.2 29.6 %collective-permute-start.8 = (bf16[256,1280]{1,0:T(8,128)(2,1)S(1)}, bf16[256,1280]{1,0:T(8,128)(2,1)S(1)}, u32[]{:S(2)}, u32[]{:S(2)}) collective-permute-start(bf16[256,1280]{1,0:T(8,128)(2,1)S(1)} %collective-permute-done.6.refs_4_.refs_5_), channel_id=1, source_target_pairs={{0,8},{4,12},{8,0},{12,4},{16,24},{20,28},{24,16},{28,20},{1,9},{5... | collective-permute-start | bytes 1966088 | tf_op jit(solution)/shard_map/ppermute | solution.py:383
  91.3 34.3 %collective-permute-start.16 = (bf16[768,256]{1,0:T(8,128)(2,1)S(1)}, bf16[768,256]{1,0:T(8,128)(2,1)S(1)}, u32[]{:S(2)}, u32[]{:S(2)}) collective-permute-start(bf16[768,256]{1,0:T(8,128)(2,1)S(1)} %get-tuple-element.38), channel_id=1, source_target_pairs={{0,8},{4,12},{8,0},{12,4},{16,24},{20,28},{24,16},{28,20},{1,9},{5... | collective-permute-start | bytes 1179656 | tf_op jit(solution)/shard_map/ppermute | solution.py:383
  98.5 60.4 %copy-start.31 = (bf16[512,384]{1,0:T(8,128)(2,1)S(1)}, bf16[512,384]{1,0:T(8,128)(2,1)}, u32[]{:S(2)}) copy-start(bf16[512,384]{1,0:T(8,128)(2,1)} %get-tuple-element.49) | copy-start | bytes 1179652
  104.8 126.2 %copy-start.13 = (bf16[256,1280]{1,0:T(8,128)(2,1)}, bf16[256,1280]{1,0:T(8,128)(2,1)S(1)}, u32[]{:S(2)}) copy-start(bf16[256,1280]{1,0:T(8,128)(2,1)S(1)} %collective-permute-done.5.refs_3_.refs_4_) | copy-start | bytes 1966084
  104.8 24.9 %collective-permute-start.19 = (bf16[512,384]{1,0:T(8,128)(2,1)}, bf16[512,384]{1,0:T(8,128)(2,1)S(1)}, u32[]{:S(2)}, u32[]{:S(2)}) collective-permute-start(bf16[512,384]{1,0:T(8,128)(2,1)} %get-tuple-element.41), channel_id=1, source_target_pairs={{0,1},{1,2},{2,3},{3,0},{4,5},{5,6},{6,7},{7,4},{8,9},{9,10},{10,1... | collective-permute-start | bytes 1179656 | tf_op jit(solution)/shard_map/ppermute | solution.py:449
  104.8 66.3 %copy-start.14 = (bf16[256,1280]{1,0:T(8,128)(2,1)}, bf16[256,1280]{1,0:T(8,128)(2,1)S(1)}, u32[]{:S(2)}) copy-start(bf16[256,1280]{1,0:T(8,128)(2,1)S(1)} %collective-permute-done.7.refs_5_.refs_6_) | copy-start | bytes 1966084
  104.8 24.8 %collective-permute-start.35 = (bf16[512,256]{1,0:T(8,128)(2,1)}, bf16[512,256]{1,0:T(8,128)(2,1)S(1)}, u32[]{:S(2)}, u32[]{:S(2)}) collective-permute-start(bf16[512,256]{1,0:T(8,128)(2,1)} %get-tuple-element.55), channel_id=1, source_target_pairs={{0,1},{1,2},{2,3},{3,0},{4,5},{5,6},{6,7},{7,4},{8,9},{9,10},{10,1... | collective-permute-start | bytes 786440 | tf_op jit(solution)/shard_map/ppermute | solution.py:449
  118.9 27.3 %copy-start.15 = (bf16[256,1280]{1,0:T(8,128)(2,1)}, bf16[256,1280]{1,0:T(8,128)(2,1)S(1)}, u32[]{:S(2)}) copy-start(bf16[256,1280]{1,0:T(8,128)(2,1)S(1)} %collective-permute-done.8.refs_6_.refs_7_) | copy-start | bytes 1966084
  118.9 21.1 %collective-permute-start.20 = (bf16[512,384]{1,0:T(8,128)(2,1)}, bf16[512,384]{1,0:T(8,128)(2,1)S(1)}, u32[]{:S(2)}, u32[]{:S(2)}) collective-permute-start(bf16[512,384]{1,0:T(8,128)(2,1)} %get-tuple-element.42), channel_id=1, source_target_pairs={{0,2},{1,3},{2,0},{3,1},{4,6},{5,7},{6,4},{7,5},{8,10},{9,11},{10,... | collective-permute-start | bytes 1179656 | tf_op jit(solution)/shard_map/ppermute | solution.py:449
  125.6 20.5 %copy-start.19 = (bf16[768,256]{1,0:T(8,128)(2,1)}, bf16[768,256]{1,0:T(8,128)(2,1)S(1)}, u32[]{:S(2)}) copy-start(bf16[768,256]{1,0:T(8,128)(2,1)S(1)} %collective-permute-done.16.refs_11_) | copy-start | bytes 1179652
  125.6 20.5 %collective-permute-start.21 = (bf16[512,384]{1,0:T(8,128)(2,1)}, bf16[512,384]{1,0:T(8,128)(2,1)S(1)}, u32[]{:S(2)}, u32[]{:S(2)}) collective-permute-start(bf16[512,384]{1,0:T(8,128)(2,1)} %get-tuple-element.43), channel_id=1, source_target_pairs={{0,3},{1,0},{2,1},{3,2},{4,7},{5,4},{6,5},{7,6},{8,11},{9,8},{10,9... | collective-permute-start | bytes 1179656 | tf_op jit(solution)/shard_map/ppermute | solution.py:449
  129.7 27.7 %collective-permute-start.36 = (bf16[512,256]{1,0:T(8,128)(2,1)}, bf16[512,256]{1,0:T(8,128)(2,1)S(1)}, u32[]{:S(2)}, u32[]{:S(2)}) collective-permute-start(bf16[512,256]{1,0:T(8,128)(2,1)} %get-tuple-element.56), channel_id=1, source_target_pairs={{0,2},{1,3},{2,0},{3,1},{4,6},{5,7},{6,4},{7,5},{8,10},{9,11},{10,... | collective-permute-start | bytes 786440 | tf_op jit(solution)/shard_map/ppermute | solution.py:449
  129.7 29.2 %collective-permute-start.37 = (bf16[512,256]{1,0:T(8,128)(2,1)}, bf16[512,256]{1,0:T(8,128)(2,1)S(1)}, u32[]{:S(2)}, u32[]{:S(2)}) collective-permute-start(bf16[512,256]{1,0:T(8,128)(2,1)} %get-tuple-element.57), channel_id=1, source_target_pairs={{0,3},{1,0},{2,1},{3,2},{4,7},{5,4},{6,5},{7,6},{8,11},{9,8},{10,9... | collective-permute-start | bytes 786440 | tf_op jit(solution)/shard_map/ppermute | solution.py:449
  140.0 31.2 %collective-permute-start.17 = (bf16[768,256]{1,0:T(8,128)(2,1)S(1)}, bf16[768,256]{1,0:T(8,128)(2,1)S(1)}, u32[]{:S(2)}, u32[]{:S(2)}) collective-permute-start(bf16[768,256]{1,0:T(8,128)(2,1)S(1)} %get-tuple-element.39), channel_id=1, source_target_pairs={{0,16},{4,20},{8,24},{12,28},{16,0},{20,4},{24,8},{28,12},{1,17},{... | collective-permute-start | bytes 1179656 | tf_op jit(solution)/shard_map/ppermute | solution.py:383
  146.1 26.6 %collective-permute-start.27 = (bf16[512,384]{1,0:T(8,128)(2,1)}, bf16[512,384]{1,0:T(8,128)(2,1)S(1)}, u32[]{:S(2)}, u32[]{:S(2)}) collective-permute-start(bf16[512,384]{1,0:T(8,128)(2,1)} %get-tuple-element.48), channel_id=1, source_target_pairs={{0,1},{1,2},{2,3},{3,0},{4,5},{5,6},{6,7},{7,4},{8,9},{9,10},{10,1... | collective-permute-start | bytes 1179656 | tf_op jit(solution)/shard_map/ppermute | solution.py:449
  156.2 45.9 %copy-start.6 = (bf16[1536,384]{1,0:T(8,128)(2,1)}, bf16[1536,384]{1,0:T(8,128)(2,1)S(1)}, u32[]{:S(2)}) copy-start(bf16[1536,384]{1,0:T(8,128)(2,1)S(1)} %shard_map.104.refs_9_) | copy-start | bytes 3538948
  157.4 48.4 %collective-permute-start.22 = (bf16[1536,384]{1,0:T(8,128)(2,1)S(1)}, bf16[1536,384]{1,0:T(8,128)(2,1)S(1)}, u32[]{:S(2)}, u32[]{:S(2)}) collective-permute-start(bf16[1536,384]{1,0:T(8,128)(2,1)S(1)} %shard_map.104.refs_9_), channel_id=1, source_target_pairs={{0,8},{4,12},{8,0},{12,4},{16,24},{20,28},{24,16},{28,20},{1,9},{5... | collective-permute-start | bytes 3538952 | tf_op jit(solution)/shard_map/ppermute | solution.py:383
  158.9 29.8 %collective-permute-start.28 = (bf16[512,384]{1,0:T(8,128)(2,1)S(1)}, bf16[512,384]{1,0:T(8,128)(2,1)S(1)}, u32[]{:S(2)}, u32[]{:S(2)}) collective-permute-start(bf16[512,384]{1,0:T(8,128)(2,1)S(1)} %copy-done.31), channel_id=1, source_target_pairs={{0,2},{1,3},{2,0},{3,1},{4,6},{5,7},{6,4},{7,5},{8,10},{9,11},{10,... | collective-permute-start | bytes 1179656 | tf_op jit(solution)/shard_map/ppermute | solution.py:449
  171.1 27.0 %copy-start.3 = (bf16[1536,256]{1,0:T(8,128)(2,1)}, bf16[1536,256]{1,0:T(8,128)(2,1)S(1)}, u32[]{:S(2)}) copy-start(bf16[1536,256]{1,0:T(8,128)(2,1)S(1)} %shard_map.110.refs_9_) | copy-start | bytes 2359300
  171.1 27.0 %copy-start.20 = (bf16[768,256]{1,0:T(8,128)(2,1)}, bf16[768,256]{1,0:T(8,128)(2,1)S(1)}, u32[]{:S(2)}) copy-start(bf16[768,256]{1,0:T(8,128)(2,1)S(1)} %collective-permute-done.17.refs_12_) | copy-start | bytes 1179652
  171.2 30.9 %collective-permute-start.38 = (bf16[1536,256]{1,0:T(8,128)(2,1)S(1)}, bf16[1536,256]{1,0:T(8,128)(2,1)S(1)}, u32[]{:S(2)}, u32[]{:S(2)}) collective-permute-start(bf16[1536,256]{1,0:T(8,128)(2,1)S(1)} %shard_map.110.refs_9_), channel_id=1, source_target_pairs={{0,8},{4,12},{8,0},{12,4},{16,24},{20,28},{24,16},{28,20},{1,9},{5... | collective-permute-start | bytes 2359304 | tf_op jit(solution)/shard_map/ppermute | solution.py:383
  172.7 31.3 %collective-permute-start.39 = (bf16[1536,256]{1,0:T(8,128)(2,1)S(1)}, bf16[1536,256]{1,0:T(8,128)(2,1)S(1)}, u32[]{:S(2)}, u32[]{:S(2)}) collective-permute-start(bf16[1536,256]{1,0:T(8,128)(2,1)S(1)} %shard_map.110.refs_9_), channel_id=1, source_target_pairs={{0,16},{4,20},{8,24},{12,28},{16,0},{20,4},{24,8},{28,12},{1,17},{... | collective-permute-start | bytes 2359304 | tf_op jit(solution)/shard_map/ppermute | solution.py:383
  188.7 11.9 %collective-permute-start.29 = (bf16[512,384]{1,0:T(8,128)(2,1)}, bf16[512,384]{1,0:T(8,128)(2,1)S(1)}, u32[]{:S(2)}, u32[]{:S(2)}) collective-permute-start(bf16[512,384]{1,0:T(8,128)(2,1)} %get-tuple-element.50), channel_id=1, source_target_pairs={{0,3},{1,0},{2,1},{3,2},{4,7},{5,4},{6,5},{7,6},{8,11},{9,8},{10,9... | collective-permute-start | bytes 1179656 | tf_op jit(solution)/shard_map/ppermute | solution.py:449
  200.6 71.1 %collective-permute-start.2 = (bf16[2,2,2048,128]{3,2,1,0:T(8,128)(2,1)}, bf16[2,2,2048,128]{3,2,1,0:T(8,128)(2,1)}, u32[]{:S(2)}, u32[]{:S(2)}) collective-permute-start(bf16[2,2,2048,128]{3,2,1,0:T(8,128)(2,1)} %get-tuple-element.33), channel_id=1, source_target_pairs={{0,4},{4,0},{8,12},{12,8},{16,20},{20,16},{24,28},{28,24},{1,5},{5... | collective-permute-start | bytes 6291464 | tf_op jit(solution)/shard_map/ppermute | solution.py:383
  202.1 57.9 %copy-start.4 = (bf16[1536,256]{1,0:T(8,128)(2,1)}, bf16[1536,256]{1,0:T(8,128)(2,1)S(1)}, u32[]{:S(2)}) copy-start(bf16[1536,256]{1,0:T(8,128)(2,1)S(1)} %collective-permute-done.38.refs_1_.refs_10_) | copy-start | bytes 2359300
  202.1 28.9 %collective-permute-start.23 = (bf16[1536,384]{1,0:T(8,128)(2,1)S(1)}, bf16[1536,384]{1,0:T(8,128)(2,1)}, u32[]{:S(2)}, u32[]{:S(2)}) collective-permute-start(bf16[1536,384]{1,0:T(8,128)(2,1)S(1)} %shard_map.104.refs_9_), channel_id=1, source_target_pairs={{0,16},{4,20},{8,24},{12,28},{16,0},{20,4},{24,8},{28,12},{1,17},{... | collective-permute-start | bytes 3538952 | tf_op jit(solution)/shard_map/ppermute | solution.py:383
  204.1 55.9 %copy-start.5 = (bf16[1536,256]{1,0:T(8,128)(2,1)}, bf16[1536,256]{1,0:T(8,128)(2,1)S(1)}, u32[]{:S(2)}) copy-start(bf16[1536,256]{1,0:T(8,128)(2,1)S(1)} %collective-permute-done.39.refs_0_.refs_11_) | copy-start | bytes 2359300
  204.1 29.7 %collective-permute-start.30 = (bf16[1536,384]{1,0:T(8,128)(2,1)}, bf16[1536,384]{1,0:T(8,128)(2,1)}, u32[]{:S(2)}, u32[]{:S(2)}) collective-permute-start(bf16[1536,384]{1,0:T(8,128)(2,1)} %shard_map.107.refs_9_), channel_id=1, source_target_pairs={{0,8},{4,12},{8,0},{12,4},{16,24},{20,28},{24,16},{28,20},{1,9},{5... | collective-permute-start | bytes 3538952 | tf_op jit(solution)/shard_map/ppermute | solution.py:383
  206.9 49.4 %collective-permute-start.31 = (bf16[1536,384]{1,0:T(8,128)(2,1)}, bf16[1536,384]{1,0:T(8,128)(2,1)}, u32[]{:S(2)}, u32[]{:S(2)}) collective-permute-start(bf16[1536,384]{1,0:T(8,128)(2,1)} %shard_map.107.refs_9_), channel_id=1, source_target_pairs={{0,16},{4,20},{8,24},{12,28},{16,0},{20,4},{24,8},{28,12},{1,17},{... | collective-permute-start | bytes 3538952 | tf_op jit(solution)/shard_map/ppermute | solution.py:383
  231.0 39.2 %collective-permute-start.9 = (bf16[256,1280]{1,0:T(8,128)(2,1)S(1)}, bf16[256,1280]{1,0:T(8,128)(2,1)S(1)}, u32[]{:S(2)}, u32[]{:S(2)}) collective-permute-start(bf16[256,1280]{1,0:T(8,128)(2,1)S(1)} %collective-permute-done.5.refs_3_.refs_4_), channel_id=1, source_target_pairs={{0,16},{4,20},{8,24},{12,28},{16,0},{20,4},{24,8},{28,12},{1,17},{... | collective-permute-start | bytes 1966088 | tf_op jit(solution)/shard_map/ppermute | solution.py:383
  232.7 27.2 %copy-start.28 = (s32[4]{0:T(128)}, s32[4]{0:T(128)S(1)}, u32[]{:S(2)}) copy-start(s32[4]{0:T(128)S(1)} %pad_add_fusion.len_ref) | copy-start | bytes 52
  233.8 52.4 %collective-permute-start.24 = (bf16[768,384]{1,0:T(8,128)(2,1)S(1)}, bf16[768,384]{1,0:T(8,128)(2,1)}, u32[]{:S(2)}, u32[]{:S(2)}) collective-permute-start(bf16[768,384]{1,0:T(8,128)(2,1)S(1)} %get-tuple-element.44), channel_id=1, source_target_pairs={{0,8},{4,12},{8,0},{12,4},{16,24},{20,28},{24,16},{28,20},{1,9},{5... | collective-permute-start | bytes 1769480 | tf_op jit(solution)/shard_map/ppermute | solution.py:383
  256.3 31.7 %collective-permute-start.25 = (bf16[768,384]{1,0:T(8,128)(2,1)S(1)}, bf16[768,384]{1,0:T(8,128)(2,1)}, u32[]{:S(2)}, u32[]{:S(2)}) collective-permute-start(bf16[768,384]{1,0:T(8,128)(2,1)S(1)} %get-tuple-element.45), channel_id=1, source_target_pairs={{0,16},{4,20},{8,24},{12,28},{16,0},{20,4},{24,8},{28,12},{1,17},{... | collective-permute-start | bytes 1769480 | tf_op jit(solution)/shard_map/ppermute | solution.py:383
  270.2 83.4 %collective-permute-start.40 = (bf16[768,256]{1,0:T(8,128)(2,1)S(1)}, bf16[768,256]{1,0:T(8,128)(2,1)S(1)}, u32[]{:S(2)}, u32[]{:S(2)}) collective-permute-start(bf16[768,256]{1,0:T(8,128)(2,1)S(1)} %get-tuple-element.58), channel_id=1, source_target_pairs={{0,8},{4,12},{8,0},{12,4},{16,24},{20,28},{24,16},{28,20},{1,9},{5... | collective-permute-start | bytes 1179656 | tf_op jit(solution)/shard_map/ppermute | solution.py:383
  271.7 81.9 %collective-permute-start.41 = (bf16[768,256]{1,0:T(8,128)(2,1)S(1)}, bf16[768,256]{1,0:T(8,128)(2,1)S(1)}, u32[]{:S(2)}, u32[]{:S(2)}) collective-permute-start(bf16[768,256]{1,0:T(8,128)(2,1)S(1)} %get-tuple-element.59), channel_id=1, source_target_pairs={{0,16},{4,20},{8,24},{12,28},{16,0},{20,4},{24,8},{28,12},{1,17},{... | collective-permute-start | bytes 1179656 | tf_op jit(solution)/shard_map/ppermute | solution.py:383
  272.2 47.4 %collective-permute-start.32 = (bf16[768,384]{1,0:T(8,128)(2,1)S(1)}, bf16[768,384]{1,0:T(8,128)(2,1)S(1)}, u32[]{:S(2)}, u32[]{:S(2)}) collective-permute-start(bf16[768,384]{1,0:T(8,128)(2,1)S(1)} %get-tuple-element.51), channel_id=1, source_target_pairs={{0,8},{4,12},{8,0},{12,4},{16,24},{20,28},{24,16},{28,20},{1,9},{5... | collective-permute-start | bytes 1769480 | tf_op jit(solution)/shard_map/ppermute | solution.py:383
  286.2 34.0 %collective-permute-start.33 = (bf16[768,384]{1,0:T(8,128)(2,1)S(1)}, bf16[768,384]{1,0:T(8,128)(2,1)S(1)}, u32[]{:S(2)}, u32[]{:S(2)}) collective-permute-start(bf16[768,384]{1,0:T(8,128)(2,1)S(1)} %get-tuple-element.52), channel_id=1, source_target_pairs={{0,16},{4,20},{8,24},{12,28},{16,0},{20,4},{24,8},{28,12},{1,17},{... | collective-permute-start | bytes 1769480 | tf_op jit(solution)/shard_map/ppermute | solution.py:383
  288.0 92.1 %collective-permute-start.43 = (bf16[512,256]{1,0:T(8,128)(2,1)}, bf16[512,256]{1,0:T(8,128)(2,1)S(1)}, u32[]{:S(2)}, u32[]{:S(2)}) collective-permute-start(bf16[512,256]{1,0:T(8,128)(2,1)} %get-tuple-element.63), channel_id=1, source_target_pairs={{0,4},{4,0},{8,12},{12,8},{16,20},{20,16},{24,28},{28,24},{1,5},{5... | collective-permute-start | bytes 786440 | tf_op jit(solution)/shard_map/ppermute | solution.py:383
  319.6 61.5 %collective-permute-start.26 = (bf16[512,384]{1,0:T(8,128)(2,1)}, bf16[512,384]{1,0:T(8,128)(2,1)S(1)}, u32[]{:S(2)}, u32[]{:S(2)}) collective-permute-start(bf16[512,384]{1,0:T(8,128)(2,1)} %get-tuple-element.47), channel_id=1, source_target_pairs={{0,4},{4,0},{8,12},{12,8},{16,20},{20,16},{24,28},{28,24},{1,5},{5... | collective-permute-start | bytes 1179656 | tf_op jit(solution)/shard_map/ppermute | solution.py:383
  353.0 28.3 %collective-permute-start.34 = (bf16[512,384]{1,0:T(8,128)(2,1)}, bf16[512,384]{1,0:T(8,128)(2,1)S(1)}, u32[]{:S(2)}, u32[]{:S(2)}) collective-permute-start(bf16[512,384]{1,0:T(8,128)(2,1)} %get-tuple-element.54), channel_id=1, source_target_pairs={{0,4},{4,0},{8,12},{12,8},{16,20},{20,16},{24,28},{28,24},{1,5},{5... | collective-permute-start | bytes 1179656 | tf_op jit(solution)/shard_map/ppermute | solution.py:383
  379.0 2.4 collective-permute-start.42
  (15 other events, 20.0 us)

commit v3 on v2

--- a/solution.py
+++ b/solution.py
@@ -19,9 +19,9 @@
 VMEM_LIMIT = 56 * 1024 * 1024
 BF = jnp.bfloat16
 
-HEAD_CHUNKS = (0, 3, 3, 2)
-SPLIT = ()
-OWN_ORDER = (0, 1, 2, 3)
+HEAD_CHUNKS = (0, 4, 4)
+SPLIT = (1, 2)
+OWN_ORDER = (0, 1, 2)
 
 
 def plain_rotate(vectors, positions):
@@ -216,10 +216,12 @@
 
 
 def chunk_kernel(
-    shard, places, heads, with_kv, block, base, n_out, len_ref, order_ref, cos_ref, sin_ref,
+    shard, places, parts, stage, heads, with_kv, block, base, n_out, len_ref, order_ref, chip_ref, cos_ref, sin_ref,
     their_tok, my_tok, their_old, my_old, *refs
 ):
-    if not with_kv:
+    if stage == "after":
+        before_ref, refs = refs[0], refs[1:]
+    if not with_kv and stage != "before":
         fresh_ref, refs = refs[0], refs[1:]
     weights, refs = refs[: len(places)], refs[len(places) :]
     out_refs, refs = refs[:n_out], refs[n_out:]
@@ -236,13 +238,20 @@
     factor = (1.0 / HEAD_DIM**0.5) * 1.4426950408889634
     nt = (((1,), (1,)), ((), ()))
     seqs = their_old.shape[1]
+    chip = w_ref.shape[0] // len(parts)
 
     def inputs(tok, old, seq, slot):
-        return [
-            pltpu.make_async_copy(tok.at[pl.ds(seq * new, new)], tok_ref.at[slot], sems.at[slot, 0]),
-            pltpu.make_async_copy(old.at[0, seq], old_ref.at[slot, 0], sems.at[slot, 1]),
-            pltpu.make_async_copy(old.at[1, seq], old_ref.at[slot, 1], sems.at[slot, 2]),
-        ]
+        copies = []
+        for j, part in enumerate(parts):
+            cols = pl.ds(pl.multiple_of(chip_ref[part] * chip, chip), chip)
+            src = tok.at[pl.ds(seq * new, new), cols]
+            copies.append(
+                pltpu.make_async_copy(src, tok_ref.at[slot, :, pl.ds(j * chip, chip)], sems.at[slot, 2 + j])
+            )
+        if stage != "before":
+            for k in range(2):
+                copies.append(pltpu.make_async_copy(old.at[k, seq], old_ref.at[slot, k], sems.at[slot, k]))
+        return copies
 
     def fetch(seq, slot):
         @pl.when(seq < seqs)
@@ -256,9 +265,9 @@
                 copy.start()
 
     copies = []
-    for (entry, col), ref in zip(places, weights):
+    for (entry, col, part), ref in zip(places, weights):
         for j in range(ref.shape[0] // shard):
-            to = pl.multiple_of(order_ref[entry + j] * shard, shard)
+            to = pl.multiple_of(part * chip + order_ref[entry + j] * shard, shard)
             copies.append(
                 pltpu.make_async_copy(
                     ref.at[pl.ds(j * shard, shard), pl.ds(col, w_ref.shape[1])],
@@ -286,6 +295,11 @@
             copy.wait()
 
     raw = jnp.dot(tok_ref[slot], w_ref[...], preferred_element_type=jnp.float32)
+    if stage == "before":
+        out_refs[0][...] = raw
+        return
+    if stage == "after":
+        raw = raw + before_ref[...]
     raw = [raw[:, h * HEAD_DIM : (h + 1) * HEAD_DIM] for h in range(raw.shape[1] // HEAD_DIM)]
     if with_kv:
         fresh_ref[0] = rotate(raw[0], cos_ref[...], sin_ref[...]).astype(BF)
@@ -491,8 +505,9 @@
     for shifts in ([0], list(range(1, T))):
         for d in range(0, R, 2):
             place[d, shifts[0]] = len(order)
-            order += [(r ^ (d + e)) * T + (z - s) % T for s in shifts for e in range(2)]
+            order += [(r ^ (d + e)) % 2 * T + (z - s) % T for s in shifts for e in range(2)]
     order = jnp.stack(order).astype(jnp.int32)
+    chips = jnp.stack([(r ^ d) // 2 for d in range(0, R, 2)]).astype(jnp.int32)
     rows_all = 2 * tok_rows
     params = pltpu.CompilerParams(vmem_limit_bytes=VMEM_LIMIT)
 
@@ -503,7 +518,9 @@
     cos, sin = jnp.cos(angles), jnp.sin(angles)
     cos, sin = jnp.concatenate([cos, cos], axis=1), jnp.concatenate([-sin, sin], axis=1)
 
-    def attend(c, fresh, group=None):
+    def attend(c, fresh, group=None, stage="all", before=None):
+        ranks = range(R // 2)
+        ranks = {"all": ranks, "before": ranks[:-1], "after": ranks[-1:]}[stage]
         n = head_chunks[c]
         width = n * HEAD_DIM
         with_kv = c == 0
@@ -516,8 +533,9 @@
         arrays, places = [], []
         for s, first, parts in ((0, own_firsts[c], own_all), (1, 0, rest_all[c])):
             for d, o, a in parts:
-                arrays.append(a)
-                places.append((place[d, s] + o // shard, first))
+                if d // 2 in ranks:
+                    arrays.append(a)
+                    places.append((place[d, s] + o // shard, first, ranks.index(d // 2)))
         row = lambda i, *_: (i + base, 0)
         out_width = width + 2 * HEAD_DIM * with_kv
         out_shape = [jax.ShapeDtypeStruct((tok_rows, out_width), BF)] * n_out
@@ -532,24 +550,29 @@
         if with_kv:
             out_shape.append(jax.ShapeDtypeStruct((2, rows_all, HEAD_DIM), BF))
             out_specs.append(fresh_spec)
+        before_spec = pl.BlockSpec((new, widths[c]), row)
+        if stage == "before":
+            n_out, out_shape = 1, [jax.ShapeDtypeStruct((rows_all, widths[c]), jnp.float32)]
+            out_specs = [before_spec]
         anywhere = pl.BlockSpec(memory_space=pl.ANY)
         call = pl.pallas_call(
-            functools.partial(chunk_kernel, shard, places, n, with_kv, block, base, n_out),
+            functools.partial(chunk_kernel, shard, places, ranks, stage, n, with_kv, block, base, n_out),
             out_shape=out_shape,
             grid_spec=pltpu.PrefetchScalarGridSpec(
-                num_scalar_prefetch=2,
+                num_scalar_prefetch=3,
                 grid=(count,),
                 in_specs=[
                     pl.BlockSpec((new, HEAD_DIM), row),
                     pl.BlockSpec((new, HEAD_DIM), row),
                     *[anywhere] * 4,
-                    *([] if with_kv else [fresh_spec]),
+                    *([before_spec] if stage == "after" else []),
+                    *([] if with_kv or stage == "before" else [fresh_spec]),
                     *[anywhere] * len(arrays),
                 ],
                 out_specs=out_specs,
                 scratch_shapes=[
-                    pltpu.VMEM((2, new, depth), BF),
-                    pltpu.VMEM((depth, widths[c]), BF),
+                    pltpu.VMEM((2, new, len(ranks) * 2 * T * shard), BF),
+                    pltpu.VMEM((len(ranks) * 2 * T * shard, widths[c]), BF),
                     pltpu.VMEM((2, 2, max_len, HEAD_DIM), BF),
                     pltpu.VMEM((m, HEAD_DIM), BF),
                     pltpu.VMEM((slots, m, block), jnp.float32),
@@ -557,7 +580,7 @@
                     pltpu.VMEM((m, 128), jnp.float32),
                     pltpu.VMEM((m, 128), jnp.float32),
                     pltpu.VMEM((m, 128), jnp.float32),
-                    pltpu.SemaphoreType.DMA((2, 3)),
+                    pltpu.SemaphoreType.DMA((2, 2 + len(ranks))),
                     pltpu.SemaphoreType.DMA((depth // shard,)),
                 ],
             ),
@@ -568,15 +591,17 @@
                 transcendentals=count * new * n * (max_len + new),
             ),
         )
-        extra = () if with_kv else (fresh,)
+        extra = () if with_kv or stage == "before" else (fresh,)
+        extra = (before, *extra) if stage == "after" else extra
         return call(
-            seq_lengths, order, cos, sin, their_tokens, tokens, their_old, my_old, *extra, *arrays
+            seq_lengths, order, chips, cos, sin, their_tokens, tokens, their_old, my_old, *extra, *arrays
         )
 
     out, at, fresh = jnp.zeros((tok_rows, q_local), BF), 0, None
     for c in range(n_chunks):
         if c in SPLIT:
-            (theirs,), (mine,) = attend(c, fresh, 0), attend(c, fresh, 1)
+            before = attend(c, None, stage="before")[0]
+            theirs, mine = attend(c, fresh, stage="after", before=before)
         else:
             theirs, mine, *rest = attend(c, fresh)
         theirs = xor(theirs, 1)

time: 385 us -> 347 us (0.901)
  waiting for transfers between devices: 168 us -> 148 us
  starting transfers between devices: 64 us -> 55.4 us
  Pallas kernels: 134 us -> 129 us
    ppermute x32 -> x27, waiting for transfers between devices: 119 us -> 93.5 us  [xor(): return lax.ppermute(a, 'rep', [(i, i ^ bit) for i in range(R)])]
    ppermute x12 -> x9, starting transfers between devices: 39.8 us -> 27.3 us  [over_tp(): lax.ppermute(ready[s, c], 'tp', [(t, (t + s) % T) for t in range(T)])]
    ppermute x12 -> x9, waiting for transfers between devices: 48.9 us -> 54.6 us  [over_tp(): lax.ppermute(ready[s, c], 'tp', [(t, (t + s) % T) for t in range(T)])]
    pallas_call x4 -> x5, Pallas kernels: 101 us -> 95.3 us  [attend(): call(seq_lengths, order, chips, cos, sin, their_tokens, tokens, their_old...]
    ppermute x32 -> x27, starting transfers between devices: 24.2 us -> 28.1 us  [xor(): return lax.ppermute(a, 'rep', [(i, i ^ bit) for i in range(R)])]
    unnamed x71 -> x65, local copies, waits for them, and re-layouts: 8.8 us -> 6.2 us
  transfers between devices with their start and end apart: 44 -> 36, of which waited for: 17 -> 16; matrix products, arithmetic and copies ran while one was open for 2% -> 2% of each run, Pallas kernels for 35% -> 37%
where the time goes in v3:
time: 347 us; the launch traced here: 346 us
  waiting for transfers between devices  148 us (43%)
  Pallas kernels  129 us (37%)
  starting transfers between devices  55.4 us (16%)
  local copies, waits for them, and re-layouts  8.07 us (2%)
  other arithmetic  4.92 us (1%)
    pallas_call x5, Pallas kernels, attend(): call(seq_lengths, order, chips, cos, sin, their_tokens, tokens, their_old...  95.3 us
    ppermute x27, waiting for transfers between devices, xor(): return lax.ppermute(a, 'rep', [(i, i ^ bit) for i in range(R)])  93.5 us
    ppermute x9, waiting for transfers between devices, over_tp(): lax.ppermute(ready[s, c], 'tp', [(t, (t + s) % T) for t in range(T)])  54.6 us
    ppermute x27, starting transfers between devices, xor(): return lax.ppermute(a, 'rep', [(i, i ^ bit) for i in range(R)])  28.1 us
    ppermute x9, starting transfers between devices, over_tp(): lax.ppermute(ready[s, c], 'tp', [(t, (t + s) % T) for t in range(T)])  27.3 us
    pallas_call x6, Pallas kernels, pack(): pl.pallas_call(functools.partial(pack_kernel, jobs, len(received)), out_s...  21.7 us
  transfers between devices with their start and end apart: 36, of which 16 were waited for; matrix products, arithmetic and copies ran while one was open for 2% of the time, Pallas kernels for 37%

profile of v3, /device:TPU:0, one launch (start us, length us, event | category | flops | bytes accessed | tf_op | source)
XLA Modules:
  0.0 346.3 jit_solution(6655469544119584777)
XLA Ops:
  1.9 3.7 %shard_map.97 = bf16[256,3072]{1,0:T(8,128)(2,1)} custom-call(s32[48]{0:T(128)} %stack.284.starts_ref, f32[256,8192]{1,0:T(8,128)} %refs_0_.11, f32[256,1024]{1,0:T(8,128)} %refs_1_.11, f32[256,1024]{1,0:T(8,128)} %refs_2_.11), custom_call_target="tpu_custom_call" | custom-call | flops 1000000 | bytes 4718592 | tf_op jit(solution)/shard_map/pallas_call | solution.py:149
  5.7 2.7 shard_map.101
  8.9 8.1 %collective-permute-done.16.refs_3_ = bf16[256,768]{1,0:T(8,128)(2,1)S(1)} collective-permute-done((bf16[256,768]{1,0:T(8,128)(2,1)}, bf16[256,768]{1,0:T(8,128)(2,1)S(1)}, u32[]{:S(2)}, u32[]{:S(2)}) %collective-permute-start.16) | collective-permute-done | bytes 393248 | tf_op jit(solution)/shard_map/ppermute | solution.py:397
  17.0 0.7 copy-done.20
  17.7 3.8 %shard_map.102 = (bf16[512,256]{1,0:T(8,128)(2,1)}, bf16[512,256]{1,0:T(8,128)(2,1)}, bf16[512,256]{1,0:T(8,128)(2,1)}) custom-call(s32[48]{0:T(128)} %stack.284.starts_ref, f32[256,8192]{1,0:T(8,128)} %refs_0_.11, f32[256,1024]{1,0:T(8,128)} %refs_1_.11, f32[256,1024]{1,0:T(8,128)} %refs_2_.11, bf16[256,768]{1,0:T(8,128)(2,1)} %copy-done.20), custom_call_target="tpu_custom_call" | custom-call | flops 1000000 | bytes 1179648 | tf_op jit(solution)/shard_map/pallas_call | solution.py:149
  21.6 3.0 collective-permute-start.17
  24.6 2.9 shard_map.96
  28.1 1.8 collective-permute-done
  29.9 2.6 collective-permute-start.18
  32.4 2.9 shard_map.95.refs_0_
  35.4 1.6 collective-permute-start.6
  37.0 5.7 %shard_map.98 = (bf16[512,512]{1,0:T(8,128)(2,1)}, bf16[512,512]{1,0:T(8,128)(2,1)}, bf16[512,512]{1,0:T(8,128)(2,1)}, bf16[512,512]{1,0:T(8,128)(2,1)}, bf16[51...) custom-call(s32[48]{0:T(128)} %stack.284.starts_ref, f32[256,8192]{1,0:T(8,128)} %refs_0_.11, f32[256,1024]{1,0:T(8,128)} %refs_1_.11, ...), custom_call_target="tpu_custom_call" | custom-call | flops 1000000 | bytes 4718592 | tf_op jit(solution)/shard_map/pallas_call | solution.py:149
  42.9 1.8 collective-permute-done.18.refs_1_
  44.7 2.7 collective-permute-start.19
  47.5 16.0 %collective-permute-done.19.refs_2_ = bf16[512,256]{1,0:T(8,128)(2,1)S(1)} collective-permute-done((bf16[512,256]{1,0:T(8,128)(2,1)S(1)}, bf16[512,256]{1,0:T(8,128)(2,1)S(1)}, u32[]{:S(2)}, u32[]{:S(2)}) %collective-permute-start.19) | collective-permute-done | bytes 262176 | tf_op jit(solution)/shard_map/ppermute | solution.py:463
  63.5 0.9 collective-permute-start.28
  64.4 1.5 collective-permute-start.4
  66.5 1.1 collective-permute-start.29
  67.5 20.9 %collective-permute-done.28.refs_1_ = bf16[512,512]{1,0:T(8,128)(2,1)S(1)} collective-permute-done((bf16[512,512]{1,0:T(8,128)(2,1)}, bf16[512,512]{1,0:T(8,128)(2,1)S(1)}, u32[]{:S(2)}, u32[]{:S(2)}) %collective-permute-start.28) | collective-permute-done | bytes 524320 | tf_op jit(solution)/shard_map/ppermute | solution.py:463
  88.5 1.5 collective-permute-start.14
  90.1 1.4 collective-permute-start.20
  91.5 1.3 shard_map.108.refs_6_
  92.8 0.7 collective-permute-start.30
  93.5 2.5 collective-permute-done.5.refs_3_
  96.1 1.3 collective-permute-start.7
  97.4 12.7 %collective-permute-done.14.refs_6_.refs_2_ = bf16[256,1280]{1,0:T(8,128)(2,1)S(1)} collective-permute-done((bf16[256,1280]{1,0:T(8,128)(2,1)S(1)}, bf16[256,1280]{1,0:T(8,128)(2,1)S(1)}, u32[]{:S(2)}, u32[]{:S(2)}) %collective-permute-start.14) | collective-permute-done | bytes 655392 | tf_op jit(solution)/shard_map/ppermute | solution.py:397
  110.1 0.9 copy-done.11
  111.0 2.0 collective-permute-start.10
  113.0 6.7 %collective-permute-start.11 = (bf16[512,512]{1,0:T(8,128)(2,1)S(1)}, bf16[512,512]{1,0:T(8,128)(2,1)S(1)}, u32[]{:S(2)}, u32[]{:S(2)}) collective-permute-start(bf16[512,512]{1,0:T(8,128)(2,1)S(1)} %copy-done.27), channel_id=1, source_target_pairs={{0,3},{1,0},{2,1},{3,2},{4,7},{5,4},{6,5},{7,6},{8,11},{9,8},{10,9... | collective-permute-start | bytes 1572872 | tf_op jit(solution)/shard_map/ppermute | solution.py:463
  119.7 7.3 %collective-permute-done.20.refs_1_.refs_9_ = bf16[1536,256]{1,0:T(8,128)(2,1)S(1)} collective-permute-done((bf16[1536,256]{1,0:T(8,128)(2,1)S(1)}, bf16[1536,256]{1,0:T(8,128)(2,1)S(1)}, u32[]{:S(2)}, u32[]{:S(2)}) %collective-permute-start.20) | collective-permute-done | bytes 786464 | tf_op jit(solution)/shard_map/ppermute | solution.py:397
  127.0 1.3 collective-permute-start.21
  128.3 8.9 %collective-permute-done.10.refs_1_ = bf16[512,512]{1,0:T(8,128)(2,1)S(1)} collective-permute-done((bf16[512,512]{1,0:T(8,128)(2,1)S(1)}, bf16[512,512]{1,0:T(8,128)(2,1)S(1)}, u32[]{:S(2)}, u32[]{:S(2)}) %collective-permute-start.10) | collective-permute-done | bytes 524320 | tf_op jit(solution)/shard_map/ppermute | solution.py:463
  137.3 8.1 %collective-permute-start.9 = (bf16[512,512]{1,0:T(8,128)(2,1)S(1)}, bf16[512,512]{1,0:T(8,128)(2,1)S(1)}, u32[]{:S(2)}, u32[]{:S(2)}) collective-permute-start(bf16[512,512]{1,0:T(8,128)(2,1)S(1)} %copy-done.26), channel_id=1, source_target_pairs={{0,1},{1,2},{2,3},{3,0},{4,5},{5,6},{6,7},{7,4},{8,9},{9,10},{10,1... | collective-permute-start | bytes 1572872 | tf_op jit(solution)/shard_map/ppermute | solution.py:463
  145.4 1.9 collective-permute-start.31
  147.2 6.1 %old.1 = (bf16[2,2,2048,128]{3,2,1,0:T(8,128)(2,1)}, bf16[2,2,2048,128]{3,2,1,0:T(8,128)(2,1)}) custom-call(s32[1]{0:T(128)} %bitcast.38.core_ref, s32[2,16]{1,0:T(2,128)} %bitcast.72, bf16[32,128,256]{2,1,0:T(8,128)(2,1)} %ck_ref.1, bf16[32,128,256]{2,1,0:T(8,128)(2,1)} %cv_ref.1), custom_call_target="tpu_custom_call" | custom-call | flops 1000000 | bytes 8000000 | tf_op jit(solution)/shard_map/old/pallas_call | solution.py:501
  153.4 6.9 %collective-permute-done.9.refs_0_ = bf16[512,512]{1,0:T(8,128)(2,1)S(1)} collective-permute-done((bf16[512,512]{1,0:T(8,128)(2,1)S(1)}, bf16[512,512]{1,0:T(8,128)(2,1)S(1)}, u32[]{:S(2)}, u32[]{:S(2)}) %collective-permute-start.9) | collective-permute-done | bytes 524320 | tf_op jit(solution)/shard_map/ppermute | solution.py:463
  160.3 1.3 shard_map.99.refs_6_
  161.6 1.6 collective-permute-start.12
  163.2 1.2 copy-done.3
  164.3 1.9 collective-permute-start.13
  167.5 15.4 %collective-permute-done.31.refs_8_.refs_0_ = bf16[1536,512]{1,0:T(8,128)(2,1)} collective-permute-done((bf16[1536,512]{1,0:T(8,128)(2,1)}, bf16[1536,512]{1,0:T(8,128)(2,1)}, u32[]{:S(2)}, u32[]{:S(2)}) %collective-permute-start.31) | collective-permute-done | bytes 1572896 | tf_op jit(solution)/shard_map/ppermute | solution.py:397
  182.9 1.9 collective-permute-start.15
  185.4 13.4 %collective-permute-done.12.refs_7_.refs_1_ = bf16[1536,512]{1,0:T(8,128)(2,1)} collective-permute-done((bf16[1536,512]{1,0:T(8,128)(2,1)}, bf16[1536,512]{1,0:T(8,128)(2,1)}, u32[]{:S(2)}, u32[]{:S(2)}) %collective-permute-start.12) | collective-permute-done | bytes 1572896 | tf_op jit(solution)/shard_map/ppermute | solution.py:397
  198.8 1.5 collective-permute-start.22
  200.3 16.4 %collective-permute-done.13.refs_8_.refs_0_ = bf16[1536,512]{1,0:T(8,128)(2,1)} collective-permute-done((bf16[1536,512]{1,0:T(8,128)(2,1)}, bf16[1536,512]{1,0:T(8,128)(2,1)}, u32[]{:S(2)}, u32[]{:S(2)}) %collective-permute-start.13) | collective-permute-done | bytes 1572896 | tf_op jit(solution)/shard_map/ppermute | solution.py:397
  216.7 1.9 collective-permute-start.23
  218.5 1.9 fusion
  220.4 1.3 pad_maximum_fusion
  221.8 1.2 shard_map.110
  222.9 1.4 shard_map.106
  224.3 1.6 collective-permute-start.32
  225.9 12.0 %collective-permute-done.23.refs_12_ = bf16[768,256]{1,0:T(8,128)(2,1)S(1)} collective-permute-done((bf16[768,256]{1,0:T(8,128)(2,1)S(1)}, bf16[768,256]{1,0:T(8,128)(2,1)S(1)}, u32[]{:S(2)}, u32[]{:S(2)}) %collective-permute-start.23) | collective-permute-done | bytes 393248 | tf_op jit(solution)/shard_map/ppermute | solution.py:397
  237.9 1.7 collective-permute-start.33
  239.7 1.5 collective-permute-start.24
  241.5 13.8 %shard_map.105 = (bf16[512,256]{1,0:T(8,128)(2,1)}, bf16[512,256]{1,0:T(8,128)(2,1)}, bf16[2,1024,128]{2,1,0:T(8,128)(2,1)}) custom-call(s32[4]{0:T(128)} %copy-done.22, s32[32]{0:T(128)} %stack.254.order_ref, s32[4]{0:T(128)} %pad_add_fusion.1.chip_ref, f32[1024,128]{1,0:T(8,128)} %get-tuple-element.57.cos_ref, f32[1024,128]{1,0:T(8,128)} %get-tuple-element.58.sin_ref, ...), custom_call_target="tpu_custom_call" | custom-call | bytes 16777216 | tf_op jit(solution)/shard_map/pallas_call | solution.py:596
  255.3 14.2 %shard_map.100.refs_0_ = f32[1024,512]{1,0:T(8,128)} custom-call(s32[4]{0:T(128)} %copy-done.22, s32[32]{0:T(128)} %stack.254.order_ref, s32[4]{0:T(128)} %pad_add_fusion.1.chip_ref, f32[1024,128]{1,0:T(8,128)} %get-tuple-element.57.cos_ref, f32[1024,128]{1,0:T(8,128)} %get-tuple-element.58.sin_ref, bf16[512,8192]{1,0:T(8,128)(2,1)} %collective-permute-done.1.their_tok, ...), custom_call_target="tpu_custom_call" | custom-call | flops 13421772800 | bytes 25165824 | tf_op jit(solution)/shard_map/pallas_call | solution.py:596
  269.5 3.8 %collective-permute-done.25.refs_5_ = bf16[768,512]{1,0:T(8,128)(2,1)} collective-permute-done((bf16[768,512]{1,0:T(8,128)(2,1)S(1)}, bf16[768,512]{1,0:T(8,128)(2,1)}, u32[]{:S(2)}, u32[]{:S(2)}) %collective-permute-start.25) | collective-permute-done | bytes 786464 | tf_op jit(solution)/shard_map/ppermute | solution.py:397
  273.4 26.5 %shard_map.107 = (bf16[512,512]{1,0:T(8,128)(2,1)}, bf16[512,512]{1,0:T(8,128)(2,1)}) custom-call(s32[4]{0:T(128)} %copy-done.22, s32[32]{0:T(128)} %stack.254.order_ref, s32[4]{0:T(128)} %pad_add_fusion.1.chip_ref, f32[1024,128]{1,0:T(8,128)} %get-tuple-element.57.cos_ref, f32[1024,128]{1,0:T(8,128)} %get-tuple-element.58.sin_ref, ...), custom_call_target="tpu_custom_call" | custom-call | flops 13421772800 | bytes 25165824 | tf_op jit(solution)/shard_map/pallas_call | solution.py:596
  299.9 14.2 %shard_map.109.refs_0_ = f32[1024,512]{1,0:T(8,128)} custom-call(s32[4]{0:T(128)} %copy-done.22, s32[32]{0:T(128)} %stack.254.order_ref, s32[4]{0:T(128)} %pad_add_fusion.1.chip_ref, f32[1024,128]{1,0:T(8,128)} %get-tuple-element.57.cos_ref, f32[1024,128]{1,0:T(8,128)} %get-tuple-element.58.sin_ref, bf16[512,8192]{1,0:T(8,128)(2,1)} %collective-permute-done.1.their_tok, ...), custom_call_target="tpu_custom_call" | custom-call | flops 13421772800 | bytes 25165824 | tf_op jit(solution)/shard_map/pallas_call | solution.py:596
  314.2 0.9 copy-done.23
  315.0 0.9 copy-done.24
  315.9 26.7 %shard_map.111 = (bf16[512,512]{1,0:T(8,128)(2,1)}, bf16[512,512]{1,0:T(8,128)(2,1)}) custom-call(s32[4]{0:T(128)} %copy-done.22, s32[32]{0:T(128)} %stack.254.order_ref, s32[4]{0:T(128)} %pad_add_fusion.1.chip_ref, f32[1024,128]{1,0:T(8,128)} %get-tuple-element.57.cos_ref, f32[1024,128]{1,0:T(8,128)} %get-tuple-element.58.sin_ref, ...), custom_call_target="tpu_custom_call" | custom-call | flops 13421772800 | bytes 25165824 | tf_op jit(solution)/shard_map/pallas_call | solution.py:596
  343.9 0.8 pad_maximum_fusion.2
  345.0 1.3 copy-done.6
  (108 shorter events, 7.2 us)
Async XLA Ops:
  0.6 240.8 %collective-permute-start.1 = (bf16[512,8192]{1,0:T(8,128)(2,1)}, bf16[512,8192]{1,0:T(8,128)(2,1)}, u32[]{:S(2)}, u32[]{:S(2)}) collective-permute-start(bf16[512,8192]{1,0:T(8,128)(2,1)} %my_tok.9), channel_id=1, source_target_pairs={{0,4},{4,0},{8,12},{12,8},{16,20},{20,16},{24,28},{28,24},{1,5},{5... | collective-permute-start | bytes 25165832 | tf_op jit(solution)/shard_map/ppermute | solution.py:397
  5.6 29.8 %collective-permute-start.8 = (bf16[256,3072]{1,0:T(8,128)(2,1)}, bf16[256,3072]{1,0:T(8,128)(2,1)S(1)}, u32[]{:S(2)}, u32[]{:S(2)}) collective-permute-start(bf16[256,3072]{1,0:T(8,128)(2,1)} %shard_map.97), channel_id=1, source_target_pairs={{0,4},{4,0},{8,12},{12,8},{16,20},{20,16},{24,28},{28,24},{1,5},{5... | collective-permute-start | bytes 4718600 | tf_op jit(solution)/shard_map/ppermute | solution.py:397
  8.4 8.6 %collective-permute-start.16 = (bf16[256,768]{1,0:T(8,128)(2,1)}, bf16[256,768]{1,0:T(8,128)(2,1)S(1)}, u32[]{:S(2)}, u32[]{:S(2)}) collective-permute-start(bf16[256,768]{1,0:T(8,128)(2,1)} %shard_map.101), channel_id=1, source_target_pairs={{0,4},{4,0},{8,12},{12,8},{16,20},{20,16},{24,28},{28,24},{1,5},{5... | collective-permute-start | bytes 1179656 | tf_op jit(solution)/shard_map/ppermute | solution.py:397
  21.6 6.0 %copy-start.31 = (s32[1,2]{1,0:T(1,128)S(1)}, s32[1,2]{1,0:T(1,128)}, u32[]{:S(2)}) copy-start(s32[1,2]{1,0:T(1,128)} %param.14) | copy-start | bytes 28
  21.6 8.3 %copy-start.30 = (bf16[512,256]{1,0:T(8,128)(2,1)S(1)}, bf16[512,256]{1,0:T(8,128)(2,1)}, u32[]{:S(2)}) copy-start(bf16[512,256]{1,0:T(8,128)(2,1)} %get-tuple-element.32) | copy-start | bytes 786436
  21.6 21.1 %collective-permute-start.17 = (bf16[512,256]{1,0:T(8,128)(2,1)}, bf16[512,256]{1,0:T(8,128)(2,1)S(1)}, u32[]{:S(2)}, u32[]{:S(2)}) collective-permute-start(bf16[512,256]{1,0:T(8,128)(2,1)} %get-tuple-element.31), channel_id=1, source_target_pairs={{0,1},{1,2},{2,3},{3,0},{4,5},{5,6},{6,7},{7,4},{8,9},{9,10},{10,1... | collective-permute-start | bytes 786440 | tf_op jit(solution)/shard_map/ppermute | solution.py:463
  27.5 36.9 %collective-permute-start.3 = (bf16[256,1280]{1,0:T(8,128)(2,1)}, bf16[256,1280]{1,0:T(8,128)(2,1)S(1)}, u32[]{:S(2)}, u32[]{:S(2)}) collective-permute-start(bf16[256,1280]{1,0:T(8,128)(2,1)} %shard_map.96), channel_id=1, source_target_pairs={{0,4},{4,0},{8,12},{12,8},{16,20},{20,16},{24,28},{28,24},{1,5},{5... | collective-permute-start | bytes 1966088 | tf_op jit(solution)/shard_map/ppermute | solution.py:397
  27.6 2.3 collective-permute-start
  29.9 14.9 %collective-permute-start.18 = (bf16[512,256]{1,0:T(8,128)(2,1)S(1)}, bf16[512,256]{1,0:T(8,128)(2,1)S(1)}, u32[]{:S(2)}, u32[]{:S(2)}) collective-permute-start(bf16[512,256]{1,0:T(8,128)(2,1)S(1)} %copy-done.30), channel_id=1, source_target_pairs={{0,2},{1,3},{2,0},{3,1},{4,6},{5,7},{6,4},{7,5},{8,10},{9,11},{10,... | collective-permute-start | bytes 786440 | tf_op jit(solution)/shard_map/ppermute | solution.py:463
  35.4 9.4 %copy-start.29 = (bf16[512,256]{1,0:T(8,128)(2,1)S(1)}, bf16[512,256]{1,0:T(8,128)(2,1)}, u32[]{:S(2)}) copy-start(bf16[512,256]{1,0:T(8,128)(2,1)} %get-tuple-element.33) | copy-start | bytes 786436
  35.4 29.0 %copy-start.5 = (bf16[256,1280]{1,0:T(8,128)(2,1)S(1)}, bf16[256,1280]{1,0:T(8,128)(2,1)}, u32[]{:S(2)}) copy-start(bf16[256,1280]{1,0:T(8,128)(2,1)} %shard_map.95.refs_0_) | copy-start | bytes 1966084
  35.4 1.6 copy-start.7
  35.4 30.5 %collective-permute-start.6 = (bf16[256,1280]{1,0:T(8,128)(2,1)}, bf16[256,1280]{1,0:T(8,128)(2,1)S(1)}, u32[]{:S(2)}, u32[]{:S(2)}) collective-permute-start(bf16[256,1280]{1,0:T(8,128)(2,1)} %shard_map.95.refs_0_), channel_id=1, source_target_pairs={{0,16},{4,20},{8,24},{12,28},{16,0},{20,4},{24,8},{28,12},{1,17},{... | collective-permute-start | bytes 1966088 | tf_op jit(solution)/shard_map/ppermute | solution.py:397
  42.7 23.8 %collective-permute-start.27 = (bf16[512,512]{1,0:T(8,128)(2,1)}, bf16[512,512]{1,0:T(8,128)(2,1)S(1)}, u32[]{:S(2)}, u32[]{:S(2)}) collective-permute-start(bf16[512,512]{1,0:T(8,128)(2,1)} %get-tuple-element.41), channel_id=1, source_target_pairs={{0,1},{1,2},{2,3},{3,0},{4,5},{5,6},{6,7},{7,4},{8,9},{9,10},{10,1... | collective-permute-start | bytes 1572872 | tf_op jit(solution)/shard_map/ppermute | solution.py:463
  44.7 18.7 %collective-permute-start.19 = (bf16[512,256]{1,0:T(8,128)(2,1)S(1)}, bf16[512,256]{1,0:T(8,128)(2,1)S(1)}, u32[]{:S(2)}, u32[]{:S(2)}) collective-permute-start(bf16[512,256]{1,0:T(8,128)(2,1)S(1)} %copy-done.29), channel_id=1, source_target_pairs={{0,3},{1,0},{2,1},{3,2},{4,7},{5,4},{6,5},{7,6},{8,11},{9,8},{10,9... | collective-permute-start | bytes 786440 | tf_op jit(solution)/shard_map/ppermute | solution.py:463
  63.5 25.0 %collective-permute-start.28 = (bf16[512,512]{1,0:T(8,128)(2,1)}, bf16[512,512]{1,0:T(8,128)(2,1)S(1)}, u32[]{:S(2)}, u32[]{:S(2)}) collective-permute-start(bf16[512,512]{1,0:T(8,128)(2,1)} %get-tuple-element.42), channel_id=1, source_target_pairs={{0,2},{1,3},{2,0},{3,1},{4,6},{5,7},{6,4},{7,5},{8,10},{9,11},{10,... | collective-permute-start | bytes 1572872 | tf_op jit(solution)/shard_map/ppermute | solution.py:463
  64.4 31.7 %copy-start.8 = (bf16[256,1280]{1,0:T(8,128)(2,1)}, bf16[256,1280]{1,0:T(8,128)(2,1)S(1)}, u32[]{:S(2)}) copy-start(bf16[256,1280]{1,0:T(8,128)(2,1)S(1)} %collective-permute-done.3.refs_1_) | copy-start | bytes 1966084
  64.4 28.4 %collective-permute-start.4 = (bf16[256,1280]{1,0:T(8,128)(2,1)S(1)}, bf16[256,1280]{1,0:T(8,128)(2,1)S(1)}, u32[]{:S(2)}, u32[]{:S(2)}) collective-permute-start(bf16[256,1280]{1,0:T(8,128)(2,1)S(1)} %copy-done.5), channel_id=1, source_target_pairs={{0,8},{4,12},{8,0},{12,4},{16,24},{20,28},{24,16},{28,20},{1,9},{5... | collective-permute-start | bytes 1966088 | tf_op jit(solution)/shard_map/ppermute | solution.py:397
  65.9 26.9 %copy-start.9 = (bf16[256,1280]{1,0:T(8,128)(2,1)}, bf16[256,1280]{1,0:T(8,128)(2,1)S(1)}, u32[]{:S(2)}) copy-start(bf16[256,1280]{1,0:T(8,128)(2,1)S(1)} %collective-permute-done.6.refs_4_) | copy-start | bytes 1966084
  65.9 30.2 %collective-permute-start.5 = (bf16[256,1280]{1,0:T(8,128)(2,1)S(1)}, bf16[256,1280]{1,0:T(8,128)(2,1)S(1)}, u32[]{:S(2)}, u32[]{:S(2)}) collective-permute-start(bf16[256,1280]{1,0:T(8,128)(2,1)S(1)} %collective-permute-done.3.refs_1_), channel_id=1, source_target_pairs={{0,8},{4,12},{8,0},{12,4},{16,24},{20,28},{24,16},{28,20},{1,9},{5... | collective-permute-start | bytes 1966088 | tf_op jit(solution)/shard_map/ppermute | solution.py:397
  66.5 44.5 %copy-start.28 = (bf16[512,512]{1,0:T(8,128)(2,1)S(1)}, bf16[512,512]{1,0:T(8,128)(2,1)}, u32[]{:S(2)}) copy-start(bf16[512,512]{1,0:T(8,128)(2,1)} %get-tuple-element.29) | copy-start | bytes 1572868
  66.5 46.6 %copy-start.27 = (bf16[512,512]{1,0:T(8,128)(2,1)S(1)}, bf16[512,512]{1,0:T(8,128)(2,1)}, u32[]{:S(2)}) copy-start(bf16[512,512]{1,0:T(8,128)(2,1)} %get-tuple-element.30) | copy-start | bytes 1572868
  66.5 70.8 %copy-start.26 = (bf16[512,512]{1,0:T(8,128)(2,1)S(1)}, bf16[512,512]{1,0:T(8,128)(2,1)}, u32[]{:S(2)}) copy-start(bf16[512,512]{1,0:T(8,128)(2,1)} %get-tuple-element.28) | copy-start | bytes 1572868
  66.5 23.6 %collective-permute-start.29 = (bf16[512,512]{1,0:T(8,128)(2,1)}, bf16[512,512]{1,0:T(8,128)(2,1)S(1)}, u32[]{:S(2)}, u32[]{:S(2)}) collective-permute-start(bf16[512,512]{1,0:T(8,128)(2,1)} %get-tuple-element.43), channel_id=1, source_target_pairs={{0,3},{1,0},{2,1},{3,2},{4,7},{5,4},{6,5},{7,6},{8,11},{9,8},{10,9... | collective-permute-start | bytes 1572872 | tf_op jit(solution)/shard_map/ppermute | solution.py:463
  88.5 21.7 %collective-permute-start.14 = (bf16[256,1280]{1,0:T(8,128)(2,1)S(1)}, bf16[256,1280]{1,0:T(8,128)(2,1)S(1)}, u32[]{:S(2)}, u32[]{:S(2)}) collective-permute-start(bf16[256,1280]{1,0:T(8,128)(2,1)S(1)} %collective-permute-done.6.refs_4_), channel_id=1, source_target_pairs={{0,8},{4,12},{8,0},{12,4},{16,24},{20,28},{24,16},{28,20},{1,9},{5... | collective-permute-start | bytes 1966088 | tf_op jit(solution)/shard_map/ppermute | solution.py:397
  90.1 63.3 %copy-start = (bf16[1536,256]{1,0:T(8,128)(2,1)}, bf16[1536,256]{1,0:T(8,128)(2,1)S(1)}, u32[]{:S(2)}) copy-start(bf16[1536,256]{1,0:T(8,128)(2,1)S(1)} %shard_map.103.refs_8_) | copy-start | bytes 2359300
  90.1 36.9 %collective-permute-start.20 = (bf16[1536,256]{1,0:T(8,128)(2,1)S(1)}, bf16[1536,256]{1,0:T(8,128)(2,1)S(1)}, u32[]{:S(2)}, u32[]{:S(2)}) collective-permute-start(bf16[1536,256]{1,0:T(8,128)(2,1)S(1)} %shard_map.103.refs_8_), channel_id=1, source_target_pairs={{0,8},{4,12},{8,0},{12,4},{16,24},{20,28},{24,16},{28,20},{1,9},{5... | collective-permute-start | bytes 2359304 | tf_op jit(solution)/shard_map/ppermute | solution.py:397
  92.8 60.6 %copy-start.10 = (bf16[256,1280]{1,0:T(8,128)(2,1)}, bf16[256,1280]{1,0:T(8,128)(2,1)S(1)}, u32[]{:S(2)}) copy-start(bf16[256,1280]{1,0:T(8,128)(2,1)S(1)} %collective-permute-done.4.refs_2_) | copy-start | bytes 1966084
  92.8 70.3 %collective-permute-start.30 = (bf16[1536,512]{1,0:T(8,128)(2,1)}, bf16[1536,512]{1,0:T(8,128)(2,1)S(1)}, u32[]{:S(2)}, u32[]{:S(2)}) collective-permute-start(bf16[1536,512]{1,0:T(8,128)(2,1)} %shard_map.108.refs_6_), channel_id=1, source_target_pairs={{0,8},{4,12},{8,0},{12,4},{16,24},{20,28},{24,16},{28,20},{1,9},{5... | collective-permute-start | bytes 4718600 | tf_op jit(solution)/shard_map/ppermute | solution.py:397
  96.1 16.9 %copy-start.12 = (bf16[256,1280]{1,0:T(8,128)(2,1)}, bf16[256,1280]{1,0:T(8,128)(2,1)S(1)}, u32[]{:S(2)}) copy-start(bf16[256,1280]{1,0:T(8,128)(2,1)S(1)} %collective-permute-done.5.refs_3_) | copy-start | bytes 1966084
  96.1 16.9 %collective-permute-start.7 = (bf16[256,1280]{1,0:T(8,128)(2,1)S(1)}, bf16[256,1280]{1,0:T(8,128)(2,1)S(1)}, u32[]{:S(2)}, u32[]{:S(2)}) collective-permute-start(bf16[256,1280]{1,0:T(8,128)(2,1)S(1)} %collective-permute-done.3.refs_1_), channel_id=1, source_target_pairs={{0,16},{4,20},{8,24},{12,28},{16,0},{20,4},{24,8},{28,12},{1,17},{... | collective-permute-start | bytes 1966088 | tf_op jit(solution)/shard_map/ppermute | solution.py:397
  111.0 26.3 %collective-permute-start.10 = (bf16[512,512]{1,0:T(8,128)(2,1)S(1)}, bf16[512,512]{1,0:T(8,128)(2,1)S(1)}, u32[]{:S(2)}, u32[]{:S(2)}) collective-permute-start(bf16[512,512]{1,0:T(8,128)(2,1)S(1)} %copy-done.28), channel_id=1, source_target_pairs={{0,2},{1,3},{2,0},{3,1},{4,6},{5,7},{6,4},{7,5},{8,10},{9,11},{10,... | collective-permute-start | bytes 1572872 | tf_op jit(solution)/shard_map/ppermute | solution.py:463
  113.0 6.7 %copy-start.14 = (bf16[256,1280]{1,0:T(8,128)(2,1)}, bf16[256,1280]{1,0:T(8,128)(2,1)S(1)}, u32[]{:S(2)}) copy-start(bf16[256,1280]{1,0:T(8,128)(2,1)S(1)} %collective-permute-done.7.refs_5_) | copy-start | bytes 1966084
  113.0 32.3 %collective-permute-start.11 = (bf16[512,512]{1,0:T(8,128)(2,1)S(1)}, bf16[512,512]{1,0:T(8,128)(2,1)S(1)}, u32[]{:S(2)}, u32[]{:S(2)}) collective-permute-start(bf16[512,512]{1,0:T(8,128)(2,1)S(1)} %copy-done.27), channel_id=1, source_target_pairs={{0,3},{1,0},{2,1},{3,2},{4,7},{5,4},{6,5},{7,6},{8,11},{9,8},{10,9... | collective-permute-start | bytes 1572872 | tf_op jit(solution)/shard_map/ppermute | solution.py:463
  127.0 58.0 %copy-start.1 = (bf16[1536,256]{1,0:T(8,128)(2,1)}, bf16[1536,256]{1,0:T(8,128)(2,1)S(1)}, u32[]{:S(2)}) copy-start(bf16[1536,256]{1,0:T(8,128)(2,1)S(1)} %collective-permute-done.20.refs_1_.refs_9_) | copy-start | bytes 2359300
  127.0 34.6 %collective-permute-start.21 = (bf16[1536,256]{1,0:T(8,128)(2,1)S(1)}, bf16[1536,256]{1,0:T(8,128)(2,1)S(1)}, u32[]{:S(2)}, u32[]{:S(2)}) collective-permute-start(bf16[1536,256]{1,0:T(8,128)(2,1)S(1)} %shard_map.103.refs_8_), channel_id=1, source_target_pairs={{0,16},{4,20},{8,24},{12,28},{16,0},{20,4},{24,8},{28,12},{1,17},{... | collective-permute-start | bytes 2359304 | tf_op jit(solution)/shard_map/ppermute | solution.py:397
  137.3 23.0 %collective-permute-start.9 = (bf16[512,512]{1,0:T(8,128)(2,1)S(1)}, bf16[512,512]{1,0:T(8,128)(2,1)S(1)}, u32[]{:S(2)}, u32[]{:S(2)}) collective-permute-start(bf16[512,512]{1,0:T(8,128)(2,1)S(1)} %copy-done.26), channel_id=1, source_target_pairs={{0,1},{1,2},{2,3},{3,0},{4,5},{5,6},{6,7},{7,4},{8,9},{9,10},{10,1... | collective-permute-start | bytes 1572872 | tf_op jit(solution)/shard_map/ppermute | solution.py:463
  145.4 37.6 %collective-permute-start.31 = (bf16[1536,512]{1,0:T(8,128)(2,1)}, bf16[1536,512]{1,0:T(8,128)(2,1)}, u32[]{:S(2)}, u32[]{:S(2)}) collective-permute-start(bf16[1536,512]{1,0:T(8,128)(2,1)} %shard_map.108.refs_6_), channel_id=1, source_target_pairs={{0,16},{4,20},{8,24},{12,28},{16,0},{20,4},{24,8},{28,12},{1,17},{... | collective-permute-start | bytes 4718600 | tf_op jit(solution)/shard_map/ppermute | solution.py:397
  153.4 29.6 %copy-start.13 = (bf16[256,1280]{1,0:T(8,128)(2,1)S(1)}, bf16[256,1280]{1,0:T(8,128)(2,1)}, u32[]{:S(2)}) copy-start(bf16[256,1280]{1,0:T(8,128)(2,1)} %copy-done.12) | copy-start | bytes 1966084
  160.3 80.9 %collective-permute-start.2 = (bf16[2,2,2048,128]{3,2,1,0:T(8,128)(2,1)}, bf16[2,2,2048,128]{3,2,1,0:T(8,128)(2,1)}, u32[]{:S(2)}, u32[]{:S(2)}) collective-permute-start(bf16[2,2,2048,128]{3,2,1,0:T(8,128)(2,1)} %get-tuple-element.26), channel_id=1, source_target_pairs={{0,4},{4,0},{8,12},{12,8},{16,20},{20,16},{24,28},{28,24},{1,5},{5... | collective-permute-start | bytes 6291464 | tf_op jit(solution)/shard_map/ppermute | solution.py:397
  161.6 60.2 %copy-start.2 = (bf16[1536,256]{1,0:T(8,128)(2,1)}, bf16[1536,256]{1,0:T(8,128)(2,1)S(1)}, u32[]{:S(2)}) copy-start(bf16[1536,256]{1,0:T(8,128)(2,1)S(1)} %collective-permute-done.21.refs_0_.refs_10_) | copy-start | bytes 2359300
  161.6 37.2 %collective-permute-start.12 = (bf16[1536,512]{1,0:T(8,128)(2,1)}, bf16[1536,512]{1,0:T(8,128)(2,1)}, u32[]{:S(2)}, u32[]{:S(2)}) collective-permute-start(bf16[1536,512]{1,0:T(8,128)(2,1)} %shard_map.99.refs_6_), channel_id=1, source_target_pairs={{0,8},{4,12},{8,0},{12,4},{16,24},{20,28},{24,16},{28,20},{1,9},{5... | collective-permute-start | bytes 4718600 | tf_op jit(solution)/shard_map/ppermute | solution.py:397
  163.2 1.2 copy-start.3
  164.3 52.3 %collective-permute-start.13 = (bf16[1536,512]{1,0:T(8,128)(2,1)}, bf16[1536,512]{1,0:T(8,128)(2,1)}, u32[]{:S(2)}, u32[]{:S(2)}) collective-permute-start(bf16[1536,512]{1,0:T(8,128)(2,1)} %shard_map.99.refs_6_), channel_id=1, source_target_pairs={{0,16},{4,20},{8,24},{12,28},{16,0},{20,4},{24,8},{28,12},{1,17},{... | collective-permute-start | bytes 4718600 | tf_op jit(solution)/shard_map/ppermute | solution.py:397
  182.9 56.7 %collective-permute-start.15 = (bf16[256,1280]{1,0:T(8,128)(2,1)S(1)}, bf16[256,1280]{1,0:T(8,128)(2,1)S(1)}, u32[]{:S(2)}, u32[]{:S(2)}) collective-permute-start(bf16[256,1280]{1,0:T(8,128)(2,1)S(1)} %copy-done.13), channel_id=1, source_target_pairs={{0,16},{4,20},{8,24},{12,28},{16,0},{20,4},{24,8},{28,12},{1,17},{... | collective-permute-start | bytes 1966088 | tf_op jit(solution)/shard_map/ppermute | solution.py:397
  184.9 36.8 %copy-start.22 = (s32[4]{0:T(128)}, s32[4]{0:T(128)S(1)}, u32[]{:S(2)}) copy-start(s32[4]{0:T(128)S(1)} %pad_add_fusion.len_ref) | copy-start | bytes 52
  198.8 25.6 %collective-permute-start.22 = (bf16[768,256]{1,0:T(8,128)(2,1)S(1)}, bf16[768,256]{1,0:T(8,128)(2,1)S(1)}, u32[]{:S(2)}, u32[]{:S(2)}) collective-permute-start(bf16[768,256]{1,0:T(8,128)(2,1)S(1)} %get-tuple-element.34), channel_id=1, source_target_pairs={{0,8},{4,12},{8,0},{12,4},{16,24},{20,28},{24,16},{28,20},{1,9},{5... | collective-permute-start | bytes 1179656 | tf_op jit(solution)/shard_map/ppermute | solution.py:397
  216.7 21.3 %collective-permute-start.23 = (bf16[768,256]{1,0:T(8,128)(2,1)S(1)}, bf16[768,256]{1,0:T(8,128)(2,1)S(1)}, u32[]{:S(2)}, u32[]{:S(2)}) collective-permute-start(bf16[768,256]{1,0:T(8,128)(2,1)S(1)} %get-tuple-element.35), channel_id=1, source_target_pairs={{0,16},{4,20},{8,24},{12,28},{16,0},{20,4},{24,8},{28,12},{1,17},{... | collective-permute-start | bytes 1179656 | tf_op jit(solution)/shard_map/ppermute | solution.py:397
  218.5 3.2 copy-start.4
  224.3 17.1 %copy-start.18 = (bf16[768,256]{1,0:T(8,128)(2,1)}, bf16[768,256]{1,0:T(8,128)(2,1)S(1)}, u32[]{:S(2)}) copy-start(bf16[768,256]{1,0:T(8,128)(2,1)S(1)} %collective-permute-done.22.refs_11_) | copy-start | bytes 1179652
  224.3 89.8 %collective-permute-start.32 = (bf16[768,512]{1,0:T(8,128)(2,1)S(1)}, bf16[768,512]{1,0:T(8,128)(2,1)S(1)}, u32[]{:S(2)}, u32[]{:S(2)}) collective-permute-start(bf16[768,512]{1,0:T(8,128)(2,1)S(1)} %get-tuple-element.44), channel_id=1, source_target_pairs={{0,8},{4,12},{8,0},{12,4},{16,24},{20,28},{24,16},{28,20},{1,9},{5... | collective-permute-start | bytes 2359304 | tf_op jit(solution)/shard_map/ppermute | solution.py:397
  237.9 3.5 %copy-start.19 = (bf16[768,256]{1,0:T(8,128)(2,1)}, bf16[768,256]{1,0:T(8,128)(2,1)S(1)}, u32[]{:S(2)}) copy-start(bf16[768,256]{1,0:T(8,128)(2,1)S(1)} %collective-permute-done.23.refs_12_) | copy-start | bytes 1179652
  237.9 76.2 %collective-permute-start.33 = (bf16[768,512]{1,0:T(8,128)(2,1)S(1)}, bf16[768,512]{1,0:T(8,128)(2,1)S(1)}, u32[]{:S(2)}, u32[]{:S(2)}) collective-permute-start(bf16[768,512]{1,0:T(8,128)(2,1)S(1)} %get-tuple-element.45), channel_id=1, source_target_pairs={{0,16},{4,20},{8,24},{12,28},{16,0},{20,4},{24,8},{28,12},{1,17},{... | collective-permute-start | bytes 2359304 | tf_op jit(solution)/shard_map/ppermute | solution.py:397
  239.7 1.8 copy-start.15
  239.7 29.8 %collective-permute-start.24 = (bf16[768,512]{1,0:T(8,128)(2,1)S(1)}, bf16[768,512]{1,0:T(8,128)(2,1)S(1)}, u32[]{:S(2)}, u32[]{:S(2)}) collective-permute-start(bf16[768,512]{1,0:T(8,128)(2,1)S(1)} %get-tuple-element.37), channel_id=1, source_target_pairs={{0,8},{4,12},{8,0},{12,4},{16,24},{20,28},{24,16},{28,20},{1,9},{5... | collective-permute-start | bytes 2359304 | tf_op jit(solution)/shard_map/ppermute | solution.py:397
  241.2 32.2 %collective-permute-start.25 = (bf16[768,512]{1,0:T(8,128)(2,1)S(1)}, bf16[768,512]{1,0:T(8,128)(2,1)}, u32[]{:S(2)}, u32[]{:S(2)}) collective-permute-start(bf16[768,512]{1,0:T(8,128)(2,1)S(1)} %get-tuple-element.38), channel_id=1, source_target_pairs={{0,16},{4,20},{8,24},{12,28},{16,0},{20,4},{24,8},{28,12},{1,17},{... | collective-permute-start | bytes 2359304 | tf_op jit(solution)/shard_map/ppermute | solution.py:397
  255.2 88.5 %collective-permute-start.35 = (bf16[512,256]{1,0:T(8,128)(2,1)}, bf16[512,256]{1,0:T(8,128)(2,1)S(1)}, u32[]{:S(2)}, u32[]{:S(2)}) collective-permute-start(bf16[512,256]{1,0:T(8,128)(2,1)} %get-tuple-element.49), channel_id=1, source_target_pairs={{0,4},{4,0},{8,12},{12,8},{16,20},{20,16},{24,28},{28,24},{1,5},{5... | collective-permute-start | bytes 786440 | tf_op jit(solution)/shard_map/ppermute | solution.py:397
  269.5 3.8 %copy-start.25 = (bf16[768,512]{1,0:T(8,128)(2,1)}, bf16[768,512]{1,0:T(8,128)(2,1)S(1)}, u32[]{:S(2)}) copy-start(bf16[768,512]{1,0:T(8,128)(2,1)S(1)} %collective-permute-done.24.refs_4_) | copy-start | bytes 2359300
  299.8 44.9 %collective-permute-start.26 = (bf16[512,512]{1,0:T(8,128)(2,1)}, bf16[512,512]{1,0:T(8,128)(2,1)S(1)}, u32[]{:S(2)}, u32[]{:S(2)}) collective-permute-start(bf16[512,512]{1,0:T(8,128)(2,1)} %get-tuple-element.40), channel_id=1, source_target_pairs={{0,4},{4,0},{8,12},{12,8},{16,20},{20,16},{24,28},{28,24},{1,5},{5... | collective-permute-start | bytes 1572872 | tf_op jit(solution)/shard_map/ppermute | solution.py:397
  342.6 1.0 copy-start.17
  342.6 1.1 copy-start.21
  342.7 2.3 collective-permute-start.34
  343.8 1.1 copy-start.16
  345.0 1.3 copy-start.6
  (4 other events, 3.4 us)
